TPU v7x, 32 devices: a whole 2x2x4 slice. The times are simulated.
32 devices in a mesh: ep: 8 (over z, y), tp: 4 (over x, core).
Axes of the slice: x: 2, y: 2, z: 4, core: 2. Of those that a mesh axis runs over, the one named last changes fastest.
Arguments:
- layer_input: bfloat16 [8192, 2048], P(('ep', 'tp')), may hold values from -6 to 6
- routes: int32 [8192, 8], P(('ep', 'tp')), may hold values from 0 to 31, all different within a row; in each aligned block of 256 rows (0 to 255, 256 to 511, ...) at most 96 rows name the same one
- doc_lengths: int32 [8, 4], P('ep'), may hold values from 1 to 512, 1024 in all within a row
- norm1_gain: bfloat16 [2048], replicated, may hold values from 0.25 to 1.75
- w_qkv: bfloat16 [2048, 3, 2048], P(None, None, 'tp'), may hold values from -0.125 to 0.125
- q_gain: bfloat16 [128], replicated, may hold values from 0.25 to 1.75
- k_gain: bfloat16 [128], replicated, may hold values from 0.25 to 1.75
- w_out: bfloat16 [2048, 2048], P('tp'), may hold values from -0.5 to 0.5
- norm2_gain: bfloat16 [2048], replicated, may hold values from 0.25 to 1.75
- w_router: bfloat16 [2048, 32], replicated, may hold values from -0.125 to 0.125
- expert_gate_up: bfloat16 [32, 2048, 2, 1024], P('ep', None, None, 'tp'), may hold values from -0.125 to 0.125
- expert_down: bfloat16 [32, 1024, 2048], P('ep', 'tp'), may hold values from -0.375 to 0.375
- d_out: bfloat16 [8192, 2048], P(('ep', 'tp')), may hold values from -6 to 6
Outputs:
- output: bfloat16 [8192, 2048], P(('ep', 'tp'))
- grad_input: float32 [8192, 2048], P(('ep', 'tp'))
- grad_norm1: float32 [2048], replicated
- grad_w_qkv: float32 [2048, 3, 2048], P('ep', None, 'tp')
- grad_q_gain: float32 [128], replicated
- grad_k_gain: float32 [128], replicated
- grad_w_out: float32 [2048, 2048], P('tp', 'ep')
- grad_norm2: float32 [2048], replicated
- grad_router: float32 [2048, 32], replicated
- grad_gate_up: float32 [32, 2048, 2, 1024], P('ep', None, None, 'tp')
- grad_down: float32 [32, 1024, 2048], P('ep', 'tp')
Inputs may be any that keep to these rules, and one draw needn't show every extreme that they name: `routes`: among the rows of one device (aligned blocks of 256 tokens), no expert is chosen by more than 96 tokens; some expert is chosen by exactly 96 of them. A token's 8 experts differ. `doc_lengths`: A sequence's 4 lengths sum to 1024; the longest is 512.
All inputs are finite; a program needn't handle non-finite values.
Results may differ from a plain program's by a relative error of at most 0.024.
Values may be sent and summed in bfloat16 or wider, within the bound.
A program may use at most 576 MiB of HBM per device.

v0:
```python
from functools import partial

import jax
import jax.numpy as jnp
from jax import lax
from jax.sharding import PartitionSpec as P

HIGH = lax.Precision.HIGHEST
EPS_NORM = 1e-05
EPS_HEAD = 1e-06
ROPE_BASE = 10000.0
MASKED = -1e30


def rms_scale(value, gain, eps):
    return value * lax.rsqrt(jnp.mean(value * value, axis=-1, keepdims=True) + eps) * gain


def norm_rows(value, gain):
    return rms_scale(value, gain, EPS_NORM)


def rotate(value, cosine, sine):
    half = value.shape[-1] // 2
    first = value[..., :half]
    second = value[..., half:]
    return jnp.concatenate(
        [first * cosine - second * sine, second * cosine + first * sine], axis=-1
    )


def positions(lengths, seq_len):
    ends = jnp.cumsum(lengths)
    starts = ends - lengths
    index = jnp.arange(seq_len, dtype=jnp.int32)
    doc_ids = jnp.sum((index[:, None] >= ends[None, :]).astype(jnp.int32), axis=1)
    member = doc_ids[:, None] == jnp.arange(lengths.shape[0], dtype=jnp.int32)[None, :]
    offset = jnp.sum(jnp.where(member, starts[None, :], 0), axis=1)
    return (doc_ids, index - offset)


def rope_tables(position, head_dim):
    half = head_dim // 2
    freq = ROPE_BASE ** (-(2.0 * jnp.arange(half, dtype=jnp.float32)) / head_dim)
    angle = position.astype(jnp.float32)[:, None] * freq[None, :]
    return (jnp.cos(angle), jnp.sin(angle))


def activate(pair):
    half = pair.shape[-1] // 2
    return jax.nn.silu(pair[..., :half]) * pair[..., half:]


def send_wide(parcel):
    return lax.all_to_all(parcel, "ep", split_axis=1, concat_axis=1, tiled=True)


def share_group(parcel):
    return lax.all_gather(parcel, "tp", axis=0, tiled=True)


def per_device(
    layer_input,
    routes,
    doc_lengths,
    norm1_gain,
    w_qkv,
    q_gain,
    k_gain,
    w_out,
    norm2_gain,
    w_router,
    expert_gate_up,
    expert_down,
    d_out,
):
    tok_rows, model_width = layer_input.shape
    tp_count = lax.axis_size("tp")
    ep_count = lax.axis_size("ep")
    seq_len = tok_rows * tp_count
    route_count = routes.shape[1]
    experts_all = w_router.shape[1]
    local_experts = expert_gate_up.shape[0]
    hidden_local = expert_down.shape[1]
    head_dim = q_gain.shape[0]
    qkv_local = w_qkv.shape[2]
    heads_local = qkv_local // head_dim
    capacity = min(3 * tok_rows * route_count // (2 * experts_all), tok_rows)
    block_rows = min(512, seq_len)
    blocks = seq_len // block_rows
    own_rows = ep_count * capacity
    all_rows = tp_count * own_rows
    buffer_rows = ep_count * capacity * local_experts
    inputs = layer_input.astype(jnp.float32)
    gain_one = norm1_gain.astype(jnp.float32)
    normed_one, norm_one_back = jax.vjp(norm_rows, inputs, gain_one)
    h_one = normed_one.astype(jnp.bfloat16)
    h_all = lax.all_gather(h_one, "tp", axis=0, tiled=True)
    w_flat = w_qkv.reshape(model_width, 3 * qkv_local)
    projected = jnp.dot(h_all, w_flat, preferred_element_type=jnp.float32).reshape(
        seq_len, 3, heads_local, head_dim
    )
    q_raw = projected[:, 0]
    k_raw = projected[:, 1]
    v_raw = projected[:, 2]
    doc_ids, position = positions(doc_lengths[0], seq_len)
    cosine, sine = rope_tables(position, head_dim)
    cosine = cosine[:, None, :]
    sine = sine[:, None, :]

    def shape_heads(value, gain):
        return rotate(rms_scale(value, gain, EPS_HEAD), cosine, sine)

    q_rot, q_back = jax.vjp(shape_heads, q_raw, q_gain.astype(jnp.float32))
    k_rot, k_back = jax.vjp(shape_heads, k_raw, k_gain.astype(jnp.float32))
    queries = q_rot.astype(jnp.bfloat16)
    keys = k_rot.astype(jnp.bfloat16)
    values = v_raw.astype(jnp.bfloat16)
    scale = head_dim ** (-0.5)
    q_blocks = queries.reshape(blocks, block_rows, heads_local, head_dim)
    doc_blocks = doc_ids.reshape(blocks, block_rows)

    def scores_of(q_block, doc_block):
        plain = (
            jnp.einsum("qhd,khd->hqk", q_block, keys, preferred_element_type=jnp.float32) * scale
        )
        return jnp.where((doc_block[:, None] == doc_ids[None, :])[None], plain, MASKED)

    def attend(item):
        q_block, doc_block = item
        scores = scores_of(q_block, doc_block)
        peak = jnp.max(scores, axis=-1, keepdims=True)
        lifted = jnp.exp(scores - peak)
        total = jnp.sum(lifted, axis=-1, keepdims=True)
        weights = (lifted / total).astype(jnp.bfloat16)
        mixed = jnp.einsum("hqk,khd->qhd", weights, values, preferred_element_type=jnp.float32)
        return (mixed, peak, total)

    mixed, peaks, totals = lax.map(attend, (q_blocks, doc_blocks))
    attn_vals = mixed.reshape(seq_len, qkv_local).astype(jnp.bfloat16)
    piece = attn_vals
    attn_out = lax.psum_scatter(
        jnp.dot(piece, w_out, preferred_element_type=jnp.float32).astype(jnp.bfloat16),
        "tp",
        scatter_dimension=0,
        tiled=True,
    ).astype(jnp.float32)
    middle = inputs + attn_out
    gain_two = norm2_gain.astype(jnp.float32)
    normed_two, norm_two_back = jax.vjp(norm_rows, middle, gain_two)
    h_two = normed_two.astype(jnp.bfloat16)
    logits = jnp.dot(h_two, w_router, preferred_element_type=jnp.float32)
    choose = routes[:, :, None] == jnp.arange(experts_all, dtype=jnp.int32)[None, None, :]
    chosen = jnp.sum(jnp.where(choose, logits[:, None, :], 0.0), axis=-1)
    probs, gate_back = jax.vjp(partial(jax.nn.softmax, axis=-1), chosen)
    flat = routes.reshape(-1)
    table = (flat[:, None] == jnp.arange(experts_all, dtype=jnp.int32)[None, :]).astype(jnp.int32)
    rank = jnp.sum((jnp.cumsum(table, axis=0) - table) * table, axis=1)
    slot = (
        flat // local_experts * (capacity * local_experts)
        + rank * local_experts
        + flat % local_experts
    )
    token_index = jnp.arange(tok_rows * route_count, dtype=jnp.int32) // route_count
    outgoing = jnp.zeros((buffer_rows, model_width), jnp.bfloat16).at[slot].set(h_two[token_index])
    outgoing = outgoing.reshape(1, ep_count, capacity, local_experts, model_width)
    arrived = share_group(send_wide(outgoing))
    expert_in = arrived.reshape(all_rows, local_experts, model_width)
    w_pair = expert_gate_up.reshape(local_experts, model_width, 2 * hidden_local)
    gate_up = jnp.einsum("red,edf->ref", expert_in, w_pair, preferred_element_type=jnp.float32)
    hidden, act_back = jax.vjp(activate, gate_up)
    hidden_low = hidden.astype(jnp.bfloat16)
    piece = hidden_low
    expert_out = lax.psum_scatter(
        jnp.einsum("ref,efd->red", piece, expert_down, preferred_element_type=jnp.float32).astype(
            jnp.bfloat16
        ),
        "tp",
        scatter_dimension=0,
        tiled=True,
    )
    returned = lax.all_to_all(
        expert_out.reshape(ep_count, capacity, local_experts, model_width),
        "ep",
        split_axis=0,
        concat_axis=0,
        tiled=True,
    )
    picked = (
        returned.reshape(buffer_rows, model_width)[slot]
        .reshape(tok_rows, route_count, model_width)
        .astype(jnp.float32)
    )
    mixture = jnp.sum(probs[:, :, None] * picked, axis=1)
    output = (middle + mixture).astype(jnp.bfloat16)
    grad_out = d_out.astype(jnp.float32)
    grad_probs = jnp.sum(picked * grad_out[:, None, :], axis=-1)
    grad_picked = (probs[:, :, None] * grad_out[:, None, :]).astype(jnp.bfloat16)
    back_send = (
        jnp.zeros((buffer_rows, model_width), jnp.bfloat16)
        .at[slot]
        .set(grad_picked.reshape(-1, model_width))
    )
    back_send = back_send.reshape(ep_count, capacity, local_experts, model_width)
    back_in = lax.all_to_all(back_send, "ep", split_axis=0, concat_axis=0, tiled=True).reshape(
        own_rows, local_experts, model_width
    )
    piece = lax.all_gather(back_in, "tp", axis=0, tiled=True)
    grad_down_part = jnp.einsum(
        "ref,red->efd", hidden_low, piece, preferred_element_type=jnp.float32
    )
    grad_hidden_part = jnp.einsum(
        "red,efd->ref", piece, expert_down, preferred_element_type=jnp.float32
    )
    grad_pair_low = act_back(grad_hidden_part)[0].astype(jnp.bfloat16)
    grad_pair = jnp.einsum(
        "red,ref->edf", expert_in, grad_pair_low, preferred_element_type=jnp.float32
    )
    grad_gate_up = grad_pair.reshape(local_experts, model_width, 2, hidden_local)
    piece = grad_pair_low
    back_out = lax.psum_scatter(
        jnp.einsum("ref,edf->red", piece, w_pair, preferred_element_type=jnp.float32).astype(
            jnp.bfloat16
        ),
        "tp",
        scatter_dimension=0,
        tiled=True,
    )
    grad_sent = lax.all_to_all(
        back_out.reshape(ep_count, capacity, local_experts, model_width),
        "ep",
        split_axis=0,
        concat_axis=0,
        tiled=True,
    )
    grad_routes = (
        grad_sent.reshape(buffer_rows, model_width)[slot]
        .reshape(tok_rows, route_count, model_width)
        .astype(jnp.float32)
    )
    grad_chosen = gate_back(grad_probs)[0]
    grad_logits = jnp.sum(jnp.where(choose, grad_chosen[:, :, None], 0.0), axis=1)
    grad_router = jnp.dot(h_two.astype(jnp.float32).T, grad_logits, precision=HIGH)
    grad_h_two = jnp.sum(grad_routes, axis=1) + jnp.dot(
        grad_logits, w_router.astype(jnp.float32).T, precision=HIGH
    )
    grad_mid_norm, grad_gain_two = norm_two_back(grad_h_two)
    grad_mid = grad_out + grad_mid_norm
    grad_attn = grad_mid.astype(jnp.bfloat16)
    piece = lax.all_gather(grad_attn, "tp", axis=0, tiled=True)
    grad_wout = lax.dot_general(
        attn_vals, piece, (((0,), (0,)), ((), ())), preferred_element_type=jnp.float32
    )
    grad_vals = lax.dot_general(
        piece, w_out, (((1,), (1,)), ((), ())), preferred_element_type=jnp.float32
    )
    grad_wout, grad_vals = (grad_wout, grad_vals)
    grad_mixed = grad_vals.astype(jnp.bfloat16).reshape(blocks, block_rows, heads_local, head_dim)

    def attend_back(carry, item):
        grad_keys, grad_values = carry
        q_block, doc_block, peak, total, grad_block = item
        scores = scores_of(q_block, doc_block)
        probs_full = jnp.exp(scores - peak) / total
        weights = probs_full.astype(jnp.bfloat16)
        grad_weights = jnp.einsum(
            "qhd,khd->hqk", grad_block, values, preferred_element_type=jnp.float32
        )
        delta = jnp.sum(grad_weights * probs_full, axis=-1, keepdims=True)
        grad_scores = (probs_full * (grad_weights - delta)).astype(jnp.bfloat16)
        grad_q = (
            jnp.einsum("hqk,khd->qhd", grad_scores, keys, preferred_element_type=jnp.float32)
            * scale
        )
        grad_keys = (
            grad_keys
            + jnp.einsum("hqk,qhd->khd", grad_scores, q_block, preferred_element_type=jnp.float32)
            * scale
        )
        grad_values = grad_values + jnp.einsum(
            "hqk,qhd->khd", weights, grad_block, preferred_element_type=jnp.float32
        )
        return ((grad_keys, grad_values), grad_q)

    head_zeros = jnp.zeros((seq_len, heads_local, head_dim), jnp.float32)
    (grad_keys, grad_values), grad_queries = lax.scan(
        attend_back, (head_zeros, head_zeros), (q_blocks, doc_blocks, peaks, totals, grad_mixed)
    )
    grad_queries = grad_queries.reshape(seq_len, heads_local, head_dim)
    grad_q_raw, grad_q_gain = q_back(grad_queries)
    grad_k_raw, grad_k_gain = k_back(grad_keys)
    grad_proj = (
        jnp.stack([grad_q_raw, grad_k_raw, grad_values], axis=1)
        .reshape(seq_len, 3 * qkv_local)
        .astype(jnp.bfloat16)
    )
    grad_wqkv = lax.dot_general(
        h_all, grad_proj, (((0,), (0,)), ((), ())), preferred_element_type=jnp.float32
    )
    piece = grad_proj
    grad_h_one = lax.psum_scatter(
        lax.dot_general(
            piece, w_flat, (((1,), (1,)), ((), ())), preferred_element_type=jnp.float32
        ).astype(jnp.bfloat16),
        "tp",
        scatter_dimension=0,
        tiled=True,
    ).astype(jnp.float32)
    grad_in_norm, grad_gain_one = norm_one_back(grad_h_one)
    grad_input = grad_mid + grad_in_norm
    dense_qkv, dense_out = (
        lax.psum_scatter(
            grad_wqkv.astype(jnp.bfloat16), "ep", scatter_dimension=0, tiled=True
        ).astype(jnp.float32),
        lax.psum_scatter(
            grad_wout.astype(jnp.bfloat16), "ep", scatter_dimension=1, tiled=True
        ).astype(jnp.float32),
    )
    summed = lax.psum(
        (grad_gain_one, grad_gain_two, grad_q_gain, grad_k_gain, grad_router), ("ep", "tp")
    )
    dense_qkv = dense_qkv.reshape(dense_qkv.shape[0], 3, qkv_local)
    return (
        output,
        grad_input,
        summed[0],
        dense_qkv,
        summed[2],
        summed[3],
        dense_out,
        summed[1],
        summed[4],
        grad_gate_up,
        grad_down_part,
    )


def solution(mesh):
    in_specs = (
        P(("ep", "tp"), None),
        P(("ep", "tp"), None),
        P("ep", None),
        P(),
        P(None, None, "tp"),
        P(),
        P(),
        P("tp", None),
        P(),
        P(),
        P("ep", None, None, "tp"),
        P("ep", "tp", None),
        P(("ep", "tp"), None),
    )
    out_specs = (
        P(("ep", "tp"), None),
        P(("ep", "tp"), None),
        P(),
        P("ep", None, "tp"),
        P(),
        P(),
        P("tp", "ep"),
        P(),
        P(),
        P("ep", None, None, "tp"),
        P("ep", "tp", None),
    )
    return jax.shard_map(
        per_device, mesh=mesh, in_specs=in_specs, out_specs=out_specs, check_vma=False
    )
```

profile of v0, /device:TPU:0, one launch (start us, length us, event | category | flops | bytes accessed | tf_op | source)
XLA Modules:
  0.0 2741.7 jit_solution(15502196323829342674)
XLA Ops:
  13.4 8.9 copy.136
  23.7 26.9 all-gather.5.cloned.1.call-done
  50.6 10.1 fusion.37
  77.2 19.3 while.29
  83.4 3.6 fusion.125
  92.9 3.6 fusion.125
  100.0 4.4 convolution_convert_fusion.2
  106.3 16.3 reduce-window.11
  125.3 23.9 reduce-scatter.7.cloned.1.call-done
  153.4 46.8 %scatter_custom_fusion = bf16[3072,2048]{1,0:T(8,128)(2,1)} fusion(s32[2048]{0:T(1024)S(1)} %bitcast.252, bf16[256,2048]{1,0:T(8,128)(2,1)} %multiply_convert_fusion.2, s32[2048]{0:T(1024)S(1)} %broadcast_clamp_fusion.1, bf16[]{:T(256)} %constant.125.clone.1), kind=kCustom, calls=%fused_computation.65 | custom fusion | bytes 12583424 | tf_op jit(solution)/shard_map/scatter | solution.py:165
  200.3 19.0 reshape.623
  219.3 278.3 %all_to_all.20 = bf16[1,8,96,4,2048]{4,3,2,0,1:T(4,128)(2,1)S(1)} all-to-all(bf16[1,8,96,4,2048]{4,3,2,0,1:T(4,128)(2,1)} %bitcast.234), channel_id=1, replica_groups=mesh['ep'=8,'tp'=4] {'ep'}, dimensions={1} | all-to-all | bytes 25165824 | tf_op jit(solution)/shard_map/all_to_all | solution.py:55
  497.6 8.8 copy.149
  511.3 24.2 scatter_custom_fusion.1
  535.5 19.6 reshape.628
  555.0 276.6 %all_to_all.21 = bf16[8,96,4,2048]{3,2,1,0:T(4,128)(2,1)S(1)} all-to-all(bf16[8,96,4,2048]{3,2,1,0:T(4,128)(2,1)} %reshape.628), channel_id=1, replica_groups=mesh['ep'=8,'tp'=4] {'ep'}, dimensions={0} | all-to-all | bytes 25165824 | tf_op jit(solution)/shard_map/all_to_all | solution.py:205
  831.6 16.3 copy.154
  848.0 15.6 reshape.625
  863.6 38.4 %copy.150 = bf16[4,8,96,4,2048]{4,2,1,0,3:T(8,128)(2,1)} copy(bf16[4,8,96,4,2048]{4,2,3,1,0:T(8,128)(2,1)} %all-gather.7.cloned.1.call-done) | data formatting | bytes 100663296 | tf_op jit(solution)/shard_map/all_gather | solution.py:59
  902.0 37.0 %convolution_bitcast_fusion = f32[3072,4,512]{2,0,1:T(8,128)} fusion(bf16[3072,4,2048]{2,0,1:T(8,128)(2,1)} %bitcast.231, bf16[4,2048,512]{2,1,0:T(8,128)(2,1)} %reshape.625), kind=kOutput, calls=%fused_computation.63 | convolution fusion | flops 25769803776 | bytes 83886080 | tf_op jit(solution)/shard_map/red,edf->ref/dot_general | solution.py:170
  939.0 203.9 %all-gather.9.cloned.1.call-done = bf16[3072,4,2048]{2,0,1:T(8,128)(2,1)} async-done(((bf16[768,4,2048]{2,0,1:T(8,128)(2,1)}), bf16[3072,4,2048]{2,0,1:T(8,128)(2,1)}) %all-gather.9.cloned.1.call-update) | async-done | bytes 50331664 | tf_op jit(solution)/shard_map/all_gather | solution.py:208
  1142.9 40.5 %bitcast_multiply_fusion.2 = (f32[3072,4,256]{2,0,1:T(8,128)}, f32[3072,4,256]{2,0,1:T(8,128)}, bf16[3072,4,256]{2,0,1:T(8,128)(2,1)}) fusion(f32[3072,4,512]{2,0,1:T(8,128)} %convolution_bitcast_fusion, bf16[3072,4,2048]{2,0,1:T(8,128)(2,1)} %all-gather.9.cloned.1.call-done, bf16[4,256,2048]{2,1,0:T(8,128)(2,1)} %param.28), kind=kOutput, calls=%fused_computation.59 | convolution fusion | flops 12928942080 | bytes 111149056 | tf_op jit(solution)/shard_map/red,efd->ref/dot_general | solution.py:212
  1183.4 23.4 convert_bitcast_fusion.1
  1206.9 40.3 %convert_bitcast_fusion = bf16[3072,4,2048]{2,0,1:T(8,128)(2,1)} fusion(bf16[4,2048,512]{2,1,0:T(8,128)(2,1)} %reshape.625, f32[3072,4,256]{2,0,1:T(8,128)} %get-tuple-element.398, f32[3072,4,256]{2,0,1:T(8,128)} %get-tuple-element.397), kind=kOutput, calls=%fused_computation.45 | convolution fusion | flops 25807552512 | bytes 83886080 | tf_op jit(solution)/shard_map/ref,edf->red/dot_general | solution.py:222
  1247.2 306.2 %reduce-scatter.9.cloned.1.call-done = bf16[768,4,2048]{2,0,1:T(8,128)(2,1)} async-done(((bf16[3072,4,2048]{2,0,1:T(8,128)(2,1)}), bf16[768,4,2048]{2,0,1:T(8,128)(2,1)}) %reduce-scatter.9.cloned.1.call-update) | async-done | bytes 12582928 | tf_op jit(solution)/shard_map/reduce_scatter | solution.py:174
  1553.5 11.3 copy.151
  1564.8 5.9 all-to-all-start.1
  1570.7 331.7 %reduce-scatter.11.cloned.1.call-done = bf16[768,4,2048]{2,0,1:T(8,128)(2,1)} async-done(((bf16[3072,4,2048]{2,0,1:T(8,128)(2,1)}), bf16[768,4,2048]{2,0,1:T(8,128)(2,1)}) %reduce-scatter.11.cloned.1.call-update) | async-done | bytes 12582928 | tf_op jit(solution)/shard_map/reduce_scatter | solution.py:221
  1902.4 10.8 copy.155
  1913.2 5.5 all-to-all-start.3
  1918.8 15.8 copy.152
  1934.6 18.1 reshape.627
  1952.7 22.5 gather_fusion
  1975.3 9.7 fusion.24
  1985.1 206.5 %all-to-all-done.3 = bf16[8,96,4,2048]{3,1,2,0:T(8,128)(2,1)} async-done(((bf16[8,96,4,2048]{3,1,2,0:T(8,128)(2,1)}), bf16[8,96,4,2048]{3,1,2,0:T(8,128)(2,1)}, u32[]{:S(2)}, u32[]{:S(2)}) %all-to-all-start.3) | async-done | bytes 12582944 | tf_op jit(solution)/shard_map/all_to_all | solution.py:229
  2191.7 15.6 copy.156
  2207.2 18.1 reshape.631
  2225.3 22.9 gather_fusion.1
  2248.2 11.4 convert_reduce_fusion
  2259.7 4.4 multiply_reduce_fusion.1
  2267.5 32.7 %all-gather.11.cloned.1.call-done = bf16[1024,2048]{1,0:T(8,128)(2,1)} async-done(((bf16[256,2048]{1,0:T(8,128)(2,1)}), bf16[1024,2048]{1,0:T(8,128)(2,1)}) %all-gather.11.cloned.1.call-update) | async-done | bytes 4194320 | tf_op jit(solution)/shard_map/all_gather | solution.py:250
  2300.1 6.3 convolution_convert_fusion.3
  2306.7 4.5 convolution_convert_fusion.4
  2312.3 97.0 %while.30 = (s32[]{:T(128)}, f32[1024,4,128]{0,2,1:T(8,128)}, f32[1024,4,128]{0,2,1:T(8,128)}, f32[2,512,4,128]{1,0,3,2:T(2,128)}, bf16[2,512,4,128]{3,1,2,0:T(8...) while((s32[]{:T(128)}, f32[1024,4,128]{0,2,1:T(8,128)}, ...), condition=%wide.region_30.31_spmd.clone, body=%wide.region_28.30_spmd.clone.sunk | while | flops 2708731904 | bytes 142683392 | solution.py:286
  2312.8 4.3 exponential_divide_fusion.2
  2326.8 3.6 copy.223
  2330.4 19.6 dynamic_update_slice.23
  2350.1 4.7 bitcast_add_fusion.4
  2354.8 5.5 bitcast_add_fusion.5
  2360.7 4.2 exponential_divide_fusion.2
  2374.6 3.6 copy.223
  2378.2 19.6 dynamic_update_slice.23
  2397.9 5.4 bitcast_add_fusion.4
  2403.2 6.1 bitcast_add_fusion.5
  2409.4 4.3 reshape.633
  2425.1 8.7 convolution_convert_fusion.1
  2433.9 11.6 convolution_convert_fusion
  2445.6 45.6 %fusion.49 = f32[4,2048,512]{1,2,0:T(8,128)} fusion(bf16[3072,4,2048]{2,0,1:T(8,128)(2,1)} %bitcast.232, f32[3072,4,256]{2,0,1:T(8,128)} %get-tuple-element.398, f32[3072,4,256]{2,0,1:T(8,128)} %get-tuple-element.397), kind=kOutput, calls=%fused_computation.118 | convolution fusion | flops 25782386688 | bytes 92274688 | tf_op jit(solution)/shard_map/red,ref->edf/dot_general | solution.py:216
  2491.2 25.1 copy.167
  2516.3 25.3 fusion.72
  2548.4 6.5 fusion.46
  2554.9 41.9 %all-reduce.6 = (f32[2048]{0:T(1024)}, f32[128]{0:T(128)}, f32[128]{0:T(128)}, f32[2048]{0:T(1024)}) all-reduce(f32[2048]{0:T(1024)S(1)} %get-tuple-element.341, f32[128]{0:T(128)S(1)} %get-tuple-element.336, f32[128]{0:T(128)S(1)} %get-tuple-element.329, f32[2048]{0:T(1024)S(1)} %copy-done.52), channel_id=1, replica_groups=mesh['ep'=8,'tp'=4] {'ep','tp'}, use_global_device_ids=true, to_apply=%region_36.37 | all-reduce | flops 4352 | bytes 34816 | tf_op jit(solution)/shard_map/psum | solution.py:319
  2596.7 4.5 reduce-scatter.15.cloned.1.call-done
  2606.8 126.2 %all-reduce.9.cloned.1.call-done = f32[2048,32]{0,1:T(8,128)} async-done(((f32[2048,32]{0,1:T(8,128)}), f32[2048,32]{0,1:T(8,128)}) %all-reduce.9.cloned.1.call-update) | async-done | bytes 262160 | tf_op jit(solution)/shard_map/psum | solution.py:319
  (302 shorter events, 103.2 us)
Async XLA Ops:
  7.2 92.8 %copy-start = (bf16[512,2048]{1,0:T(8,128)(2,1)S(1)}, bf16[512,2048]{1,0:T(8,128)(2,1)}, u32[]{:S(2)}) copy-start(bf16[512,2048]{1,0:T(8,128)(2,1)} %param.24) | copy-start | bytes 6291460
  7.2 43.4 %all-gather.5.cloned.1.call-start = ((), (), s32[]{:S(2)}) async-start(), calls=%async_computation.10 | async-start | bytes 5242880 | tf_op jit(solution)/shard_map/all_gather | solution.py:98
  13.3 135.9 %reduce-scatter.7.cloned.1.call-start = ((), (), s32[]{:S(2)}) async-start(), calls=%async_computation.11 | async-start | bytes 5242880 | tf_op jit(solution)/shard_map/reduce_scatter | solution.py:142
  13.4 8.9 copy-start.75
  13.4 8.9 copy-start.76
  13.4 8.9 copy-start.77
  22.3 40.8 %copy-start.70 = (f32[128]{0:T(128)}, f32[128]{0:T(128)S(1)}, u32[]{:S(2)}) copy-start(f32[128]{0:T(128)S(1)} %convert_element_type.151) | copy-start | bytes 1540
  22.3 40.8 %copy-start.72 = (f32[128]{0:T(128)}, f32[128]{0:T(128)S(1)}, u32[]{:S(2)}) copy-start(f32[128]{0:T(128)S(1)} %convert_element_type.153) | copy-start | bytes 1540
  23.7 40.2 %copy-start.16 = (f32[1024,64]{0,1:T(8,128)}, f32[1024,64]{0,1:T(8,128)S(1)}, u32[]{:S(2)}) copy-start(f32[1024,64]{0,1:T(8,128)S(1)} %get-tuple-element.418) | copy-start | bytes 786436
  23.7 40.2 %copy-start.18 = (f32[1024,64]{0,1:T(8,128)}, f32[1024,64]{0,1:T(8,128)S(1)}, u32[]{:S(2)}) copy-start(f32[1024,64]{0,1:T(8,128)S(1)} %get-tuple-element.419) | copy-start | bytes 786436
  96.6 7.8 copy-start.23
  96.6 7.8 copy-start.42
  96.6 7.8 copy-start.46
  96.6 7.8 copy-start.48
  104.4 44.8 %copy-start.3 = (bf16[256,2048]{1,0:T(8,128)(2,1)S(1)}, bf16[256,2048]{1,0:T(8,128)(2,1)}, u32[]{:S(2)}) copy-start(bf16[256,2048]{1,0:T(8,128)(2,1)} %param.17) | copy-start | bytes 3145732
  104.4 759.2 %all-gather.7.cloned.1.call-start = ((), (), s32[]{:S(2)}) async-start(), calls=%async_computation.12 | async-start | bytes 62914560 | tf_op jit(solution)/shard_map/all_gather | solution.py:59
  105.6 94.7 %copy-start.35 = (f32[2048]{0:T(1024)}, f32[2048]{0:T(1024)S(1)}, u32[]{:S(2)}) copy-start(f32[2048]{0:T(1024)S(1)} %convert_element_type.159) | copy-start | bytes 24580
  125.3 386.0 %copy-start.53 = (s32[2048,1]{0,1:T(1,128)}, s32[2048,1]{0,1:T(1,128)S(1)}, u32[]{:S(2)}) copy-start(s32[2048,1]{0,1:T(1,128)S(1)} %compare_select_fusion.1) | copy-start | bytes 24580
  150.8 49.4 %copy-start.66 = (f32[256]{0:T(256)}, f32[256]{0:T(256)S(1)}, u32[]{:S(2)}) copy-start(f32[256]{0:T(256)S(1)} %multiply_reduce_fusion.7) | copy-start | bytes 3076
  150.8 49.4 %copy-start.57 = (f32[256]{0:T(256)}, f32[256]{0:T(256)S(1)}, u32[]{:S(2)}) copy-start(f32[256]{0:T(256)S(1)} %fusion.65) | copy-start | bytes 3076
  506.4 636.5 %all-gather.9.cloned.1.call-start = ((), (), s32[]{:S(2)}) async-start(), calls=%async_computation.14 | async-start | bytes 62914560 | tf_op jit(solution)/shard_map/all_gather | solution.py:208
  511.1 24.3 copy-start.20
  848.0 705.5 %reduce-scatter.9.cloned.1.call-start = ((), (), s32[]{:S(2)}) async-start(), calls=%async_computation.13 | async-start | bytes 62914560 | tf_op jit(solution)/shard_map/reduce_scatter | solution.py:174
  1206.8 695.6 %reduce-scatter.11.cloned.1.call-start = ((), (), s32[]{:S(2)}) async-start(), calls=%async_computation.15 | async-start | bytes 62914560 | tf_op jit(solution)/shard_map/reduce_scatter | solution.py:221
  1564.8 348.4 %all-to-all-start.1 = ((bf16[8,96,4,2048]{3,1,2,0:T(8,128)(2,1)}), bf16[8,96,4,2048]{3,1,2,0:T(8,128)(2,1)}, u32[]{:S(2)}, u32[]{:S(2)}) async-start(bf16[8,96,4,2048]{3,1,2,0:T(8,128)(2,1)} %copy.151), calls=%async_computation.3 | async-start | bytes 25165824 | tf_op jit(solution)/shard_map/all_to_all | solution.py:182
  1913.2 5.6 copy-start.54
  1913.2 5.6 copy-start.61
  1913.2 278.4 %all-to-all-start.3 = ((bf16[8,96,4,2048]{3,1,2,0:T(8,128)(2,1)}), bf16[8,96,4,2048]{3,1,2,0:T(8,128)(2,1)}, u32[]{:S(2)}, u32[]{:S(2)}) async-start(bf16[8,96,4,2048]{3,1,2,0:T(8,128)(2,1)} %copy.155), calls=%async_computation.6 | async-start | bytes 25165824 | tf_op jit(solution)/shard_map/all_to_all | solution.py:229
  1918.7 381.4 %all-gather.11.cloned.1.call-start = ((), (), s32[]{:S(2)}) async-start(), calls=%async_computation.16 | async-start | bytes 5242880 | tf_op jit(solution)/shard_map/all_gather | solution.py:250
  1952.7 22.5 copy-start.21
  1975.2 9.8 copy-start.30
  1975.2 9.8 copy-start.56
  1975.2 9.8 copy-start.51
  1985.1 274.5 %copy-start.27 = (f32[256,32]{0,1:T(8,128)}, f32[256,32]{0,1:T(8,128)S(1)}, u32[]{:S(2)}) copy-start(f32[256,32]{0,1:T(8,128)S(1)} %select_reduce_fusion) | copy-start | bytes 98308
  2248.2 11.4 copy-start.4
  2248.2 11.4 copy-start.26
  2248.2 11.4 copy-start.36
  2248.2 11.4 copy-start.58
  2259.7 4.4 copy-start.67
  2259.7 5.7 copy-start.10
  2259.7 5.7 copy-start.14
  2264.1 42.3 %copy-start.68 = (f32[256]{0:T(256)}, f32[256]{0:T(256)S(1)}, u32[]{:S(2)}) copy-start(f32[256]{0:T(256)S(1)} %multiply_multiply_fusion.5) | copy-start | bytes 3076
  2267.4 276.9 %reduce-scatter.17.cloned.1.call-start = ((), (), s32[]{:S(2)}) async-start(), calls=%async_computation.19 | async-start | bytes 2359296 | tf_op jit(solution)/shard_map/reduce_scatter | solution.py:315
  2306.4 5.9 copy-start.24
  2306.4 5.9 copy-start.43
  2306.4 5.9 copy-start.47
  2306.4 5.9 copy-start.49
  2306.4 239.6 %reduce-scatter.13.cloned.1.call-start = ((), (), s32[]{:S(2)}) async-start(), calls=%async_computation.17 | async-start | bytes 5242880 | tf_op jit(solution)/shard_map/reduce_scatter | solution.py:301
  2312.8 4.4 copy-start.12
  2312.8 4.5 copy-start.9
  2360.7 4.4 copy-start.9
  2419.5 5.6 slice-start
  2419.5 5.6 slice-start.1
  2433.9 167.4 %reduce-scatter.15.cloned.1.call-start = ((), (), s32[]{:S(2)}) async-start(), calls=%async_computation.18 | async-start | bytes 7077888 | tf_op jit(solution)/shard_map/reduce_scatter | solution.py:312
  2445.5 287.5 %all-reduce.9.cloned.1.call-start = ((), (), s32[]{:S(2)}) async-start(), calls=%async_computation.20 | async-start | bytes 524288 | tf_op jit(solution)/shard_map/psum | solution.py:319
  2516.3 25.3 copy-start.28
  2516.3 29.7 %copy-start.5 = (bf16[256,2048]{1,0:T(8,128)(2,1)S(1)}, bf16[256,2048]{1,0:T(8,128)(2,1)}, u32[]{:S(2)}) copy-start(bf16[256,2048]{1,0:T(8,128)(2,1)} %param.17) | copy-start | bytes 3145732
  2516.3 29.7 %copy-start.45 = (f32[2048]{0:T(1024)S(1)}, f32[2048]{0:T(1024)}, u32[]{:S(2)}) copy-start(f32[2048]{0:T(1024)} %copy-done.44) | copy-start | bytes 24580
  2516.3 29.8 %copy-start.63 = (f32[256]{0:T(256)S(1)}, f32[256]{0:T(256)}, u32[]{:S(2)}) copy-start(f32[256]{0:T(256)} %copy-done.62) | copy-start | bytes 3076
  2541.6 6.7 copy-start.65
  2541.6 6.8 copy-start.37
  2541.6 6.8 copy-start.59
  2541.6 6.8 copy-start.69
  2548.4 6.5 copy-start.52
  (33 other events, 73.9 us)
Sparse Core Ops, SparseCore 0:
  13.4 37.1 all-gather.4
  104.5 44.5 reduce-scatter.6
  506.5 295.2 all-gather.6
  848.1 294.7 all-gather.8
  1206.9 346.4 reduce-scatter.8
  1555.9 346.4 reduce-scatter.10
  2267.5 32.5 all-gather.10
  2306.5 68.8 reduce-scatter.16
  2434.0 44.5 reduce-scatter.12
  2482.0 119.1 reduce-scatter.14
  2607.3 125.6 all-reduce.8
where the time goes:
time: 2760 us; the launch traced here: 2740 us
  waiting for transfers between devices  1260 us (46%)
  blocking collectives  597 us (22%)
  local copies, waits for them, and re-layouts  424 us (15%)
  matrix products  319 us (12%)
  other arithmetic  112 us (4%)
    reduce_scatter x1, waiting for transfers between devices, per_device(): lax.psum_scatter(jnp.einsum('ref,edf->red', piece, w_pair, preferred_elem...  332 us
    reduce_scatter x1, waiting for transfers between devices, per_device(): lax.psum_scatter(jnp.einsum('ref,efd->red', piece, expert_down, preferred...  306 us
    all_to_all x1, blocking collectives, send_wide(): return lax.all_to_all(parcel, 'ep', split_axis=1, concat_axis=1, tiled=True)  278 us
    all_to_all x1, blocking collectives, per_device(): lax.all_to_all(back_send, 'ep', split_axis=0, concat_axis=0, tiled=True)  277 us
    all_to_all x1, waiting for transfers between devices, per_device(): lax.all_to_all(back_out.reshape(ep_count, capacity, local_experts, model_...  207 us
    all_gather x1, waiting for transfers between devices, per_device(): piece = lax.all_gather(back_in, 'tp', axis=0, tiled=True)  204 us
    psum x1, waiting for transfers between devices, per_device(): lax.psum((grad_gain_one, grad_gain_two, grad_q_gain, grad_k_gain, grad_ro...  126 us
  transfers between devices with their start and end apart: 13, of which 9 were waited for; matrix products, arithmetic and copies ran while one was open for 20% of the time, Pallas kernels for 0%

commit v1 on v0

v1 whole, which is shorter than its diff:
```python
import jax
import jax.numpy as jnp
from jax import lax
from jax.sharding import Mesh
from jax.sharding import PartitionSpec as P

HIGH = lax.Precision.HIGHEST
EPS_NORM = 1e-05
EPS_HEAD = 1e-06
ROPE_BASE = 10000.0
MASKED = -1e30
F32 = jnp.float32
BF16 = jnp.bfloat16
PLANE = ("ep", "x")
GROUP = ("x", "core")
ALL = ("ep", "x", "core")


def norm_rows(value, gain):
    inverse = lax.rsqrt(jnp.mean(value * value, axis=-1, keepdims=True) + EPS_NORM)
    return value * inverse * gain


def norm_back(value, gain, grad):
    inverse = lax.rsqrt(jnp.mean(value * value, axis=-1, keepdims=True) + EPS_NORM)
    normed = value * inverse
    lifted = grad * gain
    inner = jnp.mean(lifted * normed, axis=-1, keepdims=True)
    return (lifted - normed * inner) * inverse, jnp.sum(grad * normed, axis=0)


def rms_scale(value, gain, eps):
    return value * lax.rsqrt(jnp.mean(value * value, axis=-1, keepdims=True) + eps) * gain


def rotate(value, cosine, sine):
    half = value.shape[-1] // 2
    first = value[..., :half]
    second = value[..., half:]
    return jnp.concatenate(
        [first * cosine - second * sine, second * cosine + first * sine], axis=-1
    )


def positions(lengths, seq_len):
    ends = jnp.cumsum(lengths)
    starts = ends - lengths
    index = jnp.arange(seq_len, dtype=jnp.int32)
    doc_ids = jnp.sum((index[:, None] >= ends[None, :]).astype(jnp.int32), axis=1)
    member = doc_ids[:, None] == jnp.arange(lengths.shape[0], dtype=jnp.int32)[None, :]
    offset = jnp.sum(jnp.where(member, starts[None, :], 0), axis=1)
    return (doc_ids, index - offset)


def rope_tables(position, head_dim):
    half = head_dim // 2
    freq = ROPE_BASE ** (-(2.0 * jnp.arange(half, dtype=F32)) / head_dim)
    angle = position.astype(F32)[:, None] * freq[None, :]
    return (jnp.cos(angle), jnp.sin(angle))


def einsum(spec, left, right):
    return jnp.einsum(spec, left, right, preferred_element_type=F32)


def swap_cores(value):
    return lax.ppermute(value, "core", [(0, 1), (1, 0)])


def gather(value, axes):
    return lax.all_gather(value, axes, axis=0, tiled=True)


def scatter(value, axes, dim=0):
    return lax.psum_scatter(value, axes, scatter_dimension=dim, tiled=True)


def masked_softmax(logits, mask):
    kept = jnp.where(mask, logits, MASKED)
    lifted = jnp.where(mask, jnp.exp(kept - jnp.max(kept, axis=-1, keepdims=True)), 0.0)
    return lifted / jnp.sum(lifted, axis=-1, keepdims=True)


def route_mask(routes, experts_all):
    ids = jnp.arange(experts_all, dtype=jnp.int32)
    return jnp.any(routes[:, :, None] == ids[None, None, :], axis=1)


def per_device(
    layer_input,
    routes,
    doc_lengths,
    norm1_gain,
    w_qkv,
    q_gain,
    k_gain,
    w_out,
    norm2_gain,
    w_router,
    expert_gate_up,
    expert_down,
    d_out,
):
    rows, width = layer_input.shape
    x_count = lax.axis_size("x")
    ep_count = lax.axis_size("ep")
    seq_len = rows * x_count * 2
    blocks = ep_count * x_count
    topk = routes.shape[1]
    experts_all = w_router.shape[1]
    local = expert_gate_up.shape[0]
    hidden_local = expert_down.shape[1]
    head_dim = q_gain.shape[0]
    qkv_local = w_qkv.shape[2]
    heads = qkv_local // head_dim
    capacity = min(3 * rows * topk // (2 * experts_all), rows)
    q_rows = min(512, seq_len)
    q_count = seq_len // q_rows
    scale = head_dim ** (-0.5)
    my_ep = lax.axis_index("ep")

    gain_one = norm1_gain.astype(F32)
    gain_two = norm2_gain.astype(F32)
    inputs = layer_input.astype(F32)
    grad_out = d_out.astype(F32)
    input_seq = gather(layer_input, GROUP)
    h_seq = norm_rows(input_seq.astype(F32), gain_one).astype(BF16)
    w_flat = w_qkv.reshape(width, 3 * qkv_local)
    projected = jnp.dot(h_seq, w_flat, preferred_element_type=F32).reshape(
        seq_len, 3, heads, head_dim
    )
    q_raw = projected[:, 0]
    k_raw = projected[:, 1]
    v_raw = projected[:, 2]
    doc_ids, position = positions(doc_lengths[0], seq_len)
    cosine, sine = rope_tables(position, head_dim)
    cosine = cosine[:, None, :]
    sine = sine[:, None, :]

    def shape_heads(value, gain):
        return rotate(rms_scale(value, gain, EPS_HEAD), cosine, sine)

    q_rot, q_back = jax.vjp(shape_heads, q_raw, q_gain.astype(F32))
    k_rot, k_back = jax.vjp(shape_heads, k_raw, k_gain.astype(F32))
    queries = q_rot.astype(BF16)
    keys = k_rot.astype(BF16)
    values = v_raw.astype(BF16)
    q_blocks = queries.reshape(q_count, q_rows, heads, head_dim)
    doc_blocks = doc_ids.reshape(q_count, q_rows)

    def scores_of(q_block, doc_block):
        plain = einsum("qhd,khd->hqk", q_block, keys) * scale
        return jnp.where((doc_block[:, None] == doc_ids[None, :])[None], plain, MASKED)

    def attend(item):
        q_block, doc_block = item
        scores = scores_of(q_block, doc_block)
        peak = jnp.max(scores, axis=-1, keepdims=True)
        lifted = jnp.exp(scores - peak)
        total = jnp.sum(lifted, axis=-1, keepdims=True)
        weights = (lifted / total).astype(BF16)
        return (einsum("hqk,khd->qhd", weights, values), peak, total)

    mixed, peaks, totals = lax.map(attend, (q_blocks, doc_blocks))
    attn_vals = mixed.reshape(seq_len, qkv_local).astype(BF16)
    attn_out = scatter(jnp.dot(attn_vals, w_out, preferred_element_type=F32).astype(BF16), GROUP)
    middle = inputs + attn_out.astype(F32)
    h_two = norm_rows(middle, gain_two).astype(BF16)

    g_plane = gather(d_out, PLANE).reshape(blocks, rows, width)
    routes_plane = gather(routes, PLANE)
    h_flat = gather(h_two, PLANE)
    h_plane = h_flat.reshape(blocks, rows, width)
    gate_own = expert_gate_up[:, :, 0]
    up_own = expert_gate_up[:, :, 1]
    pair_other = swap_cores(expert_gate_up.reshape(local, width, 2 * hidden_local))
    down_other = swap_cores(expert_down)
    pair_own = expert_gate_up.reshape(local, width, 2 * hidden_local)

    mask_plane = route_mask(routes_plane, experts_all)
    logits_plane = jnp.dot(h_flat, w_router, preferred_element_type=F32)
    probs_plane = masked_softmax(logits_plane, mask_plane)
    first = my_ep * local
    mask_here = lax.dynamic_slice_in_dim(mask_plane, first, local, axis=1)
    probs_here = lax.dynamic_slice_in_dim(probs_plane, first, local, axis=1)
    mask_here = mask_here.reshape(blocks, rows, local).transpose(0, 2, 1)
    probs_here = probs_here.reshape(blocks, rows, local).transpose(0, 2, 1)
    before = jnp.triu(jnp.ones((rows, rows), BF16), 1)
    rank = einsum("bet,tu->beu", mask_here.astype(BF16), before).astype(jnp.int32)
    slots = jnp.arange(capacity, dtype=jnp.int32)[None, None, :, None]
    picks = mask_here[:, :, None, :] & (rank[:, :, None, :] == slots)
    pick = picks.astype(BF16)
    prob_rows = jnp.sum(jnp.where(picks, probs_here[:, :, None, :], 0.0), axis=-1)
    prob_rows = prob_rows.transpose(1, 0, 2)[..., None]

    g_rows = einsum("bect,btd->ebcd", pick, g_plane).astype(BF16)
    h_rows = einsum("bect,btd->ebcd", pick, h_plane).astype(BF16)

    def expert_half(pair, down):
        gate = einsum("ebcd,edf->ebcf", h_rows, pair[:, :, :hidden_local])
        up = einsum("ebcd,edf->ebcf", h_rows, pair[:, :, hidden_local:])
        back = einsum("ebcd,efd->ebcf", g_rows, down)
        sigma = jax.nn.sigmoid(gate)
        silu = gate * sigma
        hidden = (silu * up).astype(BF16).astype(F32)
        dots = jnp.sum(hidden * back, axis=-1)
        weighted = (hidden * prob_rows).astype(BF16)
        grad_hidden = back * prob_rows
        grad_gate = (grad_hidden * up * (sigma + silu * (1.0 - sigma))).astype(BF16)
        grad_up = (grad_hidden * silu).astype(BF16)
        return dots, weighted, jnp.concatenate([grad_gate, grad_up], axis=-1)

    dots_own, weighted_own, ggu_own = expert_half(pair_own, expert_down)
    dots_other, weighted_other, ggu_other = expert_half(pair_other, down_other)
    back_rows = (
        einsum("ebcf,edf->ebcd", ggu_own, pair_own)
        + einsum("ebcf,edf->ebcd", ggu_other, pair_other)
    ).astype(BF16)
    out_rows = (
        einsum("ebcf,efd->ebcd", weighted_own, expert_down)
        + einsum("ebcf,efd->ebcd", weighted_other, down_other)
    ).astype(BF16)
    dot_rows = (dots_own + dots_other).transpose(1, 0, 2)
    dots_token = jnp.sum(jnp.where(picks, dot_rows[..., None], 0.0), axis=2)
    dots_token = dots_token.transpose(0, 2, 1).reshape(blocks * rows, local)
    dots_high = dots_token.astype(BF16)
    dots_low = (dots_token - dots_high.astype(F32)).astype(BF16)
    my_x = lax.axis_index("x")
    placed = jnp.zeros((blocks * rows, x_count, 2, experts_all), BF16)
    placed = lax.dynamic_update_slice(
        placed,
        jnp.stack([dots_high, dots_low], axis=1)[:, None],
        (0, my_x, 0, first),
    ).reshape(blocks * rows, x_count * 2 * experts_all)
    back_part = einsum("bect,ebcd->btd", pick, back_rows).astype(BF16)
    back_sum = scatter(
        jnp.concatenate([back_part.reshape(blocks * rows, width), placed], axis=1), PLANE
    )
    out_part = einsum("bect,ebcd->btd", pick, out_rows).astype(BF16)
    mixture = scatter(out_part.reshape(blocks * rows, width), PLANE).astype(F32)
    output = (middle + mixture).astype(BF16)

    grad_pair_own = einsum("ebcd,ebcf->edf", h_rows, ggu_own)
    grad_pair_other = einsum("ebcd,ebcf->edf", h_rows, ggu_other)
    grad_down_own = einsum("ebcf,ebcd->efd", weighted_own, g_rows)
    grad_down_other = einsum("ebcf,ebcd->efd", weighted_other, g_rows)
    grad_pair = grad_pair_own + swap_cores(grad_pair_other.astype(BF16)).astype(F32)
    grad_down = grad_down_own + swap_cores(grad_down_other.astype(BF16)).astype(F32)
    grad_gate_up = grad_pair.reshape(local, width, 2, hidden_local)

    grad_probs = jnp.sum(
        back_sum[:, width:].astype(F32).reshape(rows, x_count * 2, experts_all), axis=1
    )
    mask_own = route_mask(routes, experts_all)
    probs_own = masked_softmax(jnp.dot(h_two, w_router, preferred_element_type=F32), mask_own)
    inner = jnp.sum(probs_own * grad_probs, axis=-1, keepdims=True)
    grad_logits = probs_own * (grad_probs - inner)
    grad_router = jnp.dot(h_two.astype(F32).T, grad_logits, precision=HIGH)
    grad_h_two = back_sum[:, :width].astype(F32) + jnp.dot(
        grad_logits, w_router.astype(F32).T, precision=HIGH
    )
    grad_mid_norm, grad_gain_two = norm_back(middle, gain_two, grad_h_two)
    grad_mid = grad_out + grad_mid_norm

    ga_seq = gather(grad_mid.astype(BF16), GROUP)
    grad_wout = lax.dot_general(
        attn_vals, ga_seq, (((0,), (0,)), ((), ())), preferred_element_type=F32
    )
    grad_vals = lax.dot_general(
        ga_seq, w_out, (((1,), (1,)), ((), ())), preferred_element_type=F32
    )
    grad_mixed = grad_vals.astype(BF16).reshape(q_count, q_rows, heads, head_dim)

    def attend_back(carry, item):
        grad_keys, grad_values = carry
        q_block, doc_block, peak, total, grad_block = item
        scores = scores_of(q_block, doc_block)
        probs_full = jnp.exp(scores - peak) / total
        weights = probs_full.astype(BF16)
        grad_weights = einsum("qhd,khd->hqk", grad_block, values)
        delta = jnp.sum(grad_weights * probs_full, axis=-1, keepdims=True)
        grad_scores = (probs_full * (grad_weights - delta)).astype(BF16)
        grad_q = einsum("hqk,khd->qhd", grad_scores, keys) * scale
        grad_keys = grad_keys + einsum("hqk,qhd->khd", grad_scores, q_block) * scale
        grad_values = grad_values + einsum("hqk,qhd->khd", weights, grad_block)
        return ((grad_keys, grad_values), grad_q)

    head_zeros = jnp.zeros((seq_len, heads, head_dim), F32)
    (grad_keys, grad_values), grad_queries = lax.scan(
        attend_back, (head_zeros, head_zeros), (q_blocks, doc_blocks, peaks, totals, grad_mixed)
    )
    grad_queries = grad_queries.reshape(seq_len, heads, head_dim)
    grad_q_raw, grad_q_gain = q_back(grad_queries)
    grad_k_raw, grad_k_gain = k_back(grad_keys)
    grad_proj = (
        jnp.stack([grad_q_raw, grad_k_raw, grad_values], axis=1)
        .reshape(seq_len, 3 * qkv_local)
        .astype(BF16)
    )
    grad_wqkv = lax.dot_general(
        h_seq, grad_proj, (((0,), (0,)), ((), ())), preferred_element_type=F32
    )
    grad_h_one = scatter(
        lax.dot_general(
            grad_proj, w_flat, (((1,), (1,)), ((), ())), preferred_element_type=F32
        ).astype(BF16),
        GROUP,
    ).astype(F32)
    grad_in_norm, grad_gain_one = norm_back(inputs, gain_one, grad_h_one)
    grad_input = grad_mid + grad_in_norm
    dense_qkv = scatter(grad_wqkv.astype(BF16), "ep").astype(F32)
    dense_out = scatter(grad_wout.astype(BF16), "ep", 1).astype(F32)
    summed = lax.psum((grad_gain_one, grad_gain_two, grad_q_gain, grad_k_gain, grad_router), ALL)
    return (
        output,
        grad_input,
        summed[0],
        dense_qkv.reshape(dense_qkv.shape[0], 3, qkv_local),
        summed[2],
        summed[3],
        dense_out,
        summed[1],
        summed[4],
        grad_gate_up,
        grad_down,
    )


def solution(mesh):
    ep_count, tp_count = mesh.shape["ep"], mesh.shape["tp"]
    fine = Mesh(mesh.devices.reshape(ep_count, tp_count // 2, 2), ALL)
    in_specs = (
        P(ALL, None),
        P(ALL, None),
        P("ep", None),
        P(),
        P(None, None, GROUP),
        P(),
        P(),
        P(GROUP, None),
        P(),
        P(),
        P("ep", None, None, GROUP),
        P("ep", GROUP, None),
        P(ALL, None),
    )
    out_specs = (
        P(ALL, None),
        P(ALL, None),
        P(),
        P("ep", None, GROUP),
        P(),
        P(),
        P(GROUP, "ep"),
        P(),
        P(),
        P("ep", None, None, GROUP),
        P("ep", GROUP, None),
    )
    return jax.shard_map(
        per_device, mesh=fine, in_specs=in_specs, out_specs=out_specs, check_vma=False
    )
```

time: 2760 us -> 1960 us (0.71)
  blocking collectives: 597 us -> 90.8 us
  local copies, waits for them, and re-layouts: 424 us -> 155 us
  matrix products: 319 us -> 437 us
  waiting for transfers between devices: 1260 us -> 1150 us
    all_to_all x2 -> x0, blocking collectives: 555 us -> none  [the longest x1 278 us: send_wide(): return lax.all_to_all(parcel, 'ep', split_axis=1, concat_axis=1, tiled=True)]
    all_to_all x2 -> x0, waiting for transfers between devices: 207 us -> none  [the longest x1 207 us: per_device(): lax.all_to_all(back_out.reshape(ep_count, capacity, local_experts, model_...]
    dot_general x29 -> x41, matrix products: 319 us -> 437 us  [the longest x31 373 us: einsum(): return jnp.einsum(spec, left, right, preferred_element_type=F32)]
    reshape x12 -> x8, local copies, waits for them, and re-layouts: 120 us -> 40.1 us  [the longest x2 28.1 us: per_device(): pair_own = expert_gate_up.reshape(local, width, 2 * hidden_local)]
    all_to_all x4 -> x0, local copies, waits for them, and re-layouts: 56.5 us -> none  [the longest x1 16.3 us: per_device(): lax.all_to_all(back_send, 'ep', split_axis=0, concat_axis=0, tiled=True)]
    all_gather x4, waiting for transfers between devices: 263 us -> 312 us  [gather(): return lax.all_gather(value, axes, axis=0, tiled=True)]
    scatter x1 -> x0, local copies, waits for them, and re-layouts: 46.8 us -> none  [per_device(): jnp.zeros((buffer_rows, model_width), jnp.bfloat16).at[slot]]
    gather x2 -> x0, local copies, waits for them, and re-layouts: 45.4 us -> none  [the longest x1 22.9 us: per_device(): grad_sent.reshape(buffer_rows, model_width)[slot]]
  transfers between devices with their start and end apart: 13 -> 15, of which waited for: 9 -> 10; matrix products, arithmetic and copies ran while one was open for 20% -> 23% of each run, Pallas kernels for 0% -> 0%
where the time goes in v1:
time: 1960 us; the launch traced here: 1940 us
  waiting for transfers between devices  1150 us (59%)
  matrix products  437 us (22%)
  local copies, waits for them, and re-layouts  155 us (8%)
  other arithmetic  92.2 us (5%)
  blocking collectives  90.8 us (5%)
    reduce_scatter x6, waiting for transfers between devices, scatter(): return lax.psum_scatter(value, axes, scatter_dimension=dim, tiled=True)  704 us
    dot_general x31, matrix products, einsum(): return jnp.einsum(spec, left, right, preferred_element_type=F32)  373 us
    all_gather x4, waiting for transfers between devices, gather(): return lax.all_gather(value, axes, axis=0, tiled=True)  312 us
    psum x1, waiting for transfers between devices, per_device(): lax.psum((grad_gain_one, grad_gain_two, grad_q_gain, grad_k_gain, grad_ro...  126 us
    psum x1, blocking collectives, per_device(): lax.psum((grad_gain_one, grad_gain_two, grad_q_gain, grad_k_gain, grad_ro...  48.2 us
    unnamed x173, local copies, waits for them, and re-layouts  47.2 us
    dynamic_update_slice x6, local copies, waits for them, and re-layouts, per_device(): mixed, peaks, totals = lax.map(attend, (q_blocks, doc_blocks))  46.5 us
    all_gather x1, blocking collectives, gather(): return lax.all_gather(value, axes, axis=0, tiled=True)  42.6 us
  transfers between devices with their start and end apart: 15, of which 10 were waited for; matrix products, arithmetic and copies ran while one was open for 23% of the time, Pallas kernels for 0%

profile of v1, /device:TPU:0, one launch (start us, length us, event | category | flops | bytes accessed | tf_op | source)
XLA Modules:
  0.0 1944.2 jit_solution(14462203943366268276)
XLA Ops:
  9.5 8.9 copy.123
  19.9 27.7 %all-gather.5.cloned.1.call-done = bf16[1024,2048]{1,0:T(8,128)(2,1)} async-done(((bf16[256,2048]{1,0:T(8,128)(2,1)}), bf16[1024,2048]{1,0:T(8,128)(2,1)}) %all-gather.5.cloned.1.call-update) | async-done | bytes 4194320 | tf_op jit(solution)/shard_map/all_gather | solution.py:71
  47.6 3.2 fusion.41
  51.1 9.0 fusion.70
  73.4 3.1 pad_maximum_fusion.3
  76.5 19.6 %while.29 = (s32[]{:T(128)}, bf16[2,512,4,128]{3,1,2,0:T(8,128)(2,1)}, f32[2,4,512,1]{2,1,3,0:T(4,128)S(1)}, f32[2,4,512,1]{2,1,3,0:T(4,128)S(1)}, s32[2,512]{1,...) while((s32[]{:T(128)}, ...), condition=%wide.region_9.10_spmd, body=%wide.region_6.9_spmd.sunk | while | flops 1099427840 | bytes 31018092 | solution.py:164
  82.9 3.6 fusion.189
  86.9 3.1 fusion.187
  92.5 3.6 fusion.189
  99.6 4.4 convolution_convert_fusion.2
  104.7 45.7 %reduce-scatter.7.cloned.1.call-done = bf16[256,2048]{1,0:T(8,128)(2,1)} async-done(((bf16[1024,2048]{1,0:T(8,128)(2,1)}), bf16[256,2048]{1,0:T(8,128)(2,1)}) %reduce-scatter.7.cloned.1.call-update) | async-done | bytes 1048592 | tf_op jit(solution)/shard_map/reduce_scatter | solution.py:75
  155.3 14.0 reshape.356
  169.8 14.1 reshape.385
  183.9 42.6 %all_gather.16 = s32[4096,8]{0,1:T(8,128)S(1)} all-gather(s32[256,8]{0,1:T(8,128)S(1)} %copy-done.59), channel_id=1, replica_groups=mesh['ep'=8,'x'=2,'core'=2] {'ep','x'}, dimensions={0}, use_global_device_ids=true | all-gather | bytes 139264 | tf_op jit(solution)/shard_map/all_gather | solution.py:71
  230.3 68.9 %all-gather.9.cloned.1.call-done = bf16[4096,2048]{1,0:T(8,128)(2,1)} async-done(((bf16[256,2048]{1,0:T(8,128)(2,1)}), bf16[4096,2048]{1,0:T(8,128)(2,1)}) %all-gather.9.cloned.1.call-update) | async-done | bytes 16777232 | tf_op jit(solution)/shard_map/all_gather | solution.py:71
  299.2 17.8 convert_bitcast_fusion
  317.0 174.9 %all-gather.7.cloned.1.call-done = bf16[4096,2048]{1,0:T(8,128)(2,1)} async-done(((bf16[256,2048]{1,0:T(8,128)(2,1)}), bf16[4096,2048]{1,0:T(8,128)(2,1)}) %all-gather.7.cloned.1.call-update) | async-done | bytes 16777232 | tf_op jit(solution)/shard_map/all_gather | solution.py:71
  491.8 19.3 convert_bitcast_fusion.1
  511.1 14.4 fusion.37
  525.5 14.5 fusion.39
  540.0 14.7 fusion.33
  554.7 14.5 fusion.35
  569.2 19.2 fusion.49
  588.5 18.0 fusion.51
  606.5 10.9 fusion.130
  617.6 4.1 select_reduce_fusion
  624.5 23.1 %multiply_convert_fusion.4 = (bf16[4,16,96,256]{3,2,1,0:T(8,128)(2,1)}, bf16[4,16,96,256]{3,2,1,0:T(8,128)(2,1)}, bf16[4,16,96,256]{3,2,1,0:T(8,128)(2,1)}, bf16...) fusion(f32[4,16,96,256]{3,2,1,0:T(8,128)} %fusion.37, ...), kind=kLoop, calls=%fused_computation.93 | loop fusion | flops 50331648 | bytes 62939136 | tf_op jit(solution)/shard_map/convert_element_type | solution.py:209
  647.6 24.8 %fusion.44 = f32[4,16,96,2048]{3,2,0,1:T(8,128)} fusion(bf16[4,2048,512]{2,1,0:T(8,128)(2,1)} %collective-permute-done, bf16[4,16,96,256]{3,2,1,0:T(8,128)(2,1)} %get-tuple-element.397, bf16[4,16,96,256]{3,2,1,0:T(8,128)(2,1)} %get-tuple-element.398), kind=kOutput, calls=%fused_computation.74 | convolution fusion | flops 12897484800 | bytes 65011712 | tf_op jit(solution)/shard_map/ebcf,edf->ebcd/dot_general | solution.py:63
  672.4 36.1 %bitcast_convert_fusion = bf16[16,256,2048]{2,1,0:T(8,128)(2,1)} fusion(f32[4,16,96,2048]{3,2,0,1:T(8,128)} %fusion.44, bf16[4,2048,512,1]{2,1,0,3:T(8,128)(2,1)} %reshape.385, bf16[4,16,96,256]{3,2,1,0:T(8,128)(2,1)} %get-tuple-element.375, bf16[4,16,96,256]{3,2,1,0:T(8,128)(2,1)} %get-tuple-element.374, pred[16,4,96,256]{3,2,1,0:T(32,128)(4,1)} %fusion.169), kind=kOutput, calls=%fused_computation.42 | convolution fusion | flops 19373490176 | bytes 83361792 | tf_op jit(solution)/shard_map/bect,ebcd->btd/dot_general | solution.py:63
  708.5 15.6 pad_maximum_fusion
  726.7 363.3 %reduce-scatter.11.cloned.1.call-done = bf16[256,2176]{1,0:T(8,128)(2,1)} async-done(((bf16[4096,2176]{1,0:T(8,128)(2,1)}), bf16[256,2176]{1,0:T(8,128)(2,1)}) %reduce-scatter.11.cloned.1.call-update) | async-done | bytes 1114128 | tf_op jit(solution)/shard_map/reduce_scatter | solution.py:75
  1092.6 4.2 multiply_reduce_fusion.1
  1100.2 40.4 %all-gather.11.cloned.1.call-done = bf16[1024,2048]{1,0:T(8,128)(2,1)} async-done(((bf16[256,2048]{1,0:T(8,128)(2,1)}), bf16[1024,2048]{1,0:T(8,128)(2,1)}) %all-gather.11.cloned.1.call-update) | async-done | bytes 4194320 | tf_op jit(solution)/shard_map/all_gather | solution.py:71
  1140.6 5.5 convolution_convert_fusion.4
  1148.5 6.1 convolution_convert_fusion.3
  1154.7 94.2 %while.30 = (s32[]{:T(128)}, f32[1024,4,128]{0,2,1:T(8,128)S(1)}, f32[1024,4,128]{0,2,1:T(8,128)}, f32[2,512,4,128]{1,0,3,2:T(2,128)}, bf16[2,512,4,128]{3,1,2,0...) while((s32[]{:T(128)}, f32[1024,4,128]{0,2,1:T(8,128)S(1)}, ...), condition=%wide.region_29.30_spmd.clone, body=%wide.region_27.29_spmd.clone.sunk | while | flops 2708731904 | bytes 142683392 | solution.py:289
  1155.1 4.2 exponential_divide_fusion.2
  1165.6 3.5 fusion.198
  1169.1 3.6 copy.269
  1172.7 19.7 %dynamic_update_slice.28 = f32[2,512,4,128]{1,0,3,2:T(2,128)} dynamic-update-slice(f32[2,512,4,128]{1,0,3,2:T(2,128)} %get-tuple-element.602, f32[1,512,4,128]{1,0,3,2:T(1,128)} %copy.269, s32[]{:T(128)} %get-tuple-element.599, s32[]{:T(128)} %constant.53.clone.1..sunk, s32[]{:T(128)} %constant.53.clone.1..sunk, s32[]{:T(128)} %constant.53.clone.1..sunk) | dynamic-update-slice | bytes 2097156 | tf_op jit(solution)/shard_map/while/body/jit(dynamic_update_index_in_dim)/dynamic_update_slice | solution.py:164
  1192.4 3.7 bitcast_add_fusion.6
  1196.0 5.5 bitcast_add_fusion.7
  1202.0 4.2 exponential_divide_fusion.2
  1212.5 3.5 fusion.198
  1215.9 3.6 copy.269
  1219.5 19.7 %dynamic_update_slice.28 = f32[2,512,4,128]{1,0,3,2:T(2,128)} dynamic-update-slice(f32[2,512,4,128]{1,0,3,2:T(2,128)} %get-tuple-element.602, f32[1,512,4,128]{1,0,3,2:T(1,128)} %copy.269, s32[]{:T(128)} %get-tuple-element.599, s32[]{:T(128)} %constant.53.clone.1..sunk, s32[]{:T(128)} %constant.53.clone.1..sunk, s32[]{:T(128)} %constant.53.clone.1..sunk) | dynamic-update-slice | bytes 2097156 | tf_op jit(solution)/shard_map/while/body/jit(dynamic_update_index_in_dim)/dynamic_update_slice | solution.py:164
  1239.2 3.6 bitcast_add_fusion.6
  1242.8 6.1 bitcast_add_fusion.7
  1248.9 4.4 reshape.366
  1264.7 8.7 convolution_convert_fusion.1
  1273.5 24.3 %fusion.74 = f32[4,16,96,2048]{3,2,0,1:T(8,128)} fusion(bf16[4,256,2048]{2,1,0:T(8,128)(2,1)} %param.28, bf16[4,16,96,256]{3,2,1,0:T(8,128)(2,1)} %get-tuple-element.399), kind=kOutput, calls=%fused_computation.118 | convolution fusion | flops 6442450944 | bytes 57671680 | tf_op jit(solution)/shard_map/ebcf,efd->ebcd/dot_general | solution.py:63
  1297.8 29.8 %bitcast_convert_fusion.1 = bf16[16,256,2048]{2,1,0:T(8,128)(2,1)} fusion(f32[4,16,96,2048]{3,2,0,1:T(8,128)} %fusion.74, bf16[4,256,2048]{2,1,0:T(8,128)(2,1)} %collective-permute-done.1, bf16[4,16,96,256]{3,2,1,0:T(8,128)(2,1)} %get-tuple-element.396, s32[16,4,256]{2,1,0:T(4,128)S(1)} %copy-done.22, pred[16,4,256]{2,1,0:T(4,128)(4,1)S(1)} %copy-done.32), kind=kOutput, calls=%fused_computation.43 | convolution fusion | flops 12921602048 | bytes 74530816 | tf_op jit(solution)/shard_map/bect,ebcd->btd/dot_general | solution.py:63
  1328.3 12.2 convolution_convert_fusion
  1340.5 20.3 %bitcast_convert_fusion.2 = bf16[4,2048,512]{1,2,0:T(8,128)(2,1)} fusion(bf16[4,16,96,2048]{3,2,0,1:T(8,128)(2,1)} %convert_bitcast_fusion.1, bf16[4,16,96,256]{3,2,1,0:T(8,128)(2,1)} %get-tuple-element.397, bf16[4,16,96,256]{3,2,1,0:T(8,128)(2,1)} %get-tuple-element.398), kind=kOutput, calls=%fused_computation.49 | convolution fusion | flops 12901679104 | bytes 39845888 | tf_op jit(solution)/shard_map/ebcd,ebcf->edf/dot_general | solution.py:63
  1360.9 13.9 bitcast_convert_fusion.3
  1375.2 7.1 collective-permute-done.3
  1382.4 15.8 bitcast_add_fusion.3
  1398.2 24.5 %bitcast_add_fusion.2 = f32[4,2048,512]{1,2,0:T(8,128)} fusion(bf16[4,2048,512]{1,2,0:T(8,128)(2,1)} %collective-permute-done.2, bf16[4,16,96,2048]{3,2,0,1:T(8,128)(2,1)} %convert_bitcast_fusion.1, bf16[4,16,96,256]{3,2,1,0:T(8,128)(2,1)} %get-tuple-element.375, bf16[4,16,96,256]{3,2,1,0:T(8,128)(2,1)} %get-tuple-element.374), kind=kOutput, calls=%fused_computation.50 | convolution fusion | flops 12905873408 | bytes 56623104 | tf_op jit(solution)/shard_map/ebcd,ebcf->edf/dot_general | solution.py:63
  1422.8 25.2 %copy.156 = f32[4,2048,2,256]{3,2,1,0:T(2,128)} copy(f32[4,2048,2,256]{1,3,2,0:T(8,128)} %bitcast.286) | data formatting | bytes 33554432
  1453.3 220.9 %reduce-scatter.9.cloned.1.call-done = bf16[256,2048]{1,0:T(8,128)(2,1)} async-done(((bf16[4096,2048]{1,0:T(8,128)(2,1)}), bf16[256,2048]{1,0:T(8,128)(2,1)}) %reduce-scatter.9.cloned.1.call-update) | async-done | bytes 1048592 | tf_op jit(solution)/shard_map/reduce_scatter | solution.py:75
  1674.3 6.2 fusion.93
  1680.5 48.2 %all-reduce.4 = (f32[2048]{0:T(1024)}, f32[128]{0:T(128)}, f32[128]{0:T(128)}, f32[2048]{0:T(1024)}) all-reduce(f32[2048]{0:T(1024)S(1)} %get-tuple-element.307, f32[128]{0:T(128)S(1)} %copy-done.81, f32[128]{0:T(128)S(1)} %copy-done.80, f32[2048]{0:T(1024)S(1)} %copy-done.70), channel_id=1, replica_groups=mesh['ep'=8,'x'=2,'core'=2] {'ep','x','core'}, use_global_device_ids=true, to_apply=%region_36.37 | all-reduce | flops 4352 | bytes 34816 | tf_op jit(solution)/shard_map/psum | solution.py:313
  1728.7 73.9 %reduce-scatter.15.cloned.1.call-done = bf16[256,1536]{1,0:T(8,128)(2,1)} async-done(((bf16[2048,1536]{1,0:T(8,128)(2,1)}), bf16[256,1536]{1,0:T(8,128)(2,1)}) %reduce-scatter.15.cloned.1.call-update) | async-done | bytes 786448 | tf_op jit(solution)/shard_map/reduce_scatter | solution.py:75
  1808.2 126.3 %all-reduce.7.cloned.1.call-done = f32[2048,32]{0,1:T(8,128)} async-done(((f32[2048,32]{0,1:T(8,128)}), f32[2048,32]{0,1:T(8,128)}) %all-reduce.7.cloned.1.call-update) | async-done | bytes 262160 | tf_op jit(solution)/shard_map/psum | solution.py:313
  (312 shorter events, 90.1 us)
Async XLA Ops:
  8.0 91.6 %copy-start = (bf16[512,2048]{1,0:T(8,128)(2,1)S(1)}, bf16[512,2048]{1,0:T(8,128)(2,1)}, u32[]{:S(2)}) copy-start(bf16[512,2048]{1,0:T(8,128)(2,1)} %param.24) | copy-start | bytes 6291460
  8.0 39.6 %all-gather.5.cloned.1.call-start = ((), (), s32[]{:S(2)}) async-start(), calls=%async_computation.6 | async-start | bytes 5242880 | tf_op jit(solution)/shard_map/all_gather | solution.py:71
  8.8 141.6 %reduce-scatter.7.cloned.1.call-start = ((), (), s32[]{:S(2)}) async-start(), calls=%async_computation.7 | async-start | bytes 5242880 | tf_op jit(solution)/shard_map/reduce_scatter | solution.py:75
  9.5 41.3 %copy-start.57 = (f32[2048]{0:T(1024)}, f32[2048]{0:T(1024)S(1)}, u32[]{:S(2)}) copy-start(f32[2048]{0:T(1024)S(1)} %convert_element_type.220) | copy-start | bytes 24580
  9.5 8.9 copy-start.83
  9.5 8.9 copy-start.84
  9.5 8.9 copy-start.85
  18.4 44.0 %copy-start.71 = (f32[128]{0:T(128)}, f32[128]{0:T(128)S(1)}, u32[]{:S(2)}) copy-start(f32[128]{0:T(128)S(1)} %convert_element_type.222) | copy-start | bytes 1540
  18.4 44.0 %copy-start.73 = (f32[128]{0:T(128)}, f32[128]{0:T(128)S(1)}, u32[]{:S(2)}) copy-start(f32[128]{0:T(128)S(1)} %convert_element_type.224) | copy-start | bytes 1540
  19.8 43.3 %copy-start.23 = (f32[1024,64]{0,1:T(8,128)}, f32[1024,64]{0,1:T(8,128)S(1)}, u32[]{:S(2)}) copy-start(f32[1024,64]{0,1:T(8,128)S(1)} %get-tuple-element.400) | copy-start | bytes 786436
  19.9 43.3 %copy-start.25 = (f32[1024,64]{0,1:T(8,128)}, f32[1024,64]{0,1:T(8,128)S(1)}, u32[]{:S(2)}) copy-start(f32[1024,64]{0,1:T(8,128)S(1)} %get-tuple-element.401) | copy-start | bytes 786436
  50.8 9.3 copy-start.78
  96.1 7.8 copy-start.7
  96.1 7.8 copy-start.29
  96.1 7.8 copy-start.48
  96.1 7.8 copy-start.53
  96.1 7.8 copy-start.55
  104.0 46.4 %copy-start.9 = (bf16[256,2048]{1,0:T(8,128)(2,1)S(1)}, bf16[256,2048]{1,0:T(8,128)(2,1)}, u32[]{:S(2)}) copy-start(bf16[256,2048]{1,0:T(8,128)(2,1)} %param.17) | copy-start | bytes 3145732
  104.0 195.2 %all-gather.9.cloned.1.call-start = ((), (), s32[]{:S(2)}) async-start(), calls=%async_computation.10 | async-start | bytes 17825792 | tf_op jit(solution)/shard_map/all_gather | solution.py:71
  104.6 387.3 %all-gather.7.cloned.1.call-start = ((), (), s32[]{:S(2)}) async-start(), calls=%async_computation.8 | async-start | bytes 17825792 | tf_op jit(solution)/shard_map/all_gather | solution.py:71
  104.7 64.6 %copy-start.50 = (f32[2048]{0:T(1024)}, f32[2048]{0:T(1024)S(1)}, u32[]{:S(2)}) copy-start(f32[2048]{0:T(1024)S(1)} %convert_element_type.231) | copy-start | bytes 24580
  155.2 934.8 %reduce-scatter.11.cloned.1.call-start = ((), (), s32[]{:S(2)}) async-start(), calls=%async_computation.11 | async-start | bytes 18939904 | tf_op jit(solution)/shard_map/reduce_scatter | solution.py:75
  169.3 370.7 %collective-permute-start = (bf16[4,2048,512]{2,1,0:T(8,128)(2,1)}, bf16[4,2048,512]{2,1,0:T(8,128)(2,1)}, u32[]{:S(2)}, u32[]{:S(2)}) collective-permute-start(bf16[4,2048,512]{2,1,0:T(8,128)(2,1)} %reshape.356), channel_id=1, source_target_pairs={{0,1},{1,0},{2,3},{3,2},{4,5},{5,4},{6,7},{7,6},{8,9},{9,8},{10,11... | collective-permute-start | bytes 25165832 | tf_op jit(solution)/shard_map/ppermute | solution.py:67
  169.3 419.2 %collective-permute-start.1 = (bf16[4,256,2048]{2,1,0:T(8,128)(2,1)}, bf16[4,256,2048]{2,1,0:T(8,128)(2,1)}, u32[]{:S(2)}, u32[]{:S(2)}) collective-permute-start(bf16[4,256,2048]{2,1,0:T(8,128)(2,1)} %param.28), channel_id=1, source_target_pairs={{0,1},{1,0},{2,3},{3,2},{4,5},{5,4},{6,7},{7,6},{8,9},{9,8},{10,11... | collective-permute-start | bytes 12582920 | tf_op jit(solution)/shard_map/ppermute | solution.py:67
  169.8 14.1 copy-start.59
  227.5 390.2 %copy-start.21 = (s32[16,4,256]{2,1,0:T(4,128)}, s32[16,4,256]{2,1,0:T(4,128)S(1)}, u32[]{:S(2)}) copy-start(s32[16,4,256]{2,1,0:T(4,128)S(1)} %copy.130) | copy-start | bytes 196612
  227.5 390.1 %copy-start.31 = (pred[16,4,256]{2,1,0:T(4,128)(4,1)}, pred[16,4,256]{2,1,0:T(4,128)(4,1)S(1)}, u32[]{:S(2)}) copy-start(pred[16,4,256]{2,1,0:T(4,128)(4,1)S(1)} %copy.129) | copy-start | bytes 49156
  569.2 19.2 copy-start.17
  588.5 18.1 copy-start.33
  724.2 368.4 %copy-start.10 = (bf16[256,2048]{1,0:T(8,128)(2,1)S(1)}, bf16[256,2048]{1,0:T(8,128)(2,1)}, u32[]{:S(2)}) copy-start(bf16[256,2048]{1,0:T(8,128)(2,1)} %param.17) | copy-start | bytes 3145732
  724.2 368.4 %copy-start.51 = (f32[2048]{0:T(1024)S(1)}, f32[2048]{0:T(1024)}, u32[]{:S(2)}) copy-start(f32[2048]{0:T(1024)} %copy-done.50) | copy-start | bytes 24580
  724.2 368.4 %copy-start.62 = (f32[256]{0:T(256)S(1)}, f32[256]{0:T(256)}, u32[]{:S(2)}) copy-start(f32[256]{0:T(256)} %copy-done.61) | copy-start | bytes 3076
  724.2 416.3 %all-gather.11.cloned.1.call-start = ((), (), s32[]{:S(2)}) async-start(), calls=%async_computation.12 | async-start | bytes 5242880 | tf_op jit(solution)/shard_map/all_gather | solution.py:71
  724.9 371.9 %copy-start.42 = (pred[256,32]{0,1:T(8,128)(4,1)}, pred[256,32]{0,1:T(8,128)(4,1)S(1)}, u32[]{:S(2)}) copy-start(pred[256,32]{0,1:T(8,128)(4,1)S(1)} %fusion.112) | copy-start | bytes 24580
  726.6 373.4 %copy-start.34 = (f32[256,32]{0,1:T(8,128)}, f32[256,32]{0,1:T(8,128)S(1)}, u32[]{:S(2)}) copy-start(f32[256,32]{0,1:T(8,128)S(1)} %get-tuple-element.407) | copy-start | bytes 98308
  726.6 373.4 %copy-start.64 = (f32[256]{0:T(256)}, f32[256]{0:T(256)S(1)}, u32[]{:S(2)}) copy-start(f32[256]{0:T(256)S(1)} %get-tuple-element.406) | copy-start | bytes 3076
  726.7 373.4 %copy-start.66 = (f32[256]{0:T(256)}, f32[256]{0:T(256)S(1)}, u32[]{:S(2)}) copy-start(f32[256]{0:T(256)S(1)} %fusion.119) | copy-start | bytes 3076
  1096.9 49.2 %copy-start.68 = (f32[256]{0:T(256)}, f32[256]{0:T(256)S(1)}, u32[]{:S(2)}) copy-start(f32[256]{0:T(256)S(1)} %broadcast_multiply_fusion.1) | copy-start | bytes 3076
  1100.1 349.3 %reduce-scatter.17.cloned.1.call-start = ((), (), s32[]{:S(2)}) async-start(), calls=%async_computation.15 | async-start | bytes 2359296 | tf_op jit(solution)/shard_map/reduce_scatter | solution.py:75
  1100.2 48.3 %copy-start.28 = (bf16[2,512,4,128]{3,2,1,0:T(4,128)(2,1)S(1)}, bf16[2,512,4,128]{3,2,1,0:T(4,128)(2,1)}, u32[]{:S(2)}) copy-start(bf16[2,512,4,128]{3,2,1,0:T(4,128)(2,1)} %copy-done.27) | copy-start | bytes 3145732
  1154.6 296.6 %reduce-scatter.13.cloned.1.call-start = ((), (), s32[]{:S(2)}) async-start(), calls=%async_computation.13 | async-start | bytes 5242880 | tf_op jit(solution)/shard_map/reduce_scatter | solution.py:75
  1273.4 400.8 %reduce-scatter.9.cloned.1.call-start = ((), (), s32[]{:S(2)}) async-start(), calls=%async_computation.9 | async-start | bytes 17825792 | tf_op jit(solution)/shard_map/reduce_scatter | solution.py:75
  1273.5 24.3 %copy-start.22 = (s32[16,4,256]{2,1,0:T(4,128)S(1)}, s32[16,4,256]{2,1,0:T(4,128)}, u32[]{:S(2)}) copy-start(s32[16,4,256]{2,1,0:T(4,128)} %copy-done.21) | copy-start | bytes 196612
  1273.5 24.3 %copy-start.32 = (pred[16,4,256]{2,1,0:T(4,128)(4,1)S(1)}, pred[16,4,256]{2,1,0:T(4,128)(4,1)}, u32[]{:S(2)}) copy-start(pred[16,4,256]{2,1,0:T(4,128)(4,1)} %copy-done.31) | copy-start | bytes 49156
  1327.6 475.0 %reduce-scatter.15.cloned.1.call-start = ((), (), s32[]{:S(2)}) async-start(), calls=%async_computation.14 | async-start | bytes 7077888 | tf_op jit(solution)/shard_map/reduce_scatter | solution.py:75
  1340.5 594.0 %all-reduce.7.cloned.1.call-start = ((), (), s32[]{:S(2)}) async-start(), calls=%async_computation.16 | async-start | bytes 524288 | tf_op jit(solution)/shard_map/psum | solution.py:313
  1360.8 37.4 %collective-permute-start.2 = (bf16[4,2048,512]{1,2,0:T(8,128)(2,1)}, bf16[4,2048,512]{1,2,0:T(8,128)(2,1)}, u32[]{:S(2)}, u32[]{:S(2)}) collective-permute-start(bf16[4,2048,512]{1,2,0:T(8,128)(2,1)} %bitcast_convert_fusion.2), channel_id=1, source_target_pairs={{0,1},{1,0},{2,3},{3,2},{4,5},{5,4},{6,7},{7,6},{8,9},{9,8},{10,11... | collective-permute-start | bytes 25165832 | tf_op jit(solution)/shard_map/ppermute | solution.py:67
  1374.8 7.6 collective-permute-start.3
  1422.7 25.3 %copy-start.82 = (f32[256]{0:T(256)S(1)}, f32[256]{0:T(256)}, u32[]{:S(2)}) copy-start(f32[256]{0:T(256)} %get-tuple-element.309) | copy-start | bytes 3076
  1422.7 25.3 %copy-start.13 = (bf16[256,2048]{1,0:T(8,128)(2,1)S(1)}, bf16[256,2048]{1,0:T(8,128)(2,1)}, u32[]{:S(2)}) copy-start(bf16[256,2048]{1,0:T(8,128)(2,1)} %multiply_convert_fusion.7) | copy-start | bytes 3145732
  1422.7 25.3 %copy-start.35 = (f32[256,32]{0,1:T(8,128)S(1)}, f32[256,32]{0,1:T(8,128)}, u32[]{:S(2)}) copy-start(f32[256,32]{0,1:T(8,128)} %copy-done.34) | copy-start | bytes 98308
  1422.7 25.3 %copy-start.37 = (f32[256,32]{0,1:T(8,128)S(1)}, f32[256,32]{0,1:T(8,128)}, u32[]{:S(2)}) copy-start(f32[256,32]{0,1:T(8,128)} %copy-done.36) | copy-start | bytes 98308
  1422.7 25.3 %copy-start.43 = (pred[256,32]{0,1:T(8,128)(4,1)S(1)}, pred[256,32]{0,1:T(8,128)(4,1)}, u32[]{:S(2)}) copy-start(pred[256,32]{0,1:T(8,128)(4,1)} %copy-done.42) | copy-start | bytes 24580
  1422.7 25.3 %copy-start.65 = (f32[256]{0:T(256)S(1)}, f32[256]{0:T(256)}, u32[]{:S(2)}) copy-start(f32[256]{0:T(256)} %copy-done.64) | copy-start | bytes 3076
  1422.7 25.3 %copy-start.67 = (f32[256]{0:T(256)S(1)}, f32[256]{0:T(256)}, u32[]{:S(2)}) copy-start(f32[256]{0:T(256)} %copy-done.66) | copy-start | bytes 3076
  1422.7 25.3 %copy-start.76 = (f32[256]{0:T(256)S(1)}, f32[256]{0:T(256)}, u32[]{:S(2)}) copy-start(f32[256]{0:T(256)} %copy-done.75) | copy-start | bytes 3076
  1422.7 28.5 %copy-start.11 = (bf16[256,2048]{1,0:T(8,128)(2,1)S(1)}, bf16[256,2048]{1,0:T(8,128)(2,1)}, u32[]{:S(2)}) copy-start(bf16[256,2048]{1,0:T(8,128)(2,1)} %param.17) | copy-start | bytes 3145732
  1447.9 226.3 %copy-start.52 = (f32[2048]{0:T(1024)S(1)}, f32[2048]{0:T(1024)}, u32[]{:S(2)}) copy-start(f32[2048]{0:T(1024)} %copy-done.50) | copy-start | bytes 24580
  1447.9 226.3 %copy-start.63 = (f32[256]{0:T(256)S(1)}, f32[256]{0:T(256)}, u32[]{:S(2)}) copy-start(f32[256]{0:T(256)} %copy-done.61) | copy-start | bytes 3076
  1447.9 226.3 %copy-start.69 = (f32[256]{0:T(256)S(1)}, f32[256]{0:T(256)}, u32[]{:S(2)}) copy-start(f32[256]{0:T(256)} %copy-done.68) | copy-start | bytes 3076
  1453.3 227.2 %copy-start.70 = (f32[2048]{0:T(1024)S(1)}, f32[2048]{0:T(1024)}, u32[]{:S(2)}) copy-start(f32[2048]{0:T(1024)} %get-tuple-element.305) | copy-start | bytes 24580
  1453.3 227.2 %copy-start.80 = (f32[128]{0:T(128)S(1)}, f32[128]{0:T(128)}, u32[]{:S(2)}) copy-start(f32[128]{0:T(128)} %get-tuple-element.297) | copy-start | bytes 1540
  1453.3 227.2 %copy-start.81 = (f32[128]{0:T(128)S(1)}, f32[128]{0:T(128)}, u32[]{:S(2)}) copy-start(f32[128]{0:T(128)} %get-tuple-element.302) | copy-start | bytes 1540
  1674.3 261.9 %copy-start.1 = (bf16[512,2048]{1,0:T(8,128)(2,1)S(1)}, bf16[512,2048]{1,0:T(8,128)(2,1)}, u32[]{:S(2)}) copy-start(bf16[512,2048]{1,0:T(8,128)(2,1)} %param.24) | copy-start | bytes 6291460
  (43 other events, 147.6 us)
Sparse Core Ops, SparseCore 0:
  10.4 37.1 all-gather.4
  104.1 46.1 reduce-scatter.6
  1100.2 40.2 all-gather.10
  1154.7 68.8 reduce-scatter.16
  1273.5 44.5 reduce-scatter.12
  1327.7 346.4 reduce-scatter.8
  1677.8 124.7 reduce-scatter.14
  1808.7 125.7 all-reduce.6
Sparse Core Ops, SparseCore 1:
  107.3 191.9 all-gather.8
  302.4 189.4 all-gather.6
  724.3 365.6 reduce-scatter.10

commit v2 on v1

--- a/solution.py
+++ b/solution.py
@@ -1,6 +1,11 @@
+import functools
+import math
+
 import jax
 import jax.numpy as jnp
 from jax import lax
+from jax.experimental import pallas as pl
+from jax.experimental.pallas import tpu as pltpu
 from jax.sharding import Mesh
 from jax.sharding import PartitionSpec as P
 
@@ -14,6 +19,292 @@
 PLANE = ("ep", "x")
 GROUP = ("x", "core")
 ALL = ("ep", "x", "core")
+
+MESH = pl.DeviceIdType.MESH
+VMEM_BYTES = 60 * 1024 * 1024
+
+
+def remote(source, target, send, recv, where):
+    return pltpu.make_async_remote_copy(
+        src_ref=source,
+        dst_ref=target,
+        send_sem=send,
+        recv_sem=recv,
+        device_id=where,
+        device_id_type=MESH,
+    )
+
+
+def greet(where):
+    pl.semaphore_signal(
+        pltpu.get_barrier_semaphore(), inc=1, device_id=where, device_id_type=MESH
+    )
+
+
+def add_into(target, terms, step=32):
+    def body(index, carry):
+        at = pl.ds(pl.multiple_of(index * step, step), step)
+        total = terms[0][at, :].astype(F32)
+        for term in terms[1:]:
+            total = total + term[at, :].astype(F32)
+        target[at, :] = total.astype(target.dtype)
+        return carry
+
+    lax.fori_loop(0, target.shape[0] // step, body, 0)
+
+
+def peer_of(axes, counts, index):
+    where = {}
+    for axis, count in reversed(list(zip(axes, counts))):
+        where[axis] = lax.rem(index, count)
+        index = index // count
+    return where
+
+
+def spread_kernel(axes, counts, own_slices, v_ref, out_ref, local_sem, send, recv):
+    total = math.prod(counts)
+    me = 0
+    for axis, count in zip(axes, counts):
+        me = me * count + lax.axis_index(axis)
+
+    def hello(step, carry):
+        greet(peer_of(axes, counts, lax.rem(me + step, total)))
+        return carry
+
+    lax.fori_loop(1, total, hello, 0)
+    pl.semaphore_wait(pltpu.get_barrier_semaphore(), total - 1)
+
+    def copy(step):
+        peer = lax.rem(me + step, total)
+        source = v_ref.at[peer] if own_slices else v_ref
+        return remote(
+            source, out_ref.at[me], send.at[step], recv.at[step], peer_of(axes, counts, peer)
+        )
+
+    mine = pltpu.make_async_copy(
+        v_ref.at[me] if own_slices else v_ref, out_ref.at[me], local_sem
+    )
+    mine.start()
+
+    def begin(step, carry):
+        copy(step).start()
+        return carry
+
+    def finish(step, carry):
+        copy(step).wait()
+        return carry
+
+    lax.fori_loop(1, total, begin, 0)
+    mine.wait()
+    lax.fori_loop(1, total, finish, 0)
+
+
+def spread(value, axes, collective_id, own_slices=False):
+    counts = tuple(lax.axis_size(axis) for axis in axes)
+    total = math.prod(counts)
+    shape = value.shape[1:] if own_slices else value.shape
+    return pl.pallas_call(
+        functools.partial(spread_kernel, axes, counts, own_slices),
+        out_shape=jax.ShapeDtypeStruct((total,) + shape, value.dtype),
+        in_specs=[pl.BlockSpec(memory_space=pltpu.VMEM)],
+        out_specs=pl.BlockSpec(memory_space=pltpu.VMEM),
+        scratch_shapes=[
+            pltpu.SemaphoreType.DMA,
+            pltpu.SemaphoreType.DMA((total,)),
+            pltpu.SemaphoreType.DMA((total,)),
+        ],
+        compiler_params=pltpu.CompilerParams(
+            collective_id=collective_id, has_side_effects=True
+        ),
+        name="spread",
+    )(value)
+
+
+def visiting_order(count):
+    order, low, high = [], 0, count - 1
+    while low <= high:
+        order.append(high)
+        high -= 1
+        if low <= high:
+            order.append(low)
+            low += 1
+    return order
+
+
+def reduce_kernel(
+    depth, half, p_ref, out_ref, own, one, two, right, left,
+    own_sem, s1, r1, s2, r2, sr, rr, sl, rl,
+):
+    ep = lax.axis_index("ep")
+    x = lax.axis_index("x")
+    z = ep // 2
+    y = lax.rem(ep, 2)
+    first = ({"x": 1 - x}, {"ep": z * 2 + 1 - y})
+    second = (first[1], first[0])
+    up, down = {"ep": ep + 2}, {"ep": ep - 2}
+    barrier = pltpu.get_barrier_semaphore()
+    greet(first[0])
+    greet(first[1])
+    pl.when(z < depth - 1)(lambda: greet(up))
+    pl.when(z > 0)(lambda: greet(down))
+    peers = 2 + (z > 0).astype(jnp.int32) + (z < depth - 1).astype(jnp.int32)
+    pl.semaphore_wait(barrier, peers)
+
+    order = visiting_order(depth)
+    cols = (pl.ds(0, half), pl.ds(half, half))
+    mine = (y, x)
+
+    def block(part, level, step, theirs):
+        near = (x, y)[part]
+        near = 1 - near if theirs else near
+        far = 1 - mine[part] if step == 0 else mine[part]
+        at = (far, near) if part == 0 else (near, far)
+        return p_ref.at[level, at[0], at[1], :, cols[part]]
+
+    def send_one(part, level, step):
+        return remote(
+            block(part, level, step, True),
+            one.at[part, level, step],
+            s1.at[part, level, step],
+            r1.at[part, level, step],
+            first[part],
+        )
+
+    def send_two(part, level):
+        return remote(
+            one.at[part, level, 0],
+            two.at[part, level],
+            s2.at[part, level],
+            r2.at[part, level],
+            second[part],
+        )
+
+    def load(part, level, step):
+        return pltpu.make_async_copy(
+            block(part, level, step, False),
+            own.at[part, level, step],
+            own_sem.at[part, level, step],
+        )
+
+    def go_right(part, level):
+        ref = right.at[part, level]
+        return remote(ref, ref, sr.at[part, level], rr.at[part, level], up)
+
+    def go_left(part, level):
+        ref = left.at[part, level]
+        return remote(ref, ref, sl.at[part, level], rl.at[part, level], down)
+
+    for level in order:
+        for part in (0, 1):
+            send_one(part, level, 0).start()
+    for step in (0, 1):
+        for level in order:
+            for part in (0, 1):
+                load(part, level, step).start()
+    for level in order:
+        for part in (0, 1):
+            load(part, level, 0).wait()
+            send_one(part, level, 0).wait()
+            arrived = one.at[part, level, 0]
+            add_into(arrived, [arrived, own.at[part, level, 0]])
+            send_two(part, level).start()
+            send_one(part, level, 1).start()
+
+    def begin(level):
+        for part in (0, 1):
+            if level > 0:
+
+                @pl.when(z == 0)
+                def _():
+                    add_into(right.at[part, level], [two.at[part, level]])
+                    go_right(part, level).start()
+
+            if level < depth - 1:
+
+                @pl.when(z == depth - 1)
+                def _():
+                    add_into(left.at[part, level], [two.at[part, level]])
+                    go_left(part, level).start()
+
+    def forward(level):
+        for part in (0, 1):
+
+            @pl.when((z > 0) & (z < level))
+            def _():
+                go_right(part, level).wait_recv()
+                ref = right.at[part, level]
+                add_into(ref, [ref, two.at[part, level]])
+                go_right(part, level).start()
+
+            @pl.when((z < depth - 1) & (z > level))
+            def _():
+                go_left(part, level).wait_recv()
+                ref = left.at[part, level]
+                add_into(ref, [ref, two.at[part, level]])
+                go_left(part, level).start()
+
+    for turn, level in enumerate(order):
+        for part in (0, 1):
+            load(part, level, 1).wait()
+            send_one(part, level, 1).wait()
+            kept = own.at[part, level, 1]
+            add_into(kept, [one.at[part, level, 1], kept])
+            send_two(part, level).wait()
+            add_into(two.at[part, level], [two.at[part, level], kept])
+        begin(level)
+        if turn > 0:
+            forward(order[turn - 1])
+    forward(order[-1])
+    for level in range(depth):
+
+        @pl.when(z == level)
+        def _():
+            for part in (0, 1):
+                terms = [two.at[part, level]]
+                if level > 0:
+                    go_right(part, level).wait_recv()
+                    terms.append(right.at[part, level])
+                if level < depth - 1:
+                    go_left(part, level).wait_recv()
+                    terms.append(left.at[part, level])
+                add_into(out_ref.at[:, cols[part]], terms)
+
+        for part in (0, 1):
+            pl.when(z < level)(lambda: go_right(part, level).wait_send())
+            pl.when(z > level)(lambda: go_left(part, level).wait_send())
+
+
+def plane_reduce(parts, collective_id):
+    blocks, rows, columns = parts.shape
+    ep_count, x_count = lax.axis_size("ep"), lax.axis_size("x")
+    if x_count != 2 or ep_count % 2 or blocks * rows * columns > 2**24:
+        flat = parts.reshape(blocks * rows, columns)
+        return lax.psum_scatter(flat, PLANE, scatter_dimension=0, tiled=True).astype(F32)
+    depth, half = ep_count // 2, columns // 2
+
+    def buffer(*lead):
+        return pltpu.VMEM(lead + (rows, half), parts.dtype)
+
+    def sems(*lead):
+        return pltpu.SemaphoreType.DMA(lead)
+
+    return pl.pallas_call(
+        functools.partial(reduce_kernel, depth, half),
+        out_shape=jax.ShapeDtypeStruct((rows, columns), F32),
+        in_specs=[pl.BlockSpec(memory_space=pl.ANY)],
+        out_specs=pl.BlockSpec(memory_space=pltpu.VMEM),
+        scratch_shapes=[
+            buffer(2, depth, 2), buffer(2, depth, 2),
+            buffer(2, depth), buffer(2, depth), buffer(2, depth),
+            sems(2, depth, 2), sems(2, depth, 2), sems(2, depth, 2),
+            sems(2, depth), sems(2, depth), sems(2, depth),
+            sems(2, depth), sems(2, depth), sems(2, depth),
+        ],
+        compiler_params=pltpu.CompilerParams(
+            collective_id=collective_id, has_side_effects=True, vmem_limit_bytes=VMEM_BYTES
+        ),
+        name="plane_reduce",
+    )(parts.reshape(depth, 2, 2, rows, columns))
 
 
 def norm_rows(value, gain):
@@ -125,13 +416,13 @@
     grad_out = d_out.astype(F32)
     input_seq = gather(layer_input, GROUP)
     h_seq = norm_rows(input_seq.astype(F32), gain_one).astype(BF16)
-    w_flat = w_qkv.reshape(width, 3 * qkv_local)
-    projected = jnp.dot(h_seq, w_flat, preferred_element_type=F32).reshape(
-        seq_len, 3, heads, head_dim
-    )
-    q_raw = projected[:, 0]
-    k_raw = projected[:, 1]
-    v_raw = projected[:, 2]
+    w_parts = w_qkv.transpose(1, 0, 2)
+    q_raw, k_raw, v_raw = (
+        jnp.dot(h_seq, w_parts[part], preferred_element_type=F32).reshape(
+            seq_len, heads, head_dim
+        )
+        for part in range(3)
+    )
     doc_ids, position = positions(doc_lengths[0], seq_len)
     cosine, sine = rope_tables(position, head_dim)
     cosine = cosine[:, None, :]
@@ -168,7 +459,7 @@
     h_two = norm_rows(middle, gain_two).astype(BF16)
 
     g_plane = gather(d_out, PLANE).reshape(blocks, rows, width)
-    routes_plane = gather(routes, PLANE)
+    routes_plane = spread(routes.T, PLANE, 1).transpose(0, 2, 1).reshape(blocks * rows, topk)
     h_flat = gather(h_two, PLANE)
     h_plane = h_flat.reshape(blocks, rows, width)
     gate_own = expert_gate_up[:, :, 0]
@@ -222,23 +513,12 @@
     ).astype(BF16)
     dot_rows = (dots_own + dots_other).transpose(1, 0, 2)
     dots_token = jnp.sum(jnp.where(picks, dot_rows[..., None], 0.0), axis=2)
-    dots_token = dots_token.transpose(0, 2, 1).reshape(blocks * rows, local)
-    dots_high = dots_token.astype(BF16)
-    dots_low = (dots_token - dots_high.astype(F32)).astype(BF16)
-    my_x = lax.axis_index("x")
-    placed = jnp.zeros((blocks * rows, x_count, 2, experts_all), BF16)
-    placed = lax.dynamic_update_slice(
-        placed,
-        jnp.stack([dots_high, dots_low], axis=1)[:, None],
-        (0, my_x, 0, first),
-    ).reshape(blocks * rows, x_count * 2 * experts_all)
+    grad_probs = spread(dots_token, PLANE, 2, True)
+    grad_probs = jnp.sum(grad_probs.reshape(ep_count, x_count, local, rows), axis=1)
+    grad_probs = grad_probs.reshape(experts_all, rows).T
     back_part = einsum("bect,ebcd->btd", pick, back_rows).astype(BF16)
-    back_sum = scatter(
-        jnp.concatenate([back_part.reshape(blocks * rows, width), placed], axis=1), PLANE
-    )
+    back_sum = plane_reduce(back_part, 3)
     out_part = einsum("bect,ebcd->btd", pick, out_rows).astype(BF16)
-    mixture = scatter(out_part.reshape(blocks * rows, width), PLANE).astype(F32)
-    output = (middle + mixture).astype(BF16)
 
     grad_pair_own = einsum("ebcd,ebcf->edf", h_rows, ggu_own)
     grad_pair_other = einsum("ebcd,ebcf->edf", h_rows, ggu_other)
@@ -248,15 +528,12 @@
     grad_down = grad_down_own + swap_cores(grad_down_other.astype(BF16)).astype(F32)
     grad_gate_up = grad_pair.reshape(local, width, 2, hidden_local)
 
-    grad_probs = jnp.sum(
-        back_sum[:, width:].astype(F32).reshape(rows, x_count * 2, experts_all), axis=1
-    )
     mask_own = route_mask(routes, experts_all)
     probs_own = masked_softmax(jnp.dot(h_two, w_router, preferred_element_type=F32), mask_own)
     inner = jnp.sum(probs_own * grad_probs, axis=-1, keepdims=True)
     grad_logits = probs_own * (grad_probs - inner)
     grad_router = jnp.dot(h_two.astype(F32).T, grad_logits, precision=HIGH)
-    grad_h_two = back_sum[:, :width].astype(F32) + jnp.dot(
+    grad_h_two = back_sum + jnp.dot(
         grad_logits, w_router.astype(F32).T, precision=HIGH
     )
     grad_mid_norm, grad_gain_two = norm_back(middle, gain_two, grad_h_two)
@@ -292,35 +569,43 @@
     grad_queries = grad_queries.reshape(seq_len, heads, head_dim)
     grad_q_raw, grad_q_gain = q_back(grad_queries)
     grad_k_raw, grad_k_gain = k_back(grad_keys)
-    grad_proj = (
-        jnp.stack([grad_q_raw, grad_k_raw, grad_values], axis=1)
-        .reshape(seq_len, 3 * qkv_local)
-        .astype(BF16)
-    )
-    grad_wqkv = lax.dot_general(
-        h_seq, grad_proj, (((0,), (0,)), ((), ())), preferred_element_type=F32
-    )
-    grad_h_one = scatter(
-        lax.dot_general(
-            grad_proj, w_flat, (((1,), (1,)), ((), ())), preferred_element_type=F32
-        ).astype(BF16),
-        GROUP,
-    ).astype(F32)
+    grad_proj = [
+        grad.reshape(seq_len, qkv_local).astype(BF16)
+        for grad in (grad_q_raw, grad_k_raw, grad_values)
+    ]
+    grad_h_part = sum(
+        lax.dot_general(grad, w, (((1,), (1,)), ((), ())), preferred_element_type=F32)
+        for grad, w in zip(grad_proj, w_parts)
+    )
+    grad_h_one = scatter(grad_h_part.astype(BF16), GROUP).astype(F32)
+    grad_wqkv = jnp.stack(
+        [
+            lax.dot_general(
+                h_seq, grad, (((0,), (0,)), ((), ())), preferred_element_type=F32
+            ).astype(BF16)
+            for grad in grad_proj
+        ],
+    )
     grad_in_norm, grad_gain_one = norm_back(inputs, gain_one, grad_h_one)
     grad_input = grad_mid + grad_in_norm
-    dense_qkv = scatter(grad_wqkv.astype(BF16), "ep").astype(F32)
+    dense_qkv = scatter(grad_wqkv, "ep", 1).astype(F32)
     dense_out = scatter(grad_wout.astype(BF16), "ep", 1).astype(F32)
-    summed = lax.psum((grad_gain_one, grad_gain_two, grad_q_gain, grad_k_gain, grad_router), ALL)
+    out_part, grad_proj = lax.optimization_barrier((out_part, grad_proj))
+    output = (middle + plane_reduce(out_part, 4)).astype(BF16)
+    grad_router = lax.psum(grad_router, ALL)
+    small = jnp.concatenate([grad_gain_one, grad_gain_two, grad_q_gain, grad_k_gain])
+    small = jnp.sum(spread(small.reshape(-1, 128), ALL, 5), axis=0).reshape(-1)
+    gains = jnp.split(small, (width, 2 * width, 2 * width + head_dim))
     return (
         output,
         grad_input,
-        summed[0],
-        dense_qkv.reshape(dense_qkv.shape[0], 3, qkv_local),
-        summed[2],
-        summed[3],
+        gains[0],
+        dense_qkv.transpose(1, 0, 2),
+        gains[2],
+        gains[3],
         dense_out,
-        summed[1],
-        summed[4],
+        gains[1],
+        grad_router,
         grad_gate_up,
         grad_down,
     )

time: 1960 us -> 1490 us (0.76)
  waiting for transfers between devices: 1150 us -> 386 us
  Pallas kernels: 0 us -> 385 us
  blocking collectives: 90.8 us -> 0 us
    reduce_scatter x6 -> x4, waiting for transfers between devices: 704 us -> 45.7 us  [scatter(): return lax.psum_scatter(value, axes, scatter_dimension=dim, tiled=True)]
    pallas_call x0 -> x5, Pallas kernels: none -> 385 us  [the longest x2 334 us: plane_reduce(): pl.pallas_call(functools.partial(reduce_kernel, depth, half), out_shape=j...]
    psum x1, waiting for transfers between devices: 126 us -> 0.01 us  [per_device(): grad_router = lax.psum(grad_router, ALL)]
    psum x1 -> x0, blocking collectives: 48.2 us -> none  [per_device(): lax.psum((grad_gain_one, grad_gain_two, grad_q_gain, grad_k_gain, grad_ro...]
    all_gather x1 -> x0, blocking collectives: 42.6 us -> none  [gather(): return lax.all_gather(value, axes, axis=0, tiled=True)]
    all_gather x4, waiting for transfers between devices: 312 us -> 339 us  [gather(): return lax.all_gather(value, axes, axis=0, tiled=True)]
    unnamed x173 -> x189, local copies, waits for them, and re-layouts: 47.2 us -> 32.6 us
    dot_general x3 -> x9, matrix products: 29.9 us -> 39.4 us  [the longest x3 16.2 us: per_device(): lax.dot_general(grad, w, (((1,), (1,)), ((), ())), preferred_element_type...]
  transfers between devices with their start and end apart: 15 -> 13, of which waited for: 10 -> 5; matrix products, arithmetic and copies ran while one was open for 23% -> 32% of each run, Pallas kernels for 0% -> 15%
where the time goes in v2:
time: 1490 us; the launch traced here: 1470 us
  matrix products  444 us (30%)
  waiting for transfers between devices  386 us (26%)
  Pallas kernels  385 us (26%)
  local copies, waits for them, and re-layouts  153 us (10%)
  other arithmetic  84.3 us (6%)
  between operations  17.3 us (1%)
    dot_general x31, matrix products, einsum(): return jnp.einsum(spec, left, right, preferred_element_type=F32)  372 us
    all_gather x4, waiting for transfers between devices, gather(): return lax.all_gather(value, axes, axis=0, tiled=True)  339 us
    pallas_call x2, Pallas kernels, plane_reduce(): pl.pallas_call(functools.partial(reduce_kernel, depth, half), out_shape=j...  334 us
    pallas_call x3, Pallas kernels, spread(): pl.pallas_call(functools.partial(spread_kernel, axes, counts, own_slices)...  50.9 us
    dynamic_update_slice x6, local copies, waits for them, and re-layouts, per_device(): mixed, peaks, totals = lax.map(attend, (q_blocks, doc_blocks))  46.3 us
    reduce_scatter x4, waiting for transfers between devices, scatter(): return lax.psum_scatter(value, axes, scatter_dimension=dim, tiled=True)  45.7 us
    unnamed x189, local copies, waits for them, and re-layouts  32.6 us
  transfers between devices with their start and end apart: 13, of which 5 were waited for; matrix products, arithmetic and copies ran while one was open for 32% of the time, Pallas kernels for 15%

profile of v2, /device:TPU:0, one launch (start us, length us, event | category | flops | bytes accessed | tf_op | source)
XLA Modules:
  0.0 1472.2 jit_solution(17944228868553473835)
XLA Ops:
  9.5 5.7 slice_bitcast_fusion.8
  15.2 4.0 copy.117
  19.2 4.0 copy.114
  23.5 3.9 copy.118
  28.6 19.0 %all-gather.5.cloned.1.call-done = bf16[1024,2048]{1,0:T(8,128)(2,1)} async-done(((bf16[256,2048]{1,0:T(8,128)(2,1)}), bf16[1024,2048]{1,0:T(8,128)(2,1)}) %all-gather.5.cloned.1.call-update) | async-done | bytes 4194320 | tf_op jit(solution)/shard_map/all_gather | solution.py:362
  47.6 3.2 fusion.41
  51.1 4.2 multiply_reduce_fusion.8
  73.8 5.2 fusion.115
  79.1 19.1 %while.29 = (s32[]{:T(128)}, bf16[2,512,4,128]{3,1,2,0:T(8,128)(2,1)}, f32[2,4,512,1]{2,1,3,0:T(4,128)S(1)}, f32[2,4,512,1]{2,1,3,0:T(4,128)S(1)}, s32[2,512]{1,...) while((s32[]{:T(128)}, ...), condition=%wide.region_9.10_spmd, body=%wide.region_6.9_spmd.sunk | while | flops 1099427840 | bytes 31018092 | solution.py:455
  85.0 3.6 fusion.218
  94.6 3.6 fusion.218
  101.7 4.4 convolution_convert_fusion
  106.8 45.7 %reduce-scatter.5.cloned.1.call-done = bf16[256,2048]{1,0:T(8,128)(2,1)} async-done(((bf16[1024,2048]{1,0:T(8,128)(2,1)}), bf16[256,2048]{1,0:T(8,128)(2,1)}) %reduce-scatter.5.cloned.1.call-update) | async-done | bytes 1048592 | tf_op jit(solution)/shard_map/reduce_scatter | solution.py:366
  157.3 14.5 reshape.322
  172.3 14.2 reshape.344
  186.6 10.9 spread.3
  203.7 99.2 %all-gather.9.cloned.1.call-done = bf16[4096,2048]{1,0:T(8,128)(2,1)} async-done(((bf16[256,2048]{1,0:T(8,128)(2,1)}), bf16[4096,2048]{1,0:T(8,128)(2,1)}) %all-gather.9.cloned.1.call-update) | async-done | bytes 16777232 | tf_op jit(solution)/shard_map/all_gather | solution.py:362
  302.9 17.6 %convert_bitcast_fusion = bf16[4,16,96,2048]{3,2,0,1:T(8,128)(2,1)} fusion(bf16[16,256,2048,1]{2,1,3,0:T(8,128)(2,1)} %bitcast.311, s32[16,4,256]{2,1,0:T(4,128)S(1)} %copy.122, pred[16,4,256]{2,1,0:T(4,128)(4,1)S(1)} %copy.121), kind=kOutput, calls=%fused_computation.46 | convolution fusion | flops 6458179584 | bytes 42024960 | tf_op jit(solution)/shard_map/bect,btd->ebcd/dot_general | solution.py:354
  320.5 174.6 %all-gather.7.cloned.1.call-done = bf16[4096,2048]{1,0:T(8,128)(2,1)} async-done(((bf16[256,2048]{1,0:T(8,128)(2,1)}), bf16[4096,2048]{1,0:T(8,128)(2,1)}) %all-gather.7.cloned.1.call-update) | async-done | bytes 16777232 | tf_op jit(solution)/shard_map/all_gather | solution.py:362
  495.0 19.3 %convert_bitcast_fusion.1 = bf16[4,16,96,2048]{3,2,0,1:T(8,128)(2,1)} fusion(bf16[16,256,2048,1]{2,1,3,0:T(8,128)(2,1)} %bitcast.308, s32[16,4,256]{2,1,0:T(4,128)S(1)} %copy.122, pred[16,4,256]{2,1,0:T(4,128)(4,1)S(1)} %copy.121), kind=kOutput, calls=%fused_computation.47 | convolution fusion | flops 6458179584 | bytes 42024960 | tf_op jit(solution)/shard_map/bect,btd->ebcd/dot_general | solution.py:354
  514.3 14.4 fusion.39
  528.7 14.6 fusion.37
  543.3 14.4 fusion.33
  557.8 14.5 fusion.35
  572.2 19.2 %fusion.49 = (f32[4,16,96]{2,1,0:T(8,128)S(1)}, bf16[4,16,96,256]{3,2,1,0:T(8,128)(2,1)}, f32[4,16,96,256]{3,2,1,0:T(8,128)}) fusion(f32[4,16,96,256]{3,2,1,0:T(8,128)} %fusion.37, f32[4,16,96,256]{3,2,1,0:T(8,128)} %fusion.39, bf16[4,256,2048]{2,1,0:T(8,128)(2,1)} %param.28, bf16[4,16,96,2048]{3,2,0,1:T(8,128)(2,1)} %convert_bitcast_fusion), kind=kOutput, calls=%fused_computation.82 | convolution fusion | flops 6456600576 | bytes 51404800 | tf_op jit(solution)/shard_map/ebcd,efd->ebcf/dot_general | solution.py:354
  591.5 17.9 %fusion.51 = (f32[4,16,96]{2,1,0:T(8,128)S(1)}, bf16[4,16,96,256]{3,2,1,0:T(8,128)(2,1)}, f32[4,16,96,256]{3,2,1,0:T(8,128)}) fusion(f32[4,16,96,256]{3,2,1,0:T(8,128)S(1)} %copy-done.21, f32[4,16,96,256]{3,2,1,0:T(8,128)} %fusion.35, bf16[4,256,2048]{2,1,0:T(8,128)(2,1)} %collective-permute-done.1, bf16[4,16,96,2048]{3,2,0,1:T(8,128)(2,1)} %convert_bitcast_fusion), kind=kOutput, calls=%fused_computation.84 | convolution fusion | flops 6456600576 | bytes 51404800 | tf_op jit(solution)/shard_map/ebcd,efd->ebcf/dot_general | solution.py:354
  609.4 10.9 fusion.154
  620.5 4.7 select_reduce_fusion
  625.2 9.1 spread.4
  635.2 23.1 %multiply_convert_fusion.4 = (bf16[4,16,96,256]{3,2,1,0:T(8,128)(2,1)}, bf16[4,16,96,256]{3,2,1,0:T(8,128)(2,1)}, bf16[4,16,96,256]{3,2,1,0:T(8,128)(2,1)}, bf16...) fusion(f32[4,16,96,256]{3,2,1,0:T(8,128)} %fusion.37, ...), kind=kLoop, calls=%fused_computation.92 | loop fusion | flops 50331648 | bytes 62939136 | tf_op jit(solution)/shard_map/convert_element_type | solution.py:500
  658.3 24.9 %fusion.44 = f32[4,16,96,2048]{3,2,0,1:T(8,128)} fusion(bf16[4,2048,512]{2,1,0:T(8,128)(2,1)} %collective-permute-done, bf16[4,16,96,256]{3,2,1,0:T(8,128)(2,1)} %get-tuple-element.388, bf16[4,16,96,256]{3,2,1,0:T(8,128)(2,1)} %get-tuple-element.389), kind=kOutput, calls=%fused_computation.73 | convolution fusion | flops 12897484800 | bytes 65011712 | tf_op jit(solution)/shard_map/ebcf,edf->ebcd/dot_general | solution.py:354
  683.1 36.1 %bitcast_convert_fusion = bf16[16,256,2048]{2,1,0:T(8,128)(2,1)} fusion(f32[4,16,96,2048]{3,2,0,1:T(8,128)} %fusion.44, bf16[4,2048,512,1]{2,1,0,3:T(8,128)(2,1)} %reshape.344, bf16[4,16,96,256]{3,2,1,0:T(8,128)(2,1)} %get-tuple-element.367, bf16[4,16,96,256]{3,2,1,0:T(8,128)(2,1)} %get-tuple-element.366, pred[16,4,96,256]{3,2,1,0:T(32,128)(4,1)} %fusion.198), kind=kOutput, calls=%fused_computation.42 | convolution fusion | flops 19373490176 | bytes 83361792 | tf_op jit(solution)/shard_map/bect,ebcd->btd/dot_general | solution.py:354
  719.3 158.3 %plane_reduce.2 = f32[256,2048]{1,0:T(8,128)} custom-call(bf16[4,2,2,256,2048]{4,3,2,1,0:T(8,128)(2,1)} %bitcast.309), custom_call_target="tpu_custom_call" | custom-call | tf_op jit(solution)/shard_map/plane_reduce/pallas_call | solution.py:291
  877.8 4.5 multiply_reduce_fusion.3
  885.6 46.4 %all-gather.11.cloned.1.call-done = bf16[1024,2048]{1,0:T(8,128)(2,1)} async-done(((bf16[256,2048]{1,0:T(8,128)(2,1)}), bf16[1024,2048]{1,0:T(8,128)(2,1)}) %all-gather.11.cloned.1.call-update) | async-done | bytes 4194320 | tf_op jit(solution)/shard_map/all_gather | solution.py:362
  932.1 5.5 convolution_convert_fusion.5
  939.9 6.1 convolution_convert_fusion.1
  946.1 94.0 %while.30 = (s32[]{:T(128)}, f32[1024,4,128]{0,2,1:T(8,128)S(1)}, f32[1024,4,128]{0,2,1:T(8,128)}, f32[2,512,4,128]{1,0,3,2:T(2,128)}, bf16[2,512,4,128]{3,1,2,0...) while((s32[]{:T(128)}, f32[1024,4,128]{0,2,1:T(8,128)S(1)}, ...), condition=%wide.region_27.28_spmd.clone, body=%wide.region_25.27_spmd.clone.sunk | while | flops 2708731904 | bytes 142683392 | solution.py:566
  946.6 4.2 exponential_divide_fusion.2
  957.1 3.5 fusion.227
  960.5 3.6 copy.256
  964.1 19.6 %dynamic_update_slice.23 = f32[2,512,4,128]{1,0,3,2:T(2,128)} dynamic-update-slice(f32[2,512,4,128]{1,0,3,2:T(2,128)} %get-tuple-element.601, f32[1,512,4,128]{1,0,3,2:T(1,128)} %copy.256, s32[]{:T(128)} %get-tuple-element.598, s32[]{:T(128)} %constant.51.clone.1..sunk, s32[]{:T(128)} %constant.51.clone.1..sunk, s32[]{:T(128)} %constant.51.clone.1..sunk) | dynamic-update-slice | bytes 2097156 | tf_op jit(solution)/shard_map/while/body/jit(dynamic_update_index_in_dim)/dynamic_update_slice | solution.py:455
  983.7 3.7 bitcast_add_fusion.6
  987.4 5.6 bitcast_add_fusion.7
  993.3 4.2 exponential_divide_fusion.2
  1003.8 3.5 fusion.227
  1007.3 3.6 copy.256
  1010.9 19.6 %dynamic_update_slice.23 = f32[2,512,4,128]{1,0,3,2:T(2,128)} dynamic-update-slice(f32[2,512,4,128]{1,0,3,2:T(2,128)} %get-tuple-element.601, f32[1,512,4,128]{1,0,3,2:T(1,128)} %copy.256, s32[]{:T(128)} %get-tuple-element.598, s32[]{:T(128)} %constant.51.clone.1..sunk, s32[]{:T(128)} %constant.51.clone.1..sunk, s32[]{:T(128)} %constant.51.clone.1..sunk) | dynamic-update-slice | bytes 2097156 | tf_op jit(solution)/shard_map/while/body/jit(dynamic_update_index_in_dim)/dynamic_update_slice | solution.py:455
  1030.4 3.6 bitcast_add_fusion.6
  1034.0 6.1 bitcast_add_fusion.7
  1040.2 4.2 reshape.329
  1055.9 5.8 fusion.109
  1061.7 8.0 add_convert_fusion.8
  1070.5 5.5 fusion.96
  1085.2 20.7 %bitcast_convert_fusion.2 = bf16[4,2048,512]{1,2,0:T(8,128)(2,1)} fusion(bf16[4,16,96,2048]{3,2,0,1:T(8,128)(2,1)} %convert_bitcast_fusion.1, bf16[4,16,96,256]{3,2,1,0:T(8,128)(2,1)} %get-tuple-element.388, bf16[4,16,96,256]{3,2,1,0:T(8,128)(2,1)} %get-tuple-element.389), kind=kOutput, calls=%fused_computation.48 | convolution fusion | flops 12901679104 | bytes 39845888 | tf_op jit(solution)/shard_map/ebcd,ebcf->edf/dot_general | solution.py:354
  1106.2 14.2 bitcast_convert_fusion.3
  1122.0 22.4 %fusion.72 = f32[4,16,96,2048]{3,2,0,1:T(8,128)} fusion(bf16[4,256,2048]{2,1,0:T(8,128)(2,1)} %param.28, bf16[4,16,96,256]{3,2,1,0:T(8,128)(2,1)} %get-tuple-element.390), kind=kOutput, calls=%fused_computation.115 | convolution fusion | flops 6442450944 | bytes 57671680 | tf_op jit(solution)/shard_map/ebcf,efd->ebcd/dot_general | solution.py:354
  1144.5 30.4 %bitcast_convert_fusion.1 = bf16[16,256,2048]{2,1,0:T(8,128)(2,1)} fusion(f32[4,16,96,2048]{3,2,0,1:T(8,128)} %fusion.72, bf16[4,256,2048]{2,1,0:T(8,128)(2,1)} %collective-permute-done.1, bf16[4,16,96,256]{3,2,1,0:T(8,128)(2,1)} %get-tuple-element.387, s32[16,4,256]{2,1,0:T(4,128)S(1)} %copy-done.25, pred[16,4,256]{2,1,0:T(4,128)(4,1)S(1)} %copy-done.42), kind=kOutput, calls=%fused_computation.43 | convolution fusion | flops 12921602048 | bytes 74530816 | tf_op jit(solution)/shard_map/bect,ebcd->btd/dot_general | solution.py:354
  1174.9 16.1 %bitcast_add_fusion.3 = f32[4,256,2048]{2,1,0:T(8,128)} fusion(bf16[4,256,2048]{2,1,0:T(8,128)(2,1)} %collective-permute-done.3, bf16[4,16,96,256]{3,2,1,0:T(8,128)(2,1)} %get-tuple-element.390, bf16[4,16,96,2048]{3,2,0,1:T(8,128)(2,1)} %convert_bitcast_fusion), kind=kOutput, calls=%fused_computation.72 | convolution fusion | flops 6446645248 | bytes 40894464 | tf_op jit(solution)/shard_map/ebcf,ebcd->efd/dot_general | solution.py:354
  1190.9 175.6 %plane_reduce.3 = f32[256,2048]{1,0:T(8,128)} custom-call(bf16[4,2,2,256,2048]{4,3,2,1,0:T(8,128)(2,1)} %bitcast.310), custom_call_target="tpu_custom_call" | custom-call | tf_op jit(solution)/shard_map/plane_reduce/pallas_call | solution.py:291
  1366.5 24.3 %bitcast_add_fusion.2 = f32[4,2048,512]{1,2,0:T(8,128)} fusion(bf16[4,2048,512]{1,2,0:T(8,128)(2,1)} %collective-permute-done.2, bf16[4,16,96,2048]{3,2,0,1:T(8,128)(2,1)} %convert_bitcast_fusion.1, bf16[4,16,96,256]{3,2,1,0:T(8,128)(2,1)} %get-tuple-element.367, bf16[4,16,96,256]{3,2,1,0:T(8,128)(2,1)} %get-tuple-element.366), kind=kOutput, calls=%fused_computation.49 | convolution fusion | flops 12905873408 | bytes 56623104 | tf_op jit(solution)/shard_map/ebcd,ebcf->edf/dot_general | solution.py:354
  1390.9 25.0 %copy.143 = f32[4,2048,2,256]{3,2,1,0:T(2,128)} copy(f32[4,2048,2,256]{1,3,2,0:T(8,128)} %bitcast.312) | data formatting | bytes 33554432
  1420.4 31.0 %spread.5 = f32[32,34,128]{2,1,0:T(8,128)} custom-call(f32[34,128]{1,0:T(8,128)} %maximum_bitcast_fusion.v_ref), custom_call_target="tpu_custom_call" | custom-call | tf_op jit(solution)/shard_map/spread/pallas_call | solution.py:106
  1453.7 6.5 fusion.100
  (334 shorter events, 103.0 us)
Async XLA Ops:
  8.0 93.7 %copy-start = (bf16[512,2048]{1,0:T(8,128)(2,1)S(1)}, bf16[512,2048]{1,0:T(8,128)(2,1)}, u32[]{:S(2)}) copy-start(bf16[512,2048]{1,0:T(8,128)(2,1)} %param.24) | copy-start | bytes 6291460
  8.0 39.6 %all-gather.5.cloned.1.call-start = ((), (), s32[]{:S(2)}) async-start(), calls=%async_computation.4 | async-start | bytes 5242880 | tf_op jit(solution)/shard_map/all_gather | solution.py:362
  8.8 143.7 %reduce-scatter.5.cloned.1.call-start = ((), (), s32[]{:S(2)}) async-start(), calls=%async_computation.5 | async-start | bytes 5242880 | tf_op jit(solution)/shard_map/reduce_scatter | solution.py:366
  9.5 64.3 %copy-start.61 = (f32[2048]{0:T(1024)}, f32[2048]{0:T(1024)S(1)}, u32[]{:S(2)}) copy-start(f32[2048]{0:T(1024)S(1)} %convert_element_type.192) | copy-start | bytes 24580
  15.2 8.0 copy-start.92
  15.2 8.0 copy-start.93
  15.2 8.1 copy-start.94
  23.3 34.6 %copy-start.82 = (f32[128]{0:T(128)}, f32[128]{0:T(128)S(1)}, u32[]{:S(2)}) copy-start(f32[128]{0:T(128)S(1)} %convert_element_type.194) | copy-start | bytes 1540
  23.3 34.6 %copy-start.84 = (f32[128]{0:T(128)}, f32[128]{0:T(128)S(1)}, u32[]{:S(2)}) copy-start(f32[128]{0:T(128)S(1)} %convert_element_type.196) | copy-start | bytes 1540
  28.6 30.9 %copy-start.26 = (f32[1024,64]{0,1:T(8,128)}, f32[1024,64]{0,1:T(8,128)S(1)}, u32[]{:S(2)}) copy-start(f32[1024,64]{0,1:T(8,128)S(1)} %get-tuple-element.395) | copy-start | bytes 786436
  28.6 30.9 %copy-start.28 = (f32[1024,64]{0,1:T(8,128)}, f32[1024,64]{0,1:T(8,128)S(1)}, u32[]{:S(2)}) copy-start(f32[1024,64]{0,1:T(8,128)S(1)} %get-tuple-element.396) | copy-start | bytes 786436
  50.8 23.0 %copy-start.87 = (f32[1024]{0:T(1024)}, f32[1024]{0:T(1024)S(1)}, u32[]{:S(2)}) copy-start(f32[1024]{0:T(1024)S(1)} %add_rsqrt_fusion) | copy-start | bytes 12292
  98.2 7.8 copy-start.39
  98.2 7.8 copy-start.55
  98.2 7.8 copy-start.57
  98.2 7.8 copy-start.59
  106.1 46.4 %copy-start.5 = (bf16[256,2048]{1,0:T(8,128)(2,1)S(1)}, bf16[256,2048]{1,0:T(8,128)(2,1)}, u32[]{:S(2)}) copy-start(bf16[256,2048]{1,0:T(8,128)(2,1)} %param.17) | copy-start | bytes 3145732
  106.1 196.8 %all-gather.9.cloned.1.call-start = ((), (), s32[]{:S(2)}) async-start(), calls=%async_computation.7 | async-start | bytes 17825792 | tf_op jit(solution)/shard_map/all_gather | solution.py:362
  106.7 388.3 %all-gather.7.cloned.1.call-start = ((), (), s32[]{:S(2)}) async-start(), calls=%async_computation.6 | async-start | bytes 17825792 | tf_op jit(solution)/shard_map/all_gather | solution.py:362
  106.7 65.1 %copy-start.52 = (f32[2048]{0:T(1024)}, f32[2048]{0:T(1024)S(1)}, u32[]{:S(2)}) copy-start(f32[2048]{0:T(1024)S(1)} %convert_element_type.203) | copy-start | bytes 24580
  157.3 774.8 %all-gather.11.cloned.1.call-start = ((), (), s32[]{:S(2)}) async-start(), calls=%async_computation.8 | async-start | bytes 5242880 | tf_op jit(solution)/shard_map/all_gather | solution.py:362
  171.8 371.5 %collective-permute-start = (bf16[4,2048,512]{2,1,0:T(8,128)(2,1)}, bf16[4,2048,512]{2,1,0:T(8,128)(2,1)}, u32[]{:S(2)}, u32[]{:S(2)}) collective-permute-start(bf16[4,2048,512]{2,1,0:T(8,128)(2,1)} %reshape.322), channel_id=1, source_target_pairs={{0,1},{1,0},{2,3},{3,2},{4,5},{5,4},{6,7},{7,6},{8,9},{9,8},{10,11... | collective-permute-start | bytes 25165832 | tf_op jit(solution)/shard_map/ppermute | solution.py:358
  171.8 419.7 %collective-permute-start.1 = (bf16[4,256,2048]{2,1,0:T(8,128)(2,1)}, bf16[4,256,2048]{2,1,0:T(8,128)(2,1)}, u32[]{:S(2)}, u32[]{:S(2)}) collective-permute-start(bf16[4,256,2048]{2,1,0:T(8,128)(2,1)} %param.28), channel_id=1, source_target_pairs={{0,1},{1,0},{2,3},{3,2},{4,5},{5,4},{6,7},{7,6},{8,9},{9,8},{10,11... | collective-permute-start | bytes 12582920 | tf_op jit(solution)/shard_map/ppermute | solution.py:358
  172.3 26.9 %copy-start.69 = (s32[256,8]{0,1:T(8,128)S(1)}, s32[256,8]{0,1:T(8,128)}, u32[]{:S(2)}) copy-start(s32[256,8]{0,1:T(8,128)} %param.18) | copy-start | bytes 24580
  172.3 29.7 %copy-start.16 = (bf16[256,2048]{1,0:T(8,128)(2,1)S(1)}, bf16[256,2048]{1,0:T(8,128)(2,1)}, u32[]{:S(2)}) copy-start(bf16[256,2048]{1,0:T(8,128)(2,1)} %multiply_convert_fusion.7) | copy-start | bytes 3145732
  172.3 29.7 %copy-start.30 = (bf16[2048,32]{0,1:T(8,128)(2,1)S(1)}, bf16[2048,32]{0,1:T(8,128)(2,1)}, u32[]{:S(2)}) copy-start(bf16[2048,32]{0,1:T(8,128)(2,1)} %param.26) | copy-start | bytes 393220
  199.2 421.3 %copy-start.24 = (s32[16,4,256]{2,1,0:T(4,128)}, s32[16,4,256]{2,1,0:T(4,128)S(1)}, u32[]{:S(2)}) copy-start(s32[16,4,256]{2,1,0:T(4,128)S(1)} %copy.122) | copy-start | bytes 196612
  199.2 421.2 %copy-start.41 = (pred[16,4,256]{2,1,0:T(4,128)(4,1)}, pred[16,4,256]{2,1,0:T(4,128)(4,1)S(1)}, u32[]{:S(2)}) copy-start(pred[16,4,256]{2,1,0:T(4,128)(4,1)S(1)} %copy.121) | copy-start | bytes 49156
  572.2 19.2 %copy-start.21 = (f32[4,16,96,256]{3,2,1,0:T(8,128)S(1)}, f32[4,16,96,256]{3,2,1,0:T(8,128)}, u32[]{:S(2)}) copy-start(f32[4,16,96,256]{3,2,1,0:T(8,128)} %fusion.33) | copy-start | bytes 18874372
  635.2 242.5 %copy-start.43 = (f32[32,256]{1,0:T(8,128)}, f32[32,256]{1,0:T(8,128)S(1)}, u32[]{:S(2)}) copy-start(f32[32,256]{1,0:T(8,128)S(1)} %reshape.327) | copy-start | bytes 98308
  719.3 158.4 %copy-start.37 = (f32[256,32]{0,1:T(8,128)S(1)}, f32[256,32]{0,1:T(8,128)}, u32[]{:S(2)}) copy-start(f32[256,32]{0,1:T(8,128)} %copy-done.36) | copy-start | bytes 98308
  719.3 158.4 %copy-start.46 = (pred[256,32]{0,1:T(8,128)(4,1)S(1)}, pred[256,32]{0,1:T(8,128)(4,1)}, u32[]{:S(2)}) copy-start(pred[256,32]{0,1:T(8,128)(4,1)} %copy-done.45) | copy-start | bytes 24580
  719.3 158.4 %copy-start.71 = (f32[256]{0:T(256)S(1)}, f32[256]{0:T(256)}, u32[]{:S(2)}) copy-start(f32[256]{0:T(256)} %copy-done.70) | copy-start | bytes 3076
  719.3 158.4 %copy-start.76 = (f32[256]{0:T(256)S(1)}, f32[256]{0:T(256)}, u32[]{:S(2)}) copy-start(f32[256]{0:T(256)} %fusion.135) | copy-start | bytes 3076
  719.3 158.5 %copy-start.6 = (bf16[256,2048]{1,0:T(8,128)(2,1)S(1)}, bf16[256,2048]{1,0:T(8,128)(2,1)}, u32[]{:S(2)}) copy-start(bf16[256,2048]{1,0:T(8,128)(2,1)} %param.17) | copy-start | bytes 3145732
  719.3 158.5 %copy-start.53 = (f32[2048]{0:T(1024)S(1)}, f32[2048]{0:T(1024)}, u32[]{:S(2)}) copy-start(f32[2048]{0:T(1024)} %copy-done.52) | copy-start | bytes 24580
  719.3 158.5 %copy-start.74 = (f32[256]{0:T(256)S(1)}, f32[256]{0:T(256)}, u32[]{:S(2)}) copy-start(f32[256]{0:T(256)} %copy-done.73) | copy-start | bytes 3076
  877.8 7.7 copy-start.78
  885.5 530.4 %reduce-scatter.11.cloned.1.call-start = ((), (), s32[]{:S(2)}) async-start(), calls=%async_computation.11 | async-start | bytes 2359296 | tf_op jit(solution)/shard_map/reduce_scatter | solution.py:366
  885.6 54.3 %copy-start.32 = (bf16[2,512,4,128]{3,2,1,0:T(4,128)(2,1)S(1)}, bf16[2,512,4,128]{3,2,1,0:T(4,128)(2,1)}, u32[]{:S(2)}) copy-start(bf16[2,512,4,128]{3,2,1,0:T(4,128)(2,1)} %copy-done.31) | copy-start | bytes 3145732
  946.0 471.7 %reduce-scatter.7.cloned.1.call-start = ((), (), s32[]{:S(2)}) async-start(), calls=%async_computation.9 | async-start | bytes 5242880 | tf_op jit(solution)/shard_map/reduce_scatter | solution.py:366
  1069.8 390.4 %reduce-scatter.9.cloned.1.call-start = ((), (), s32[]{:S(2)}) async-start(), calls=%async_computation.10 | async-start | bytes 7077888 | tf_op jit(solution)/shard_map/reduce_scatter | solution.py:366
  1085.0 377.7 %all-reduce.6.cloned.1.call-start = ((), (), s32[]{:S(2)}) async-start(), calls=%async_computation.12 | async-start | bytes 524288 | tf_op jit(solution)/shard_map/psum | solution.py:595
  1105.9 260.6 %collective-permute-start.2 = (bf16[4,2048,512]{1,2,0:T(8,128)(2,1)}, bf16[4,2048,512]{1,2,0:T(8,128)(2,1)}, u32[]{:S(2)}, u32[]{:S(2)}) collective-permute-start(bf16[4,2048,512]{1,2,0:T(8,128)(2,1)} %bitcast_convert_fusion.2), channel_id=1, source_target_pairs={{0,1},{1,0},{2,3},{3,2},{4,5},{5,4},{6,7},{7,6},{8,9},{9,8},{10,11... | collective-permute-start | bytes 25165832 | tf_op jit(solution)/shard_map/ppermute | solution.py:358
  1106.2 14.5 copy-start.89
  1106.2 14.5 copy-start.17
  1106.2 14.5 copy-start.38
  1106.2 14.5 copy-start.44
  1106.2 14.5 copy-start.47
  1106.2 14.5 copy-start.72
  1106.2 14.5 copy-start.77
  1106.2 14.5 copy-start.79
  1120.4 54.5 %collective-permute-start.3 = (bf16[4,256,2048]{2,1,0:T(8,128)(2,1)}, bf16[4,256,2048]{2,1,0:T(8,128)(2,1)}, u32[]{:S(2)}, u32[]{:S(2)}) collective-permute-start(bf16[4,256,2048]{2,1,0:T(8,128)(2,1)} %bitcast_convert_fusion.3), channel_id=1, source_target_pairs={{0,1},{1,0},{2,3},{3,2},{4,5},{5,4},{6,7},{7,6},{8,9},{9,8},{10,11... | collective-permute-start | bytes 12582920 | tf_op jit(solution)/shard_map/ppermute | solution.py:358
  1122.0 22.4 %copy-start.25 = (s32[16,4,256]{2,1,0:T(4,128)S(1)}, s32[16,4,256]{2,1,0:T(4,128)}, u32[]{:S(2)}) copy-start(s32[16,4,256]{2,1,0:T(4,128)} %copy-done.24) | copy-start | bytes 196612
  1122.0 22.5 %copy-start.42 = (pred[16,4,256]{2,1,0:T(4,128)(4,1)S(1)}, pred[16,4,256]{2,1,0:T(4,128)(4,1)}, u32[]{:S(2)}) copy-start(pred[16,4,256]{2,1,0:T(4,128)(4,1)} %copy-done.41) | copy-start | bytes 49156
  1390.9 26.9 %copy-start.7 = (bf16[256,2048]{1,0:T(8,128)(2,1)S(1)}, bf16[256,2048]{1,0:T(8,128)(2,1)}, u32[]{:S(2)}) copy-start(bf16[256,2048]{1,0:T(8,128)(2,1)} %param.17) | copy-start | bytes 3145732
  1390.9 26.9 %copy-start.63 = (f32[2048]{0:T(1024)S(1)}, f32[2048]{0:T(1024)}, u32[]{:S(2)}) copy-start(f32[2048]{0:T(1024)} %copy-done.61) | copy-start | bytes 24580
  1390.9 28.9 %copy-start.68 = (f32[2048]{0:T(1024)S(1)}, f32[2048]{0:T(1024)}, u32[]{:S(2)}) copy-start(f32[2048]{0:T(1024)} %get-tuple-element.299) | copy-start | bytes 24580
  1390.9 28.9 %copy-start.90 = (f32[128]{0:T(128)S(1)}, f32[128]{0:T(128)}, u32[]{:S(2)}) copy-start(f32[128]{0:T(128)} %get-tuple-element.303) | copy-start | bytes 1540
  1390.9 28.9 %copy-start.91 = (f32[128]{0:T(128)S(1)}, f32[128]{0:T(128)}, u32[]{:S(2)}) copy-start(f32[128]{0:T(128)} %get-tuple-element.301) | copy-start | bytes 1540
  1415.9 37.8 %copy-start.54 = (f32[2048]{0:T(1024)S(1)}, f32[2048]{0:T(1024)}, u32[]{:S(2)}) copy-start(f32[2048]{0:T(1024)} %copy-done.52) | copy-start | bytes 24580
  1415.9 37.8 %copy-start.75 = (f32[256]{0:T(256)S(1)}, f32[256]{0:T(256)}, u32[]{:S(2)}) copy-start(f32[256]{0:T(256)} %copy-done.73) | copy-start | bytes 3076
  1415.9 37.8 %copy-start.81 = (f32[256]{0:T(256)S(1)}, f32[256]{0:T(256)}, u32[]{:S(2)}) copy-start(f32[256]{0:T(256)} %copy-done.80) | copy-start | bytes 3076
  1453.7 10.7 copy-start.1
  (50 other events, 152.9 us)
Sparse Core Ops, SparseCore 0:
  10.4 37.1 all-gather.4
  106.2 46.1 reduce-scatter.4
  885.7 46.3 all-gather.10
  946.1 69.1 reduce-scatter.10
  1069.9 44.5 reduce-scatter.6
  1118.0 126.1 reduce-scatter.8
  1250.2 125.3 all-reduce.5
Sparse Core Ops, SparseCore 1:
  109.3 193.5 all-gather.8
  306.1 188.9 all-gather.6

commit v3 on v2

--- a/solution.py
+++ b/solution.py
@@ -8,6 +8,7 @@
 from jax.experimental.pallas import tpu as pltpu
 from jax.sharding import Mesh
 from jax.sharding import PartitionSpec as P
+
 
 HIGH = lax.Precision.HIGHEST
 EPS_NORM = 1e-05
@@ -307,6 +308,177 @@
     )(parts.reshape(depth, 2, 2, rows, columns))
 
 
+def turn(value, cosine, sine):
+    return value * cosine + pltpu.roll(value, value.shape[-1] // 2, 1) * sine
+
+
+def turn_back(value, cosine, sine):
+    return value * cosine + pltpu.roll(value * sine, value.shape[-1] // 2, 1)
+
+
+def head_norm(raw):
+    inverse = lax.rsqrt(jnp.mean(raw * raw, axis=-1, keepdims=True) + EPS_HEAD)
+    return raw * inverse, inverse
+
+
+def dot_nt(left, right):
+    return lax.dot_general(left, right, (((1,), (1,)), ((), ())), preferred_element_type=F32)
+
+
+def dot_tn(left, right):
+    return lax.dot_general(left, right, (((0,), (0,)), ((), ())), preferred_element_type=F32)
+
+
+def dot_nn(left, right):
+    return lax.dot_general(left, right, (((1,), (0,)), ((), ())), preferred_element_type=F32)
+
+
+def weights_of(q_rows, keys, doc_rows, doc_keys, scale):
+    scores = dot_nt(q_rows, keys) * scale
+    scores = jnp.where(doc_rows == doc_keys, scores, MASKED)
+    lifted = jnp.exp(scores - jnp.max(scores, axis=-1, keepdims=True))
+    return lifted / jnp.sum(lifted, axis=-1, keepdims=True)
+
+
+def attend_kernel(step, q_ref, k_ref, v_ref, qg_ref, kg_ref, cos_ref, sin_ref, dr_ref, dk_ref, o_ref):
+    scale = q_ref.shape[-1] ** (-0.5)
+    cosine, sine = cos_ref[...], sin_ref[...]
+    queries = turn(head_norm(q_ref[...])[0] * qg_ref[...], cosine, sine).astype(BF16)
+    keys = turn(head_norm(k_ref[...])[0] * kg_ref[...], cosine, sine).astype(BF16)
+    values = v_ref[...].astype(BF16)
+    for at in range(0, q_ref.shape[0], step):
+        rows = slice(at, at + step)
+        weights = weights_of(queries[rows], keys, dr_ref[rows, :], dk_ref[...], scale)
+        o_ref[rows, :] = dot_nn(weights.astype(BF16), values).astype(BF16)
+
+
+def attend_back_kernel(
+    step, q_ref, k_ref, v_ref, go_ref, qg_ref, kg_ref, cos_ref, sin_ref, dr_ref, dk_ref,
+    gq_ref, gk_ref, gv_ref, gqg_ref, gkg_ref,
+):
+    scale = q_ref.shape[-1] ** (-0.5)
+    cosine, sine = cos_ref[...], sin_ref[...]
+    q_normed, q_inverse = head_norm(q_ref[...])
+    k_normed, k_inverse = head_norm(k_ref[...])
+    queries = turn(q_normed * qg_ref[...], cosine, sine).astype(BF16)
+    keys = turn(k_normed * kg_ref[...], cosine, sine).astype(BF16)
+    values = v_ref[...].astype(BF16)
+    grad_keys = jnp.zeros(k_ref.shape, F32)
+    grad_values = jnp.zeros(v_ref.shape, F32)
+    grad_queries = []
+    for at in range(0, q_ref.shape[0], step):
+        rows = slice(at, at + step)
+        probs = weights_of(queries[rows], keys, dr_ref[rows, :], dk_ref[...], scale)
+        grad_rows = go_ref[rows, :]
+        grad_weights = dot_nt(grad_rows, values)
+        delta = jnp.sum(grad_weights * probs, axis=-1, keepdims=True)
+        grad_scores = (probs * (grad_weights - delta)).astype(BF16)
+        grad_queries.append(dot_nn(grad_scores, keys))
+        grad_keys = grad_keys + dot_tn(grad_scores, queries[rows])
+        grad_values = grad_values + dot_tn(probs.astype(BF16), grad_rows)
+
+    @pl.when(pl.program_id(0) == 0)
+    def _():
+        gqg_ref[...] = jnp.zeros_like(gqg_ref)
+        gkg_ref[...] = jnp.zeros_like(gkg_ref)
+
+    def finish(grad, normed, inverse, gain_ref, out_ref, gain_grad_ref):
+        grad = turn_back(grad * scale, cosine, sine)
+        gain_grad_ref[...] += jnp.sum(grad * normed, axis=0, keepdims=True)
+        lifted = grad * gain_ref[...]
+        inner = jnp.mean(lifted * normed, axis=-1, keepdims=True)
+        out_ref[...] = ((lifted - normed * inner) * inverse).astype(BF16)
+
+    finish(jnp.concatenate(grad_queries, axis=0), q_normed, q_inverse, qg_ref, gq_ref, gqg_ref)
+    finish(grad_keys, k_normed, k_inverse, kg_ref, gk_ref, gkg_ref)
+    gv_ref[...] = grad_values.astype(BF16)
+
+
+def attention_call(kernel, heads, head_dim, seq_len, values, tables, outs, flops):
+    column = pl.BlockSpec((seq_len, head_dim), lambda head: (0, head))
+    whole = [pl.BlockSpec(t.shape, lambda head: (0, 0)) for t in tables]
+    shapes = [
+        jax.ShapeDtypeStruct((seq_len, heads * head_dim), BF16) if wide
+        else jax.ShapeDtypeStruct((1, head_dim), F32)
+        for wide in outs
+    ]
+    specs = [column if wide else pl.BlockSpec((1, head_dim), lambda head: (0, 0)) for wide in outs]
+    return pl.pallas_call(
+        functools.partial(kernel, min(512, seq_len)),
+        grid=(heads,),
+        out_shape=shapes,
+        in_specs=[column] * len(values) + whole,
+        out_specs=specs,
+        compiler_params=pltpu.CompilerParams(vmem_limit_bytes=VMEM_BYTES),
+        cost_estimate=pl.CostEstimate(
+            flops=flops, bytes_accessed=16 * seq_len * heads * head_dim, transcendentals=heads * seq_len**2
+        ),
+        name="attention",
+    )(*values, *tables)
+
+
+def params(flops, moved):
+    return dict(compiler_params=pltpu.CompilerParams(vmem_limit_bytes=VMEM_BYTES),
+        cost_estimate=pl.CostEstimate(flops=flops, bytes_accessed=moved, transcendentals=0))
+
+
+def combine_kernel(pick_ref, value_ref, out_ref):
+    local, _, capacity, width = value_ref.shape
+    out_ref[0] = dot_tn(pick_ref[0], value_ref[...].reshape(local*capacity, width)).astype(BF16)
+
+
+def combine(pick, value):
+    blocks, picked, rows = pick.shape
+    local, _, capacity, width = value.shape
+    return pl.pallas_call(
+        combine_kernel, grid=(blocks,),
+        out_shape=jax.ShapeDtypeStruct((blocks, rows, width), BF16),
+        in_specs=[pl.BlockSpec((1, picked, rows), lambda b: (b, 0, 0)), pl.BlockSpec((local, 1, capacity, width), lambda b: (0, b, 0, 0))],
+        out_specs=pl.BlockSpec((1, rows, width), lambda b: (b, 0, 0)),
+        name="combine", **params(2*blocks*picked*rows*width, 2*blocks*width*(picked+rows)),
+    )(pick, value)
+
+
+def expert_kernel(x_ref, w0_ref, w1_ref, u0_ref, u1_ref, pr_ref, gx_ref, dots_ref, *outs):
+    x = x_ref[0]
+    prob = pr_ref[0]
+    total = None
+    dots = None
+    for w_ref, u_ref, hp_ref, ggu_ref in ((w0_ref, u0_ref, outs[0], outs[2]), (w1_ref, u1_ref, outs[1], outs[3])):
+        n = u_ref.shape[-1]
+        both = dot_nn(x, w_ref[0])
+        gate, up = both[:, :n], both[:, n:]
+        sigma = jax.nn.sigmoid(gate)
+        silu = gate * sigma
+        hidden = (silu * up).astype(BF16).astype(F32)
+        back = u_ref[0]
+        part = jnp.sum(hidden * back, axis=-1, keepdims=True)
+        dots = part if dots is None else dots + part
+        hp_ref[0] = (hidden * prob).astype(BF16)
+        gh = back * prob
+        ggu_ref[0, :, :n] = (gh * up * (sigma + silu * (1.0 - sigma))).astype(BF16)
+        ggu_ref[0, :, n:] = (gh * silu).astype(BF16)
+        part = dot_nt(ggu_ref[0], w_ref[0])
+        total = part if total is None else total + part
+    gx_ref[0] = total.astype(BF16)
+    dots_ref[0] = dots
+
+
+def expert(x, w0, w1, u0, u1, prob, step):
+    local, count, width = x.shape
+    n = u0.shape[-1]
+    r = lambda c: pl.BlockSpec((1, step, c), lambda e, i: (e, i, 0))
+    w = pl.BlockSpec((1, width, 2*n), lambda e, i: (e, 0, 0))
+    s = lambda c, t: jax.ShapeDtypeStruct((local, count, c), t)
+    return pl.pallas_call(
+        expert_kernel, grid=(local, count//step),
+        out_shape=[s(width,BF16), s(1,F32), s(n,BF16), s(n,BF16), s(2*n,BF16), s(2*n,BF16)],
+        in_specs=[r(width), w, w, r(n), r(n), r(1)],
+        out_specs=[r(width), r(1), r(n), r(n), r(2*n), r(2*n)],
+        name="expert", **params(16*local*count*width*n, local*(count*(width*4+n*20)+8*width*n)),
+    )(x, w0, w1, u0, u1, prob)
+
+
 def norm_rows(value, gain):
     inverse = lax.rsqrt(jnp.mean(value * value, axis=-1, keepdims=True) + EPS_NORM)
     return value * inverse * gain
@@ -318,19 +490,6 @@
     lifted = grad * gain
     inner = jnp.mean(lifted * normed, axis=-1, keepdims=True)
     return (lifted - normed * inner) * inverse, jnp.sum(grad * normed, axis=0)
-
-
-def rms_scale(value, gain, eps):
-    return value * lax.rsqrt(jnp.mean(value * value, axis=-1, keepdims=True) + eps) * gain
-
-
-def rotate(value, cosine, sine):
-    half = value.shape[-1] // 2
-    first = value[..., :half]
-    second = value[..., half:]
-    return jnp.concatenate(
-        [first * cosine - second * sine, second * cosine + first * sine], axis=-1
-    )
 
 
 def positions(lengths, seq_len):
@@ -405,9 +564,6 @@
     qkv_local = w_qkv.shape[2]
     heads = qkv_local // head_dim
     capacity = min(3 * rows * topk // (2 * experts_all), rows)
-    q_rows = min(512, seq_len)
-    q_count = seq_len // q_rows
-    scale = head_dim ** (-0.5)
     my_ep = lax.axis_index("ep")
 
     gain_one = norm1_gain.astype(F32)
@@ -415,115 +571,80 @@
     inputs = layer_input.astype(F32)
     grad_out = d_out.astype(F32)
     input_seq = gather(layer_input, GROUP)
+    g_flat = gather(d_out, PLANE)
     h_seq = norm_rows(input_seq.astype(F32), gain_one).astype(BF16)
     w_parts = w_qkv.transpose(1, 0, 2)
-    q_raw, k_raw, v_raw = (
-        jnp.dot(h_seq, w_parts[part], preferred_element_type=F32).reshape(
-            seq_len, heads, head_dim
-        )
-        for part in range(3)
-    )
+    raw = [jnp.dot(h_seq, w_parts[part], preferred_element_type=F32) for part in range(3)]
     doc_ids, position = positions(doc_lengths[0], seq_len)
     cosine, sine = rope_tables(position, head_dim)
-    cosine = cosine[:, None, :]
-    sine = sine[:, None, :]
-
-    def shape_heads(value, gain):
-        return rotate(rms_scale(value, gain, EPS_HEAD), cosine, sine)
-
-    q_rot, q_back = jax.vjp(shape_heads, q_raw, q_gain.astype(F32))
-    k_rot, k_back = jax.vjp(shape_heads, k_raw, k_gain.astype(F32))
-    queries = q_rot.astype(BF16)
-    keys = k_rot.astype(BF16)
-    values = v_raw.astype(BF16)
-    q_blocks = queries.reshape(q_count, q_rows, heads, head_dim)
-    doc_blocks = doc_ids.reshape(q_count, q_rows)
-
-    def scores_of(q_block, doc_block):
-        plain = einsum("qhd,khd->hqk", q_block, keys) * scale
-        return jnp.where((doc_block[:, None] == doc_ids[None, :])[None], plain, MASKED)
-
-    def attend(item):
-        q_block, doc_block = item
-        scores = scores_of(q_block, doc_block)
-        peak = jnp.max(scores, axis=-1, keepdims=True)
-        lifted = jnp.exp(scores - peak)
-        total = jnp.sum(lifted, axis=-1, keepdims=True)
-        weights = (lifted / total).astype(BF16)
-        return (einsum("hqk,khd->qhd", weights, values), peak, total)
-
-    mixed, peaks, totals = lax.map(attend, (q_blocks, doc_blocks))
-    attn_vals = mixed.reshape(seq_len, qkv_local).astype(BF16)
+    tables = (
+        q_gain.astype(F32)[None],
+        k_gain.astype(F32)[None],
+        jnp.concatenate([cosine, cosine], axis=1),
+        jnp.concatenate([-sine, sine], axis=1),
+        doc_ids[:, None],
+        doc_ids[None, :],
+    )
+    (attn_vals,) = attention_call(
+        attend_kernel, heads, head_dim, seq_len, raw, tables, (True,), 4 * seq_len**2 * qkv_local
+    )
     attn_out = scatter(jnp.dot(attn_vals, w_out, preferred_element_type=F32).astype(BF16), GROUP)
     middle = inputs + attn_out.astype(F32)
     h_two = norm_rows(middle, gain_two).astype(BF16)
 
-    g_plane = gather(d_out, PLANE).reshape(blocks, rows, width)
+    g_plane = g_flat.reshape(blocks, rows, width)
     routes_plane = spread(routes.T, PLANE, 1).transpose(0, 2, 1).reshape(blocks * rows, topk)
     h_flat = gather(h_two, PLANE)
-    h_plane = h_flat.reshape(blocks, rows, width)
-    gate_own = expert_gate_up[:, :, 0]
-    up_own = expert_gate_up[:, :, 1]
     pair_other = swap_cores(expert_gate_up.reshape(local, width, 2 * hidden_local))
     down_other = swap_cores(expert_down)
     pair_own = expert_gate_up.reshape(local, width, 2 * hidden_local)
 
     mask_plane = route_mask(routes_plane, experts_all)
-    logits_plane = jnp.dot(h_flat, w_router, preferred_element_type=F32)
-    probs_plane = masked_softmax(logits_plane, mask_plane)
     first = my_ep * local
     mask_here = lax.dynamic_slice_in_dim(mask_plane, first, local, axis=1)
-    probs_here = lax.dynamic_slice_in_dim(probs_plane, first, local, axis=1)
     mask_here = mask_here.reshape(blocks, rows, local).transpose(0, 2, 1)
-    probs_here = probs_here.reshape(blocks, rows, local).transpose(0, 2, 1)
     before = jnp.triu(jnp.ones((rows, rows), BF16), 1)
     rank = einsum("bet,tu->beu", mask_here.astype(BF16), before).astype(jnp.int32)
     slots = jnp.arange(capacity, dtype=jnp.int32)[None, None, :, None]
     picks = mask_here[:, :, None, :] & (rank[:, :, None, :] == slots)
     pick = picks.astype(BF16)
+    pick_rows = pick.reshape(blocks, local * capacity, rows)
+    count = blocks * capacity
+
+    g_rows = einsum("bect,btd->ebcd", pick, g_plane).astype(BF16)
+    back_own = einsum("ebcd,efd->ebcf", g_rows, expert_down).reshape(local, count, -1)
+    back_other = einsum("ebcd,efd->ebcf", g_rows, down_other).reshape(local, count, -1)
+    h_flat, back_own, back_other = lax.optimization_barrier((h_flat, back_own, back_other))
+    h_plane = h_flat.reshape(blocks, rows, width)
+    h_rows = einsum("bect,btd->ebcd", pick, h_plane).astype(BF16)
+    logits_plane = jnp.dot(h_flat, w_router, preferred_element_type=F32)
+    probs_plane = masked_softmax(logits_plane, mask_plane)
+    probs_here = lax.dynamic_slice_in_dim(probs_plane, first, local, axis=1)
+    probs_here = probs_here.reshape(blocks, rows, local).transpose(0, 2, 1)
     prob_rows = jnp.sum(jnp.where(picks, probs_here[:, :, None, :], 0.0), axis=-1)
-    prob_rows = prob_rows.transpose(1, 0, 2)[..., None]
-
-    g_rows = einsum("bect,btd->ebcd", pick, g_plane).astype(BF16)
-    h_rows = einsum("bect,btd->ebcd", pick, h_plane).astype(BF16)
-
-    def expert_half(pair, down):
-        gate = einsum("ebcd,edf->ebcf", h_rows, pair[:, :, :hidden_local])
-        up = einsum("ebcd,edf->ebcf", h_rows, pair[:, :, hidden_local:])
-        back = einsum("ebcd,efd->ebcf", g_rows, down)
-        sigma = jax.nn.sigmoid(gate)
-        silu = gate * sigma
-        hidden = (silu * up).astype(BF16).astype(F32)
-        dots = jnp.sum(hidden * back, axis=-1)
-        weighted = (hidden * prob_rows).astype(BF16)
-        grad_hidden = back * prob_rows
-        grad_gate = (grad_hidden * up * (sigma + silu * (1.0 - sigma))).astype(BF16)
-        grad_up = (grad_hidden * silu).astype(BF16)
-        return dots, weighted, jnp.concatenate([grad_gate, grad_up], axis=-1)
-
-    dots_own, weighted_own, ggu_own = expert_half(pair_own, expert_down)
-    dots_other, weighted_other, ggu_other = expert_half(pair_other, down_other)
-    back_rows = (
-        einsum("ebcf,edf->ebcd", ggu_own, pair_own)
-        + einsum("ebcf,edf->ebcd", ggu_other, pair_other)
-    ).astype(BF16)
-    out_rows = (
-        einsum("ebcf,efd->ebcd", weighted_own, expert_down)
-        + einsum("ebcf,efd->ebcd", weighted_other, down_other)
-    ).astype(BF16)
-    dot_rows = (dots_own + dots_other).transpose(1, 0, 2)
+    prob_rows = prob_rows.transpose(1, 0, 2).reshape(local, count, 1)
+    h_rows = h_rows.reshape(local, count, width)
+    g_rows = g_rows.reshape(local, count, width)
+    back_rows, dot_rows, weighted_own, weighted_other, ggu_own, ggu_other = expert(
+        h_rows, pair_own, pair_other, back_own, back_other, prob_rows, min(384, count)
+    )
+    dot_rows = dot_rows.reshape(local, blocks, capacity).transpose(1, 0, 2)
     dots_token = jnp.sum(jnp.where(picks, dot_rows[..., None], 0.0), axis=2)
     grad_probs = spread(dots_token, PLANE, 2, True)
     grad_probs = jnp.sum(grad_probs.reshape(ep_count, x_count, local, rows), axis=1)
     grad_probs = grad_probs.reshape(experts_all, rows).T
-    back_part = einsum("bect,ebcd->btd", pick, back_rows).astype(BF16)
+    back_part = combine(pick_rows, back_rows.reshape(local, blocks, capacity, width))
     back_sum = plane_reduce(back_part, 3)
-    out_part = einsum("bect,ebcd->btd", pick, out_rows).astype(BF16)
-
-    grad_pair_own = einsum("ebcd,ebcf->edf", h_rows, ggu_own)
-    grad_pair_other = einsum("ebcd,ebcf->edf", h_rows, ggu_other)
-    grad_down_own = einsum("ebcf,ebcd->efd", weighted_own, g_rows)
-    grad_down_other = einsum("ebcf,ebcd->efd", weighted_other, g_rows)
+    out_rows = (
+        einsum("emf,efd->emd", weighted_own, expert_down)
+        + einsum("emf,efd->emd", weighted_other, down_other)
+    ).astype(BF16)
+    out_part = combine(pick_rows, out_rows.reshape(local, blocks, capacity, width))
+
+    grad_pair_own = einsum("emd,emf->edf", h_rows, ggu_own)
+    grad_pair_other = einsum("emd,emf->edf", h_rows, ggu_other)
+    grad_down_own = einsum("emf,emd->efd", weighted_own, g_rows)
+    grad_down_other = einsum("emf,emd->efd", weighted_other, g_rows)
     grad_pair = grad_pair_own + swap_cores(grad_pair_other.astype(BF16)).astype(F32)
     grad_down = grad_down_own + swap_cores(grad_down_other.astype(BF16)).astype(F32)
     grad_gate_up = grad_pair.reshape(local, width, 2, hidden_local)
@@ -540,39 +661,23 @@
     grad_mid = grad_out + grad_mid_norm
 
     ga_seq = gather(grad_mid.astype(BF16), GROUP)
+    ga_seq, out_part = lax.optimization_barrier((ga_seq, out_part))
     grad_wout = lax.dot_general(
         attn_vals, ga_seq, (((0,), (0,)), ((), ())), preferred_element_type=F32
     )
     grad_vals = lax.dot_general(
         ga_seq, w_out, (((1,), (1,)), ((), ())), preferred_element_type=F32
     )
-    grad_mixed = grad_vals.astype(BF16).reshape(q_count, q_rows, heads, head_dim)
-
-    def attend_back(carry, item):
-        grad_keys, grad_values = carry
-        q_block, doc_block, peak, total, grad_block = item
-        scores = scores_of(q_block, doc_block)
-        probs_full = jnp.exp(scores - peak) / total
-        weights = probs_full.astype(BF16)
-        grad_weights = einsum("qhd,khd->hqk", grad_block, values)
-        delta = jnp.sum(grad_weights * probs_full, axis=-1, keepdims=True)
-        grad_scores = (probs_full * (grad_weights - delta)).astype(BF16)
-        grad_q = einsum("hqk,khd->qhd", grad_scores, keys) * scale
-        grad_keys = grad_keys + einsum("hqk,qhd->khd", grad_scores, q_block) * scale
-        grad_values = grad_values + einsum("hqk,qhd->khd", weights, grad_block)
-        return ((grad_keys, grad_values), grad_q)
-
-    head_zeros = jnp.zeros((seq_len, heads, head_dim), F32)
-    (grad_keys, grad_values), grad_queries = lax.scan(
-        attend_back, (head_zeros, head_zeros), (q_blocks, doc_blocks, peaks, totals, grad_mixed)
-    )
-    grad_queries = grad_queries.reshape(seq_len, heads, head_dim)
-    grad_q_raw, grad_q_gain = q_back(grad_queries)
-    grad_k_raw, grad_k_gain = k_back(grad_keys)
-    grad_proj = [
-        grad.reshape(seq_len, qkv_local).astype(BF16)
-        for grad in (grad_q_raw, grad_k_raw, grad_values)
-    ]
+    *grad_proj, grad_q_gain, grad_k_gain = attention_call(
+        attend_back_kernel,
+        heads,
+        head_dim,
+        seq_len,
+        (*raw, grad_vals.astype(BF16)),
+        tables,
+        (True, True, True, False, False),
+        10 * seq_len**2 * qkv_local,
+    )
     grad_h_part = sum(
         lax.dot_general(grad, w, (((1,), (1,)), ((), ())), preferred_element_type=F32)
         for grad, w in zip(grad_proj, w_parts)
@@ -593,7 +698,7 @@
     out_part, grad_proj = lax.optimization_barrier((out_part, grad_proj))
     output = (middle + plane_reduce(out_part, 4)).astype(BF16)
     grad_router = lax.psum(grad_router, ALL)
-    small = jnp.concatenate([grad_gain_one, grad_gain_two, grad_q_gain, grad_k_gain])
+    small = jnp.concatenate([grad_gain_one, grad_gain_two, grad_q_gain[0], grad_k_gain[0]])
     small = jnp.sum(spread(small.reshape(-1, 128), ALL, 5), axis=0).reshape(-1)
     gains = jnp.split(small, (width, 2 * width, 2 * width + head_dim))
     return (
@@ -642,6 +747,7 @@
         P("ep", None, None, GROUP),
         P("ep", GROUP, None),
     )
+
     return jax.shard_map(
         per_device, mesh=fine, in_specs=in_specs, out_specs=out_specs, check_vma=False
     )

time: 1490 us -> 1370 us (0.919)
  Pallas kernels: 385 us -> 581 us
  matrix products: 444 us -> 272 us
  local copies, waits for them, and re-layouts: 153 us -> 95.1 us
  waiting for transfers between devices: 386 us -> 342 us
  other arithmetic: 84.3 us -> 46.4 us
    dot_general x31 -> x11, matrix products: 372 us -> 199 us  [einsum(): return jnp.einsum(spec, left, right, preferred_element_type=F32)]
    pallas_call x0 -> x5, Pallas kernels: none -> 167 us  [the longest x1 63.5 us: expert(): pl.pallas_call(expert_kernel, grid=(local, count // step), out_shape=[s(w...]
    all_gather x4, waiting for transfers between devices: 339 us -> 289 us  [gather(): return lax.all_gather(value, axes, axis=0, tiled=True)]
    dynamic_update_slice x6 -> x0, local copies, waits for them, and re-layouts: 46.3 us -> none  [per_device(): mixed, peaks, totals = lax.map(attend, (q_blocks, doc_blocks))]
    convert_element_type x1 -> x2, local copies, waits for them, and re-layouts: 2.43 us -> 43.2 us  [the longest x1 22.2 us: per_device(): g_rows = einsum('bect,btd->ebcd', pick, g_plane).astype(BF16)]
    pallas_call x2, Pallas kernels: 334 us -> 366 us  [plane_reduce(): pl.pallas_call(functools.partial(reduce_kernel, depth, half), out_shape=j...]
    convert_element_type x8 -> x1, other arithmetic: 27.9 us -> 2.74 us  [per_device(): pick = picks.astype(BF16)]
    dot_general x4 -> x0, local copies, waits for them, and re-layouts: 17.6 us -> none  [per_device(): jnp.dot(h_seq, w_parts[part], preferred_element_type=F32)]
  transfers between devices with their start and end apart: 13 -> 13, of which waited for: 5 -> 5; matrix products, arithmetic and copies ran while one was open for 32% -> 27% of each run, Pallas kernels for 15% -> 22%
where the time goes in v3:
time: 1370 us; the launch traced here: 1350 us
  Pallas kernels  581 us (42%)
  waiting for transfers between devices  342 us (25%)
  matrix products  272 us (20%)
  local copies, waits for them, and re-layouts  95.1 us (7%)
  other arithmetic  46.4 us (3%)
  between operations  16.5 us (1%)
    pallas_call x2, Pallas kernels, plane_reduce(): pl.pallas_call(functools.partial(reduce_kernel, depth, half), out_shape=j...  366 us
    all_gather x4, waiting for transfers between devices, gather(): return lax.all_gather(value, axes, axis=0, tiled=True)  289 us
    dot_general x11, matrix products, einsum(): return jnp.einsum(spec, left, right, preferred_element_type=F32)  199 us
    pallas_call x1, Pallas kernels, expert(): pl.pallas_call(expert_kernel, grid=(local, count // step), out_shape=[s(w...  63.5 us
    pallas_call x2, Pallas kernels, attention_call(): pl.pallas_call(functools.partial(kernel, min(512, seq_len)), grid=(heads,...  53 us
    pallas_call x2, Pallas kernels, combine(): pl.pallas_call(combine_kernel, grid=(blocks,), out_shape=jax.ShapeDtypeSt...  50 us
    pallas_call x3, Pallas kernels, spread(): pl.pallas_call(functools.partial(spread_kernel, axes, counts, own_slices)...  48.9 us
    reduce_scatter x4, waiting for transfers between devices, scatter(): return lax.psum_scatter(value, axes, scatter_dimension=dim, tiled=True)  45.7 us
  transfers between devices with their start and end apart: 13, of which 5 were waited for; matrix products, arithmetic and copies ran while one was open for 27% of the time, Pallas kernels for 22%

profile of v3, /device:TPU:0, one launch (start us, length us, event | category | flops | bytes accessed | tf_op | source)
XLA Modules:
  0.0 1354.7 jit_solution(17787570135849754551)
XLA Ops:
  12.3 1.9 fusion.37
  14.2 1.4 pad_maximum_fusion.1
  16.1 31.6 %all-gather.5.cloned.1.call-done = bf16[1024,2048]{1,0:T(8,128)(2,1)} async-done(((bf16[256,2048]{1,0:T(8,128)(2,1)}), bf16[1024,2048]{1,0:T(8,128)(2,1)}) %all-gather.5.cloned.1.call-update) | async-done | bytes 4194320 | tf_op jit(solution)/shard_map/all_gather | solution.py:521
  47.6 3.2 fusion
  51.1 5.7 fusion.32.k_ref
  56.8 3.7 fusion.33.v_ref
  60.5 3.7 fusion.30.q_ref
  64.2 22.6 %attention.2 = bf16[1024,512]{1,0:T(8,128)(2,1)} custom-call(f32[1024,512]{1,0:T(8,128)} %fusion.30.q_ref, f32[1024,512]{1,0:T(8,128)} %fusion.32.k_ref, f32[1024,512]{1,0:T(8,128)} %fusion.33.v_ref, f32[1,128]{1,0:T(1,128)} %get-tuple-element.113.qg_ref, f32[1,128]{1,0:T(1,128)} %get-tuple-element.112.kg_ref, f32[1024,128]{1,0:T(8,128)} %get-tuple-element.110.cos_ref, ...), custom_call_target="tpu_custom_call" | custom-call | flops 2147483648 | bytes 8388608 | tf_op jit(solution)/shard_map/attention/pallas_call | solution.py:406
  86.8 5.6 convolution_convert_fusion.2
  93.0 45.7 %reduce-scatter.5.cloned.1.call-done = bf16[256,2048]{1,0:T(8,128)(2,1)} async-done(((bf16[1024,2048]{1,0:T(8,128)(2,1)}), bf16[256,2048]{1,0:T(8,128)(2,1)}) %reduce-scatter.5.cloned.1.call-update) | async-done | bytes 1048592 | tf_op jit(solution)/shard_map/reduce_scatter | solution.py:525
  138.7 1.6 multiply_reduce_fusion.2
  140.9 2.6 multiply_convert_fusion
  143.7 14.6 %reshape.167.w0_ref = bf16[4,2048,512]{2,1,0:T(8,128)(2,1)} reshape(bf16[4,2048,2,256]{3,2,1,0:T(2,128)(2,1)} %param.23) | data formatting | bytes 16777216 | tf_op jit(solution)/shard_map/reshape | solution.py:600
  158.8 10.5 spread.3
  169.3 1.4 fusion.12
  171.1 2.7 fusion.7.pick_ref
  175.6 112.4 %all-gather.9.cloned.1.call-done = bf16[4096,2048]{1,0:T(8,128)(2,1)} async-done(((bf16[256,2048]{1,0:T(8,128)(2,1)}), bf16[4096,2048]{1,0:T(8,128)(2,1)}) %all-gather.9.cloned.1.call-update) | async-done | bytes 16777232 | tf_op jit(solution)/shard_map/all_gather | solution.py:521
  288.0 17.7 %convert_bitcast_fusion.1 = bf16[4,16,96,2048]{3,2,0,1:T(8,128)(2,1)} fusion(bf16[16,256,2048,1]{2,1,3,0:T(8,128)(2,1)} %bitcast.162, s32[16,4,256]{2,1,0:T(4,128)S(1)} %copy.76, pred[16,4,256]{2,1,0:T(4,128)(4,1)S(1)} %copy.75), kind=kOutput, calls=%fused_computation.2 | convolution fusion | flops 6458179584 | bytes 42024960 | tf_op jit(solution)/shard_map/bect,btd->ebcd/dot_general | solution.py:513
  305.6 14.6 %fusion.10 = f32[4,16,96,256]{3,2,1,0:T(8,128)} fusion(bf16[4,256,2048]{2,1,0:T(8,128)(2,1)} %param.24, bf16[4,16,96,2048]{3,2,0,1:T(8,128)(2,1)} %convert_bitcast_fusion.1), kind=kOutput, calls=%fused_computation.23 | convolution fusion | flops 6442450944 | bytes 35651584 | tf_op jit(solution)/shard_map/ebcd,efd->ebcf/dot_general | solution.py:513
  320.3 14.6 %fusion.8 = f32[4,16,96,256]{3,2,1,0:T(8,128)} fusion(bf16[4,256,2048]{2,1,0:T(8,128)(2,1)} %collective-permute-done, bf16[4,16,96,2048]{3,2,0,1:T(8,128)(2,1)} %convert_bitcast_fusion.1), kind=kOutput, calls=%fused_computation.21 | convolution fusion | flops 6442450944 | bytes 35651584 | tf_op jit(solution)/shard_map/ebcd,efd->ebcf/dot_general | solution.py:513
  334.9 145.2 %all-gather.7.cloned.1.call-done = bf16[4096,2048]{1,0:T(8,128)(2,1)} async-done(((bf16[256,2048]{1,0:T(8,128)(2,1)}), bf16[4096,2048]{1,0:T(8,128)(2,1)}) %all-gather.7.cloned.1.call-update) | async-done | bytes 16777232 | tf_op jit(solution)/shard_map/all_gather | solution.py:521
  480.1 10.9 fusion.64
  491.2 1.5 select_reduce_fusion.1
  492.7 4.8 reshape.187.pr_ref
  497.5 19.4 %convert_bitcast_fusion = bf16[4,16,96,2048]{3,2,0,1:T(8,128)(2,1)} fusion(bf16[16,256,2048,1]{2,1,3,0:T(8,128)(2,1)} %bitcast.159, s32[16,4,256]{2,1,0:T(4,128)S(1)} %copy.76, pred[16,4,256]{2,1,0:T(4,128)(4,1)S(1)} %copy.75), kind=kOutput, calls=%fused_computation.1 | convolution fusion | flops 6458179584 | bytes 42024960 | tf_op jit(solution)/shard_map/bect,btd->ebcd/dot_general | solution.py:513
  516.9 21.0 %copy.79 = bf16[4,16,96,2048]{3,2,1,0:T(8,128)(2,1)} copy(bf16[4,16,96,2048]{3,2,0,1:T(8,128)(2,1)} %convert_bitcast_fusion) | data formatting | bytes 50331648 | tf_op jit(solution)/shard_map/convert_element_type | solution.py:619
  537.9 63.5 %expert.1 = (bf16[4,1536,2048]{2,1,0:T(8,128)(2,1)}, f32[4,1536,1]{2,1,0:T(8,128)}, bf16[4,1536,256]{2,1,0:T(8,128)(2,1)}, bf16[4,1536,256]{2,1,0:T(8,128)(2,1)}...) custom-call(bf16[4,1536,2048]{2,1,0:T(8,128)(2,1)} %bitcast.163, bf16[4,2048,512]{2,1,0:T(8,128)(2,1)} %reshape.167.w0_ref, ...), custom_call_target="tpu_custom_call" | custom-call | flops 51539607552 | bytes 98566144 | tf_op jit(solution)/shard_map/expert/pallas_call | solution.py:473
  601.5 2.8 reduce
  604.4 3.3 select_reduce_fusion.v_ref
  607.6 9.1 spread.4
  617.6 25.0 %combine.2 = bf16[16,256,2048]{2,1,0:T(8,128)(2,1)} custom-call(bf16[16,384,256]{2,1,0:T(8,128)(2,1)} %fusion.7.pick_ref, bf16[4,16,96,2048]{3,2,1,0:T(8,128)(2,1)} %bitcast.168), custom_call_target="tpu_custom_call" | custom-call | flops 6442450944 | bytes 41943040 | tf_op jit(solution)/shard_map/combine/pallas_call | solution.py:433
  642.6 158.4 %plane_reduce.2 = f32[256,2048]{1,0:T(8,128)} custom-call(bf16[4,2,2,256,2048]{4,3,2,1,0:T(8,128)(2,1)} %bitcast.161), custom_call_target="tpu_custom_call" | custom-call | tf_op jit(solution)/shard_map/plane_reduce/pallas_call | solution.py:292
  801.1 4.5 multiply_reduce_fusion
  805.7 1.3 copy-done.5
  807.0 1.8 fusion.54
  808.9 23.8 %fusion.66 = f32[4,1536,2048]{2,1,0:T(8,128)} fusion(bf16[4,1536,256]{2,1,0:T(8,128)(2,1)} %get-tuple-element.34, bf16[4,256,2048]{2,1,0:T(8,128)(2,1)} %collective-permute-done), kind=kOutput, calls=%fused_computation.126 | convolution fusion | flops 6442450944 | bytes 57671680 | tf_op jit(solution)/shard_map/emf,efd->emd/dot_general | solution.py:513
  832.7 29.1 %add_convert_fusion = bf16[4,1536,2048]{2,1,0:T(8,128)(2,1)} fusion(f32[4,1536,2048]{2,1,0:T(8,128)} %fusion.66, bf16[4,1536,256]{2,1,0:T(8,128)(2,1)} %get-tuple-element.33, bf16[4,256,2048]{2,1,0:T(8,128)(2,1)} %param.24), kind=kOutput, calls=%fused_computation | convolution fusion | flops 6467616768 | bytes 82837504 | tf_op jit(solution)/shard_map/emf,efd->emd/dot_general | solution.py:513
  861.9 25.0 %combine.3 = bf16[16,256,2048]{2,1,0:T(8,128)(2,1)} custom-call(bf16[16,384,256]{2,1,0:T(8,128)(2,1)} %fusion.7.pick_ref, bf16[4,16,96,2048]{3,2,1,0:T(8,128)(2,1)} %bitcast.158), custom_call_target="tpu_custom_call" | custom-call | flops 6442450944 | bytes 41943040 | tf_op jit(solution)/shard_map/combine/pallas_call | solution.py:433
  886.9 5.9 convolution_convert_fusion.3
  892.9 5.5 convolution_convert_fusion.7.go_ref
  898.4 30.4 %attention.3 = (bf16[1024,512]{1,0:T(8,128)(2,1)}, bf16[1024,512]{1,0:T(8,128)(2,1)}, bf16[1024,512]{1,0:T(8,128)(2,1)}, f32[1,128]{1,0:T(1,128)}, f32[1,128]{1,0:T(1,128)}) custom-call(f32[1024,512]{1,0:T(8,128)} %fusion.30.q_ref, f32[1024,512]{1,0:T(8,128)} %fusion.32.k_ref, f32[1024,512]{1,0:T(8,128)} %fusion.33.v_ref, ...), custom_call_target="tpu_custom_call" | custom-call | flops 5368709120 | bytes 8388608 | tf_op jit(solution)/shard_map/attention/pallas_call | solution.py:406
  928.8 4.4 fusion.29
  933.2 4.0 fusion.31
  937.2 6.3 add_convert_fusion.1
  944.2 5.3 fusion.20
  949.6 2.7 fusion.21
  952.3 2.7 fusion.22
  955.0 3.1 pad_maximum_fusion
  958.5 20.1 %convolution_convert_fusion = bf16[4,2048,512]{1,2,0:T(8,128)(2,1)} fusion(bf16[4,1536,2048]{2,1,0:T(8,128)(2,1)} %bitcast.164, bf16[4,1536,512]{2,1,0:T(8,128)(2,1)} %get-tuple-element.44), kind=kOutput, calls=%fused_computation.19 | convolution fusion | flops 12889096192 | bytes 39845888 | tf_op jit(solution)/shard_map/emd,emf->edf/dot_general | solution.py:513
  978.6 22.2 %copy.77 = bf16[4,16,96,2048]{3,2,1,0:T(8,128)(2,1)} copy(bf16[4,16,96,2048]{3,2,0,1:T(8,128)(2,1)} %convert_bitcast_fusion.1) | data formatting | bytes 50331648 | tf_op jit(solution)/shard_map/convert_element_type | solution.py:614
  1000.9 16.9 %convolution_convert_fusion.1 = bf16[4,256,2048]{2,1,0:T(8,128)(2,1)} fusion(bf16[4,1536,256]{2,1,0:T(8,128)(2,1)S(1)} %copy-done.11, bf16[4,1536,2048]{2,1,0:T(8,128)(2,1)} %bitcast.166), kind=kOutput, calls=%fused_computation.27 | convolution fusion | flops 6444548096 | bytes 32505856 | tf_op jit(solution)/shard_map/emf,emd->efd/dot_general | solution.py:513
  1018.0 1.3 fusion.46
  1019.4 5.9 collective-permute-done.3
  1025.3 19.0 %convert_add_fusion.1 = f32[4,256,2048]{2,1,0:T(8,128)} fusion(bf16[4,256,2048]{2,1,0:T(8,128)(2,1)} %collective-permute-done.3, bf16[4,1536,256]{2,1,0:T(8,128)(2,1)} %get-tuple-element.33, bf16[4,1536,2048]{2,1,0:T(8,128)(2,1)} %bitcast.167), kind=kOutput, calls=%fused_computation.9 | convolution fusion | flops 6446645248 | bytes 40894464 | tf_op jit(solution)/shard_map/emf,emd->efd/dot_general | solution.py:513
  1044.3 207.2 %plane_reduce.3 = f32[256,2048]{1,0:T(8,128)} custom-call(bf16[4,2,2,256,2048]{4,3,2,1,0:T(8,128)(2,1)} %bitcast.160), custom_call_target="tpu_custom_call" | custom-call | tf_op jit(solution)/shard_map/plane_reduce/pallas_call | solution.py:292
  1251.5 23.9 %convert_add_fusion = f32[4,2048,512]{1,2,0:T(8,128)} fusion(bf16[4,2048,512]{1,2,0:T(8,128)(2,1)} %collective-permute-done.2, bf16[4,1536,2048]{2,1,0:T(8,128)(2,1)} %bitcast.165, bf16[4,1536,512]{2,1,0:T(8,128)(2,1)} %get-tuple-element.43), kind=kOutput, calls=%fused_computation.3 | convolution fusion | flops 12893290496 | bytes 56623104 | tf_op jit(solution)/shard_map/emd,emf->edf/dot_general | solution.py:513
  1275.4 25.0 %copy.90 = f32[4,2048,2,256]{3,2,1,0:T(2,128)} copy(f32[4,2048,2,256]{1,3,2,0:T(8,128)} %bitcast.169) | data formatting | bytes 33554432
  1300.4 1.8 convert_element_type.134
  1302.2 2.1 fusion.27
  1304.9 29.3 %spread.5 = f32[32,34,128]{2,1,0:T(8,128)} custom-call(f32[34,128]{1,0:T(8,128)} %maximum_bitcast_fusion.v_ref), custom_call_target="tpu_custom_call" | custom-call | tf_op jit(solution)/shard_map/spread/pallas_call | solution.py:107
  1334.2 1.1 reduce_sum.163
  1336.5 6.3 fusion.25
  1342.9 2.5 convert_bitcast_fusion.2
  1345.4 1.7 copy.109
  (176 shorter events, 13.4 us)
Async XLA Ops:
  8.0 78.7 %copy-start = (bf16[512,2048]{1,0:T(8,128)(2,1)S(1)}, bf16[512,2048]{1,0:T(8,128)(2,1)}, u32[]{:S(2)}) copy-start(bf16[512,2048]{1,0:T(8,128)(2,1)} %param.20) | copy-start | bytes 6291460
  8.0 7.5 copy-start.50
  8.0 7.5 copy-start.49
  8.0 39.6 %all-gather.5.cloned.1.call-start = ((), (), s32[]{:S(2)}) async-start(), calls=%async_computation.4 | async-start | bytes 5242880 | tf_op jit(solution)/shard_map/all_gather | solution.py:521
  8.8 129.9 %reduce-scatter.5.cloned.1.call-start = ((), (), s32[]{:S(2)}) async-start(), calls=%async_computation.5 | async-start | bytes 5242880 | tf_op jit(solution)/shard_map/reduce_scatter | solution.py:525
  9.5 51.0 %copy-start.26 = (f32[2048]{0:T(1024)}, f32[2048]{0:T(1024)S(1)}, u32[]{:S(2)}) copy-start(f32[2048]{0:T(1024)S(1)} %convert_element_type.109) | copy-start | bytes 24580
  10.4 40.4 %copy-start.28 = (s32[1024]{0:T(1024)}, s32[1024]{0:T(1024)S(1)}, u32[]{:S(2)}) copy-start(s32[1024]{0:T(1024)S(1)} %convert_reduce_fusion) | copy-start | bytes 12292
  47.6 3.4 copy-start.9
  47.6 9.2 slice-start
  50.9 9.6 copy-start.44
  51.1 5.7 slice-start.1
  92.3 0.7 copy-start.43
  92.3 46.4 %copy-start.1 = (bf16[256,2048]{1,0:T(8,128)(2,1)S(1)}, bf16[256,2048]{1,0:T(8,128)(2,1)}, u32[]{:S(2)}) copy-start(bf16[256,2048]{1,0:T(8,128)(2,1)} %param.13) | copy-start | bytes 3145732
  92.4 195.6 %all-gather.9.cloned.1.call-start = ((), (), s32[]{:S(2)}) async-start(), calls=%async_computation.7 | async-start | bytes 17825792 | tf_op jit(solution)/shard_map/all_gather | solution.py:521
  92.9 387.2 %all-gather.7.cloned.1.call-start = ((), (), s32[]{:S(2)}) async-start(), calls=%async_computation.6 | async-start | bytes 17825792 | tf_op jit(solution)/shard_map/all_gather | solution.py:521
  93.0 65.2 %copy-start.23 = (f32[2048]{0:T(1024)}, f32[2048]{0:T(1024)S(1)}, u32[]{:S(2)}) copy-start(f32[2048]{0:T(1024)S(1)} %convert_element_type.118) | copy-start | bytes 24580
  143.5 30.3 %copy-start.30 = (s32[256,8]{0,1:T(8,128)S(1)}, s32[256,8]{0,1:T(8,128)}, u32[]{:S(2)}) copy-start(s32[256,8]{0,1:T(8,128)} %param.14) | copy-start | bytes 24580
  143.5 743.4 %all-gather.11.cloned.1.call-start = ((), (), s32[]{:S(2)}) async-start(), calls=%async_computation.8 | async-start | bytes 5242880 | tf_op jit(solution)/shard_map/all_gather | solution.py:521
  143.6 176.7 %collective-permute-start = (bf16[4,256,2048]{2,1,0:T(8,128)(2,1)}, bf16[4,256,2048]{2,1,0:T(8,128)(2,1)}, u32[]{:S(2)}, u32[]{:S(2)}) collective-permute-start(bf16[4,256,2048]{2,1,0:T(8,128)(2,1)} %param.24), channel_id=1, source_target_pairs={{0,1},{1,0},{2,3},{3,2},{4,5},{5,4},{6,7},{7,6},{8,9},{9,8},{10,11... | collective-permute-start | bytes 12582920 | tf_op jit(solution)/shard_map/ppermute | solution.py:517
  158.3 15.6 %copy-start.6 = (bf16[256,2048]{1,0:T(8,128)(2,1)S(1)}, bf16[256,2048]{1,0:T(8,128)(2,1)}, u32[]{:S(2)}) copy-start(bf16[256,2048]{1,0:T(8,128)(2,1)} %multiply_convert_fusion) | copy-start | bytes 3145732
  158.3 15.6 %copy-start.12 = (bf16[2048,32]{0,1:T(8,128)(2,1)S(1)}, bf16[2048,32]{0,1:T(8,128)(2,1)}, u32[]{:S(2)}) copy-start(bf16[2048,32]{0,1:T(8,128)(2,1)} %param.22) | copy-start | bytes 393220
  158.3 379.6 %collective-permute-start.1 = (bf16[4,2048,512]{2,1,0:T(8,128)(2,1)}, bf16[4,2048,512]{2,1,0:T(8,128)(2,1)}, u32[]{:S(2)}, u32[]{:S(2)}) collective-permute-start(bf16[4,2048,512]{2,1,0:T(8,128)(2,1)} %reshape.167.w0_ref), channel_id=1, source_target_pairs={{0,1},{1,0},{2,3},{3,2},{4,5},{5,4},{6,7},{7,6},{8,9},{9,8},{10,11... | collective-permute-start | bytes 25165832 | tf_op jit(solution)/shard_map/ppermute | solution.py:517
  617.6 183.5 %copy-start.18 = (f32[32,256]{1,0:T(8,128)}, f32[32,256]{1,0:T(8,128)S(1)}, u32[]{:S(2)}) copy-start(f32[32,256]{1,0:T(8,128)S(1)} %reshape.174) | copy-start | bytes 98308
  642.6 158.4 %copy-start.16 = (f32[256,32]{0,1:T(8,128)S(1)}, f32[256,32]{0,1:T(8,128)}, u32[]{:S(2)}) copy-start(f32[256,32]{0,1:T(8,128)} %copy-done.15) | copy-start | bytes 98308
  642.6 158.4 %copy-start.21 = (pred[256,32]{0,1:T(8,128)(4,1)S(1)}, pred[256,32]{0,1:T(8,128)(4,1)}, u32[]{:S(2)}) copy-start(pred[256,32]{0,1:T(8,128)(4,1)} %copy-done.20) | copy-start | bytes 24580
  642.6 158.4 %copy-start.32 = (f32[256]{0:T(256)S(1)}, f32[256]{0:T(256)}, u32[]{:S(2)}) copy-start(f32[256]{0:T(256)} %copy-done.31) | copy-start | bytes 3076
  642.6 158.4 %copy-start.37 = (f32[256]{0:T(256)S(1)}, f32[256]{0:T(256)}, u32[]{:S(2)}) copy-start(f32[256]{0:T(256)} %fusion.45) | copy-start | bytes 3076
  642.6 158.5 %copy-start.2 = (bf16[256,2048]{1,0:T(8,128)(2,1)S(1)}, bf16[256,2048]{1,0:T(8,128)(2,1)}, u32[]{:S(2)}) copy-start(bf16[256,2048]{1,0:T(8,128)(2,1)} %param.13) | copy-start | bytes 3145732
  642.6 158.5 %copy-start.24 = (f32[2048]{0:T(1024)S(1)}, f32[2048]{0:T(1024)}, u32[]{:S(2)}) copy-start(f32[2048]{0:T(1024)} %copy-done.23) | copy-start | bytes 24580
  642.6 158.5 %copy-start.35 = (f32[256]{0:T(256)S(1)}, f32[256]{0:T(256)}, u32[]{:S(2)}) copy-start(f32[256]{0:T(256)} %copy-done.34) | copy-start | bytes 3076
  801.0 6.0 copy-start.4
  801.0 6.0 copy-start.8
  801.1 7.7 copy-start.39
  805.7 1.4 copy-start.5
  805.7 27.1 %copy-start.41 = (f32[256]{0:T(256)}, f32[256]{0:T(256)S(1)}, u32[]{:S(2)}) copy-start(f32[256]{0:T(256)S(1)} %broadcast_multiply_fusion.1) | copy-start | bytes 3076
  808.9 491.5 %reduce-scatter.11.cloned.1.call-start = ((), (), s32[]{:S(2)}) async-start(), calls=%async_computation.11 | async-start | bytes 2359296 | tf_op jit(solution)/shard_map/reduce_scatter | solution.py:525
  861.9 25.0 %copy-start.13 = (bf16[1024,512]{1,0:T(8,128)(2,1)S(1)}, bf16[1024,512]{1,0:T(8,128)(2,1)}, u32[]{:S(2)}) copy-start(bf16[1024,512]{1,0:T(8,128)(2,1)} %attention.2) | copy-start | bytes 3145732
  892.8 409.4 %reduce-scatter.7.cloned.1.call-start = ((), (), s32[]{:S(2)}) async-start(), calls=%async_computation.9 | async-start | bytes 5242880 | tf_op jit(solution)/shard_map/reduce_scatter | solution.py:525
  928.8 4.4 copy-start.51
  943.5 0.7 copy-start.27
  943.5 0.7 copy-start.45
  943.5 6.0 copy-start.52
  943.5 399.4 %reduce-scatter.9.cloned.1.call-start = ((), (), s32[]{:S(2)}) async-start(), calls=%async_computation.10 | async-start | bytes 7077888 | tf_op jit(solution)/shard_map/reduce_scatter | solution.py:525
  944.2 5.4 copy-start.10
  949.5 2.7 copy-start.14
  958.1 387.3 %all-reduce.2.cloned.1.call-start = ((), (), s32[]{:S(2)}) async-start(), calls=%async_computation.12 | async-start | bytes 524288 | tf_op jit(solution)/shard_map/psum | solution.py:700
  978.6 22.2 %copy-start.11 = (bf16[4,1536,256]{2,1,0:T(8,128)(2,1)S(1)}, bf16[4,1536,256]{2,1,0:T(8,128)(2,1)}, u32[]{:S(2)}) copy-start(bf16[4,1536,256]{2,1,0:T(8,128)(2,1)} %get-tuple-element.34) | copy-start | bytes 9437188
  978.6 272.9 %collective-permute-start.2 = (bf16[4,2048,512]{1,2,0:T(8,128)(2,1)}, bf16[4,2048,512]{1,2,0:T(8,128)(2,1)}, u32[]{:S(2)}, u32[]{:S(2)}) collective-permute-start(bf16[4,2048,512]{1,2,0:T(8,128)(2,1)} %convolution_convert_fusion), channel_id=1, source_target_pairs={{0,1},{1,0},{2,3},{3,2},{4,5},{5,4},{6,7},{7,6},{8,9},{9,8},{10,11... | collective-permute-start | bytes 25165832 | tf_op jit(solution)/shard_map/ppermute | solution.py:517
  1000.8 17.2 %copy-start.7 = (bf16[256,2048]{1,0:T(8,128)(2,1)S(1)}, bf16[256,2048]{1,0:T(8,128)(2,1)}, u32[]{:S(2)}) copy-start(bf16[256,2048]{1,0:T(8,128)(2,1)} %multiply_convert_fusion) | copy-start | bytes 3145732
  1000.8 17.2 %copy-start.17 = (f32[256,32]{0,1:T(8,128)S(1)}, f32[256,32]{0,1:T(8,128)}, u32[]{:S(2)}) copy-start(f32[256,32]{0,1:T(8,128)} %copy-done.15) | copy-start | bytes 98308
  1000.8 17.2 %copy-start.19 = (f32[32,256]{1,0:T(8,128)S(1)}, f32[32,256]{1,0:T(8,128)}, u32[]{:S(2)}) copy-start(f32[32,256]{1,0:T(8,128)} %copy-done.18) | copy-start | bytes 98308
  1000.8 17.2 %copy-start.22 = (pred[256,32]{0,1:T(8,128)(4,1)S(1)}, pred[256,32]{0,1:T(8,128)(4,1)}, u32[]{:S(2)}) copy-start(pred[256,32]{0,1:T(8,128)(4,1)} %copy-done.20) | copy-start | bytes 24580
  1000.8 17.2 %copy-start.33 = (f32[256]{0:T(256)S(1)}, f32[256]{0:T(256)}, u32[]{:S(2)}) copy-start(f32[256]{0:T(256)} %copy-done.31) | copy-start | bytes 3076
  1000.8 17.2 %copy-start.38 = (f32[256]{0:T(256)S(1)}, f32[256]{0:T(256)}, u32[]{:S(2)}) copy-start(f32[256]{0:T(256)} %fusion.45) | copy-start | bytes 3076
  1000.8 17.2 %copy-start.40 = (f32[256]{0:T(256)S(1)}, f32[256]{0:T(256)}, u32[]{:S(2)}) copy-start(f32[256]{0:T(256)} %copy-done.39) | copy-start | bytes 3076
  1000.8 18.5 %copy-start.46 = (f32[256]{0:T(256)S(1)}, f32[256]{0:T(256)}, u32[]{:S(2)}) copy-start(f32[256]{0:T(256)} %get-tuple-element.93) | copy-start | bytes 3076
  1017.8 7.5 collective-permute-start.3
  1275.3 26.9 %copy-start.3 = (bf16[256,2048]{1,0:T(8,128)(2,1)S(1)}, bf16[256,2048]{1,0:T(8,128)(2,1)}, u32[]{:S(2)}) copy-start(bf16[256,2048]{1,0:T(8,128)(2,1)} %param.13) | copy-start | bytes 3145732
  1275.3 28.9 %copy-start.29 = (f32[2048]{0:T(1024)S(1)}, f32[2048]{0:T(1024)}, u32[]{:S(2)}) copy-start(f32[2048]{0:T(1024)} %get-tuple-element.89) | copy-start | bytes 24580
  1275.3 28.9 %copy-start.47 = (f32[1,128]{1,0:T(1,128)S(1)}, f32[1,128]{1,0:T(1,128)}, u32[]{:S(2)}) copy-start(f32[1,128]{1,0:T(1,128)} %get-tuple-element.41) | copy-start | bytes 1540
  1275.4 28.9 %copy-start.48 = (f32[1,128]{1,0:T(1,128)S(1)}, f32[1,128]{1,0:T(1,128)}, u32[]{:S(2)}) copy-start(f32[1,128]{1,0:T(1,128)} %get-tuple-element.42) | copy-start | bytes 1540
  1300.4 36.1 %copy-start.25 = (f32[2048]{0:T(1024)S(1)}, f32[2048]{0:T(1024)}, u32[]{:S(2)}) copy-start(f32[2048]{0:T(1024)} %copy-done.23) | copy-start | bytes 24580
  1300.4 36.1 %copy-start.36 = (f32[256]{0:T(256)S(1)}, f32[256]{0:T(256)}, u32[]{:S(2)}) copy-start(f32[256]{0:T(256)} %copy-done.34) | copy-start | bytes 3076
  1300.4 36.1 %copy-start.42 = (f32[256]{0:T(256)S(1)}, f32[256]{0:T(256)}, u32[]{:S(2)}) copy-start(f32[256]{0:T(256)} %copy-done.41) | copy-start | bytes 3076
  (4 other events, 2.3 us)
Sparse Core Ops, SparseCore 0:
  10.4 37.1 all-gather.4
  92.5 46.1 reduce-scatter.4
  809.0 46.3 all-gather.10
  892.9 80.3 reduce-scatter.10
  975.7 44.8 reduce-scatter.6
  1024.1 141.9 reduce-scatter.8
  1172.1 125.9 all-reduce.1
Sparse Core Ops, SparseCore 1:
  95.6 192.3 all-gather.8
  291.2 188.9 all-gather.6

commit v4 on v3

--- a/solution.py
+++ b/solution.py
@@ -306,6 +306,89 @@
         ),
         name="plane_reduce",
     )(parts.reshape(depth, 2, 2, rows, columns))
+
+
+def group_kernel(pieces, p_ref, out_ref, near, far, kept, got, own_sem, s1, r1, s2, r2, s3, r3):
+    x, core = lax.axis_index("x"), lax.axis_index("core")
+    partner, across = {"core": 1 - core}, {"x": 1 - x}
+    greet(partner)
+    greet(across)
+    pl.semaphore_wait(pltpu.get_barrier_semaphore(), 2)
+    step = out_ref.shape[0] // pieces
+
+    def at(piece):
+        return pl.ds(piece * step, step)
+
+    def hand_over(piece):
+        return remote(
+            p_ref.at[1 - x, 1 - core, at(piece), :],
+            near.at[at(piece), :],
+            s1.at[piece],
+            r1.at[piece],
+            partner,
+        )
+
+    def send_across(piece):
+        return remote(
+            far.at[at(piece), :], got.at[at(piece), :], s2.at[piece], r2.at[piece], across
+        )
+
+    stay = remote(p_ref.at[x, 1 - core], kept.at[0], s3, r3, partner)
+    loads = (
+        pltpu.make_async_copy(p_ref.at[1 - x, core], far, own_sem.at[0]),
+        pltpu.make_async_copy(p_ref.at[x, core], kept.at[1], own_sem.at[1]),
+    )
+    loads[0].start()
+    for piece in range(pieces):
+        hand_over(piece).start()
+    stay.start()
+    loads[1].start()
+    loads[0].wait()
+    for piece in range(pieces):
+        hand_over(piece).wait()
+        mine = far.at[at(piece), :]
+        add_into(mine, [mine, near.at[at(piece), :]])
+        send_across(piece).start()
+    loads[1].wait()
+    stay.wait()
+    for piece in range(pieces):
+        send_across(piece).wait()
+        rows = at(piece)
+        add_into(
+            out_ref.at[rows, :], [kept.at[0, rows, :], kept.at[1, rows, :], got.at[rows, :]]
+        )
+
+
+def group_reduce(parts, collective_id):
+    if lax.axis_size("x") != 2:
+        return scatter(parts, GROUP).astype(F32)
+    rows, columns = parts.shape[0] // 4, parts.shape[1]
+    pieces = 4
+
+    def sems(*lead):
+        return pltpu.SemaphoreType.DMA(lead)
+
+    return pl.pallas_call(
+        functools.partial(group_kernel, pieces),
+        out_shape=jax.ShapeDtypeStruct((rows, columns), F32),
+        in_specs=[pl.BlockSpec(memory_space=pl.ANY)],
+        out_specs=pl.BlockSpec(memory_space=pltpu.VMEM),
+        scratch_shapes=[
+            pltpu.VMEM((rows, columns), BF16),
+            pltpu.VMEM((rows, columns), BF16),
+            pltpu.VMEM((2, rows, columns), BF16),
+            pltpu.VMEM((rows, columns), BF16),
+            sems(2),
+            sems(pieces),
+            sems(pieces),
+            sems(pieces),
+            sems(pieces),
+            pltpu.SemaphoreType.DMA,
+            pltpu.SemaphoreType.DMA,
+        ],
+        compiler_params=pltpu.CompilerParams(collective_id=collective_id, has_side_effects=True),
+        name="group_reduce",
+    )(parts.reshape(2, 2, rows, columns))
 
 
 def turn(value, cosine, sine):
@@ -422,21 +505,133 @@
         cost_estimate=pl.CostEstimate(flops=flops, bytes_accessed=moved, transcendentals=0))
 
 
-def combine_kernel(pick_ref, value_ref, out_ref):
-    local, _, capacity, width = value_ref.shape
-    out_ref[0] = dot_tn(pick_ref[0], value_ref[...].reshape(local*capacity, width)).astype(BF16)
-
-
-def combine(pick, value):
+def pick_rows_of(pick, value, out_ref, index):
+    local, _, capacity, _ = out_ref.shape
+    rows = dot_nn(pick, value).astype(BF16)
+    for expert_at in range(local):
+        out_ref[expert_at, index] = rows[expert_at * capacity : (expert_at + 1) * capacity]
+
+
+def dispatch_kernel(pick_ref, value_ref, out_ref):
+    for index in range(pick_ref.shape[0]):
+        pick_rows_of(pick_ref[index], value_ref[index], out_ref, index)
+
+
+def route_kernel(pick_ref, value_ref, mask_ref, router_ref, select_ref, out_ref, prob_ref):
+    local, _, capacity, _ = out_ref.shape
+    for index in range(pick_ref.shape[0]):
+        pick, value, mask = pick_ref[index], value_ref[index], mask_ref[index] > 0
+        pick_rows_of(pick, value, out_ref, index)
+        kept = jnp.where(mask, dot_nn(value, router_ref[...]), MASKED)
+        lifted = jnp.exp(kept - jnp.max(kept, axis=-1, keepdims=True))
+        lifted = jnp.where(mask, lifted, 0.0)
+        rest = lifted / jnp.sum(lifted, axis=-1, keepdims=True)
+        picked = jnp.zeros((pick.shape[0], rest.shape[1]), F32)
+        for _ in range(3):
+            piece = rest.astype(BF16)
+            rest = rest - piece.astype(F32)
+            picked = picked + dot_nn(pick, piece)
+        prob = jnp.sum(picked * select_ref[...], axis=-1, keepdims=True)
+        for expert_at in range(local):
+            prob_ref[expert_at, index] = prob[expert_at * capacity : (expert_at + 1) * capacity]
+
+
+def dispatch(pick, value, local, routing=None, group=2):
+    blocks, picked, rows = pick.shape
+    width = value.shape[-1]
+    capacity = picked // local
+
+    def block(*shape):
+        return pl.BlockSpec((group,) + shape, lambda b: (b, 0, 0))
+
+    def result(columns):
+        return pl.BlockSpec((local, group, capacity, columns), lambda b: (0, b, 0, 0))
+
+    def shape(columns, kind):
+        return jax.ShapeDtypeStruct((local, blocks, capacity, columns), kind)
+
+    ins, specs = [pick, value], [block(picked, rows), block(rows, width)]
+    shapes, outs = [shape(width, BF16)], [result(width)]
+    if routing is not None:
+        mask, router, select = routing
+        ins += [mask, router, select]
+        specs += [block(rows, mask.shape[-1])]
+        specs += [pl.BlockSpec(t.shape, lambda b: (0, 0)) for t in (router, select)]
+        shapes += [shape(1, F32)]
+        outs += [result(1)]
+    return pl.pallas_call(
+        dispatch_kernel if routing is None else route_kernel,
+        grid=(blocks // group,),
+        out_shape=shapes,
+        in_specs=specs,
+        out_specs=outs,
+        name="dispatch",
+        **params(2 * blocks * picked * rows * width, 2 * blocks * width * (picked + rows)),
+    )(*ins)
+
+
+def combine_kernel(pick_ref, value_ref, *refs):
+    local, group, capacity, width = value_ref.shape
+    out_ref = refs[-2] if len(refs) == 3 else refs[0]
+    for index in range(group):
+        pick = pick_ref[index]
+        if group == 1:
+            value = value_ref[...].reshape(local * capacity, width)
+        else:
+            value = jnp.concatenate([value_ref[e, index] for e in range(local)], axis=0)
+        out_ref[index] = dot_tn(pick, value).astype(BF16)
+        if len(refs) == 3:
+            for e in range(local):
+                part = pick[e * capacity : (e + 1) * capacity].astype(F32)
+                refs[2][index, e : e + 1, :] = jnp.sum(
+                    part * refs[0][e, index], axis=0, keepdims=True
+                )
+
+
+def combine(pick, value, dots=None, group=2):
     blocks, picked, rows = pick.shape
     local, _, capacity, width = value.shape
+
+    def rows_of(columns):
+        return pl.BlockSpec((local, group, capacity, columns), lambda b: (0, b, 0, 0))
+
+    ins, specs = [pick, value], [pl.BlockSpec((group, picked, rows), lambda b: (b, 0, 0)), rows_of(width)]
+    shapes = [jax.ShapeDtypeStruct((blocks, rows, width), BF16)]
+    outs = [pl.BlockSpec((group, rows, width), lambda b: (b, 0, 0))]
+    if dots is not None:
+        ins += [dots]
+        specs += [rows_of(1)]
+        shapes += [jax.ShapeDtypeStruct((blocks, local, rows), F32)]
+        outs += [pl.BlockSpec((group, local, rows), lambda b: (b, 0, 0))]
     return pl.pallas_call(
-        combine_kernel, grid=(blocks,),
-        out_shape=jax.ShapeDtypeStruct((blocks, rows, width), BF16),
-        in_specs=[pl.BlockSpec((1, picked, rows), lambda b: (b, 0, 0)), pl.BlockSpec((local, 1, capacity, width), lambda b: (0, b, 0, 0))],
-        out_specs=pl.BlockSpec((1, rows, width), lambda b: (b, 0, 0)),
-        name="combine", **params(2*blocks*picked*rows*width, 2*blocks*width*(picked+rows)),
-    )(pick, value)
+        combine_kernel,
+        grid=(blocks // group,),
+        out_shape=shapes,
+        in_specs=specs,
+        out_specs=outs,
+        name="combine",
+        **params(2 * blocks * picked * rows * width, 2 * blocks * width * (picked + rows)),
+    )(*ins)
+
+
+def down_kernel(h0_ref, h1_ref, w0_ref, w1_ref, out_ref):
+    out_ref[0] = (dot_nn(h0_ref[0], w0_ref[0]) + dot_nn(h1_ref[0], w1_ref[0])).astype(BF16)
+
+
+def down_rows(h0, h1, w0, w1, step):
+    local, count, hidden = h0.shape
+    width = w0.shape[-1]
+    rows = pl.BlockSpec((1, step, hidden), lambda e, i: (e, i, 0))
+    weight = pl.BlockSpec((1, hidden, width), lambda e, i: (e, 0, 0))
+    return pl.pallas_call(
+        down_kernel,
+        grid=(local, count // step),
+        out_shape=jax.ShapeDtypeStruct((local, count, width), BF16),
+        in_specs=[rows, rows, weight, weight],
+        out_specs=pl.BlockSpec((1, step, width), lambda e, i: (e, i, 0)),
+        name="down_rows",
+        **params(4 * local * count * hidden * width, 2 * local * (count + 2 * hidden) * width),
+    )(h0, h1, w0, w1)
 
 
 def expert_kernel(x_ref, w0_ref, w1_ref, u0_ref, u1_ref, pr_ref, gx_ref, dots_ref, *outs):
@@ -588,8 +783,9 @@
     (attn_vals,) = attention_call(
         attend_kernel, heads, head_dim, seq_len, raw, tables, (True,), 4 * seq_len**2 * qkv_local
     )
-    attn_out = scatter(jnp.dot(attn_vals, w_out, preferred_element_type=F32).astype(BF16), GROUP)
-    middle = inputs + attn_out.astype(F32)
+    attn_part = jnp.dot(attn_vals, w_out, preferred_element_type=F32).astype(BF16)
+    attn_out = group_reduce(attn_part, 7)
+    middle = inputs + attn_out
     h_two = norm_rows(middle, gain_two).astype(BF16)
 
     g_plane = g_flat.reshape(blocks, rows, width)
@@ -611,35 +807,42 @@
     pick_rows = pick.reshape(blocks, local * capacity, rows)
     count = blocks * capacity
 
-    g_rows = einsum("bect,btd->ebcd", pick, g_plane).astype(BF16)
-    back_own = einsum("ebcd,efd->ebcf", g_rows, expert_down).reshape(local, count, -1)
-    back_other = einsum("ebcd,efd->ebcf", g_rows, down_other).reshape(local, count, -1)
+    (g_rows,) = dispatch(pick_rows, g_plane, local, group=4)
+    g_rows = g_rows.reshape(local, count, width)
+    back_own = einsum("emd,efd->emf", g_rows, expert_down)
+    back_other = einsum("emd,efd->emf", g_rows, down_other)
     h_flat, back_own, back_other = lax.optimization_barrier((h_flat, back_own, back_other))
-    h_plane = h_flat.reshape(blocks, rows, width)
-    h_rows = einsum("bect,btd->ebcd", pick, h_plane).astype(BF16)
-    logits_plane = jnp.dot(h_flat, w_router, preferred_element_type=F32)
-    probs_plane = masked_softmax(logits_plane, mask_plane)
-    probs_here = lax.dynamic_slice_in_dim(probs_plane, first, local, axis=1)
-    probs_here = probs_here.reshape(blocks, rows, local).transpose(0, 2, 1)
-    prob_rows = jnp.sum(jnp.where(picks, probs_here[:, :, None, :], 0.0), axis=-1)
-    prob_rows = prob_rows.transpose(1, 0, 2).reshape(local, count, 1)
+    select_column = first + jnp.arange(local * capacity, dtype=jnp.int32) // capacity
+    select = select_column[:, None] == jnp.arange(experts_all, dtype=jnp.int32)[None, :]
+    routing = (
+        mask_plane.astype(F32).reshape(blocks, rows, experts_all),
+        w_router,
+        select.astype(F32),
+    )
+    h_rows, prob_rows = dispatch(
+        pick_rows, h_flat.reshape(blocks, rows, width), local, routing, group=2
+    )
     h_rows = h_rows.reshape(local, count, width)
-    g_rows = g_rows.reshape(local, count, width)
+    prob_rows = prob_rows.reshape(local, count, 1)
     back_rows, dot_rows, weighted_own, weighted_other, ggu_own, ggu_other = expert(
         h_rows, pair_own, pair_other, back_own, back_other, prob_rows, min(384, count)
     )
-    dot_rows = dot_rows.reshape(local, blocks, capacity).transpose(1, 0, 2)
-    dots_token = jnp.sum(jnp.where(picks, dot_rows[..., None], 0.0), axis=2)
+    back_part, dots_token = combine(
+        pick_rows,
+        back_rows.reshape(local, blocks, capacity, width),
+        dot_rows.reshape(local, blocks, capacity, 1),
+        group=2,
+    )
     grad_probs = spread(dots_token, PLANE, 2, True)
     grad_probs = jnp.sum(grad_probs.reshape(ep_count, x_count, local, rows), axis=1)
     grad_probs = grad_probs.reshape(experts_all, rows).T
-    back_part = combine(pick_rows, back_rows.reshape(local, blocks, capacity, width))
     back_sum = plane_reduce(back_part, 3)
-    out_rows = (
-        einsum("emf,efd->emd", weighted_own, expert_down)
-        + einsum("emf,efd->emd", weighted_other, down_other)
-    ).astype(BF16)
-    out_part = combine(pick_rows, out_rows.reshape(local, blocks, capacity, width))
+    out_rows = down_rows(
+        weighted_own, weighted_other, expert_down, down_other, min(384, count)
+    )
+    (out_part,) = combine(
+        pick_rows, out_rows.reshape(local, blocks, capacity, width), group=4
+    )
 
     grad_pair_own = einsum("emd,emf->edf", h_rows, ggu_own)
     grad_pair_other = einsum("emd,emf->edf", h_rows, ggu_other)
@@ -653,7 +856,9 @@
     probs_own = masked_softmax(jnp.dot(h_two, w_router, preferred_element_type=F32), mask_own)
     inner = jnp.sum(probs_own * grad_probs, axis=-1, keepdims=True)
     grad_logits = probs_own * (grad_probs - inner)
-    grad_router = jnp.dot(h_two.astype(F32).T, grad_logits, precision=HIGH)
+    grad_router = lax.dot_general(
+        grad_logits, h_two.astype(F32), (((0,), (0,)), ((), ())), precision=HIGH
+    )
     grad_h_two = back_sum + jnp.dot(
         grad_logits, w_router.astype(F32).T, precision=HIGH
     )
@@ -695,12 +900,21 @@
     grad_input = grad_mid + grad_in_norm
     dense_qkv = scatter(grad_wqkv, "ep", 1).astype(F32)
     dense_out = scatter(grad_wout.astype(BF16), "ep", 1).astype(F32)
-    out_part, grad_proj = lax.optimization_barrier((out_part, grad_proj))
+    devices = blocks * 2
+    small = jnp.concatenate(
+        [grad_router.reshape(-1), grad_gain_one, grad_gain_two, grad_q_gain[0], grad_k_gain[0]]
+    )
+    length = small.shape[0]
+    padded = -(-length // (devices * 1024)) * devices * 1024
+    small = jnp.pad(small, (0, padded - length)).reshape(devices, -1, 128)
+    small = jnp.sum(spread(small, ALL, 5, True), axis=0)
+    small = spread(small, ALL, 6).reshape(-1)
+    out_part, small = lax.optimization_barrier((out_part, small))
     output = (middle + plane_reduce(out_part, 4)).astype(BF16)
-    grad_router = lax.psum(grad_router, ALL)
-    small = jnp.concatenate([grad_gain_one, grad_gain_two, grad_q_gain[0], grad_k_gain[0]])
-    small = jnp.sum(spread(small.reshape(-1, 128), ALL, 5), axis=0).reshape(-1)
-    gains = jnp.split(small, (width, 2 * width, 2 * width + head_dim))
+    cuts = (experts_all * width, width, width, head_dim, head_dim)
+    starts = [sum(cuts[:index]) for index in range(5)]
+    router_sum, *gains = (small[at : at + cut] for at, cut in zip(starts, cuts))
+    grad_router = router_sum.reshape(experts_all, width).T
     return (
         output,
         grad_input,

time: 1370 us -> 1240 us (0.905)
  matrix products: 272 us -> 172 us
  Pallas kernels: 581 us -> 677 us
  waiting for transfers between devices: 342 us -> 264 us
  local copies, waits for them, and re-layouts: 95.1 us -> 51 us
    pallas_call x2 -> x6, Pallas kernels: 50 us -> 174 us  [the longest x2 56.5 us: dispatch(): pl.pallas_call(dispatch_kernel if routing is None else route_kernel, grid...]
    dot_general x11 -> x7, matrix products: 199 us -> 111 us  [einsum(): return jnp.einsum(spec, left, right, preferred_element_type=F32)]
    reduce_scatter x4 -> x3, waiting for transfers between devices: 45.7 us -> 0.02 us  [scatter(): return lax.psum_scatter(value, axes, scatter_dimension=dim, tiled=True)]
    convert_element_type x2 -> x1, local copies, waits for them, and re-layouts: 43.2 us -> 3 us  [per_device(): mask_plane.astype(F32).reshape(blocks, rows, experts_all)]
    pallas_call x2, Pallas kernels: 366 us -> 325 us  [plane_reduce(): pl.pallas_call(functools.partial(reduce_kernel, depth, half), out_shape=j...]
    all_gather x4, waiting for transfers between devices: 289 us -> 256 us  [gather(): return lax.all_gather(value, axes, axis=0, tiled=True)]
    pallas_call x3 -> x4, Pallas kernels: 48.9 us -> 61.1 us  [spread(): pl.pallas_call(functools.partial(spread_kernel, axes, counts, own_slices)...]
    unnamed x113 -> x88, local copies, waits for them, and re-layouts: 30 us -> 29.7 us
  transfers between devices with their start and end apart: 13 -> 11, of which waited for: 5 -> 5; matrix products, arithmetic and copies ran while one was open for 27% -> 20% of each run, Pallas kernels for 22% -> 35%
where the time goes in v4:
time: 1240 us; the launch traced here: 1220 us
  Pallas kernels  677 us (55%)
  waiting for transfers between devices  264 us (21%)
  matrix products  172 us (14%)
  local copies, waits for them, and re-layouts  51 us (4%)
  other arithmetic  39.7 us (3%)
  between operations  15.1 us (1%)
    pallas_call x2, Pallas kernels, plane_reduce(): pl.pallas_call(functools.partial(reduce_kernel, depth, half), out_shape=j...  325 us
    all_gather x4, waiting for transfers between devices, gather(): return lax.all_gather(value, axes, axis=0, tiled=True)  256 us
    dot_general x7, matrix products, einsum(): return jnp.einsum(spec, left, right, preferred_element_type=F32)  111 us
    pallas_call x1, Pallas kernels, expert(): pl.pallas_call(expert_kernel, grid=(local, count // step), out_shape=[s(w...  63.3 us
    pallas_call x4, Pallas kernels, spread(): pl.pallas_call(functools.partial(spread_kernel, axes, counts, own_slices)...  61.1 us
    pallas_call x2, Pallas kernels, dispatch(): pl.pallas_call(dispatch_kernel if routing is None else route_kernel, grid...  56.5 us
    pallas_call x2, Pallas kernels, attention_call(): pl.pallas_call(functools.partial(kernel, min(512, seq_len)), grid=(heads,...  53.1 us
    pallas_call x1, Pallas kernels, group_reduce(): pl.pallas_call(functools.partial(group_kernel, pieces), out_shape=jax.Sha...  51.5 us
  transfers between devices with their start and end apart: 11, of which 5 were waited for; matrix products, arithmetic and copies ran while one was open for 20% of the time, Pallas kernels for 35%

profile of v4, /device:TPU:0, one launch (start us, length us, event | category | flops | bytes accessed | tf_op | source)
XLA Modules:
  0.0 1220.1 jit_solution(4571897296062905577)
XLA Ops:
  9.4 0.8 reduce-window.4
  10.4 1.0 copy.49.dr_ref
  12.9 1.9 fusion.26
  14.8 1.3 pad_maximum_fusion.1
  16.6 30.2 %all-gather.5.cloned.1.call-done = bf16[1024,2048]{1,0:T(8,128)(2,1)} async-done(((bf16[256,2048]{1,0:T(8,128)(2,1)}), bf16[1024,2048]{1,0:T(8,128)(2,1)}) %all-gather.5.cloned.1.call-update) | async-done | bytes 4194320 | tf_op jit(solution)/shard_map/all_gather | solution.py:716
  46.8 3.2 fusion
  50.3 5.7 fusion.21.k_ref
  56.0 3.7 fusion.22.v_ref
  59.7 3.7 fusion.19.q_ref
  63.4 22.5 %attention.2 = bf16[1024,512]{1,0:T(8,128)(2,1)} custom-call(f32[1024,512]{1,0:T(8,128)} %fusion.19.q_ref, f32[1024,512]{1,0:T(8,128)} %fusion.21.k_ref, f32[1024,512]{1,0:T(8,128)} %fusion.22.v_ref, f32[1,128]{1,0:T(1,128)} %get-tuple-element.110.qg_ref, f32[1,128]{1,0:T(1,128)} %get-tuple-element.109.kg_ref, f32[1024,128]{1,0:T(8,128)} %get-tuple-element.107.cos_ref, ...), custom_call_target="tpu_custom_call" | custom-call | flops 2147483648 | bytes 8388608 | tf_op jit(solution)/shard_map/attention/pallas_call | solution.py:489
  85.9 5.8 convolution_convert_fusion.2
  91.7 51.5 %group_reduce.1 = f32[256,2048]{1,0:T(8,128)} custom-call(bf16[2,2,256,2048]{3,2,1,0:T(8,128)(2,1)} %bitcast.137), custom_call_target="tpu_custom_call" | custom-call | tf_op jit(solution)/shard_map/group_reduce/pallas_call | solution.py:371
  143.2 2.7 multiply_reduce_fusion.2
  145.9 1.3 copy-done.2
  147.2 1.2 multiply_convert_fusion
  148.5 14.3 %reshape.185.w0_ref = bf16[4,2048,512]{2,1,0:T(8,128)(2,1)} reshape(bf16[4,2048,2,256]{3,2,1,0:T(2,128)(2,1)} %param.23) | data formatting | bytes 16777216 | tf_op jit(solution)/shard_map/reshape | solution.py:796
  163.4 11.0 spread.4
  174.5 1.4 fusion.5
  175.9 0.8 convert_element_type.130
  177.1 3.0 copy.52
  180.1 1.1 copy.53.router_ref
  181.2 2.7 fusion.4.pick_ref
  184.0 0.8 fusion.25.select_ref
  185.2 79.1 %all-gather.9.cloned.1.call-done = bf16[4096,2048]{1,0:T(8,128)(2,1)} async-done(((bf16[256,2048]{1,0:T(8,128)(2,1)}), bf16[4096,2048]{1,0:T(8,128)(2,1)}) %all-gather.9.cloned.1.call-update) | async-done | bytes 16777232 | tf_op jit(solution)/shard_map/all_gather | solution.py:716
  264.3 17.6 %dispatch.2 = bf16[4,16,96,2048]{3,2,1,0:T(8,128)(2,1)} custom-call(bf16[16,384,256]{2,1,0:T(8,128)(2,1)} %fusion.4.pick_ref, bf16[16,256,2048]{2,1,0:T(8,128)(2,1)} %bitcast.136), custom_call_target="tpu_custom_call" | custom-call | flops 6442450944 | bytes 41943040 | tf_op jit(solution)/shard_map/dispatch/pallas_call | solution.py:562
  281.9 14.6 %fusion.56.u0_ref = f32[4,1536,256]{2,1,0:T(8,128)} fusion(bf16[4,1536,2048]{2,1,0:T(8,128)(2,1)} %bitcast.128, bf16[4,256,2048]{2,1,0:T(8,128)(2,1)} %w0_ref.1), kind=kOutput, calls=%fused_computation.115 | convolution fusion | flops 6442450944 | bytes 35651584 | tf_op jit(solution)/shard_map/emd,efd->emf/dot_general | solution.py:708
  296.5 14.7 %fusion.57.u1_ref = f32[4,1536,256]{2,1,0:T(8,128)} fusion(bf16[4,1536,2048]{2,1,0:T(8,128)(2,1)} %bitcast.129, bf16[4,256,2048]{2,1,0:T(8,128)(2,1)} %collective-permute-done.w1_ref), kind=kOutput, calls=%fused_computation.116 | convolution fusion | flops 6442450944 | bytes 35651584 | tf_op jit(solution)/shard_map/emd,efd->emf/dot_general | solution.py:708
  311.2 145.8 %all-gather.7.cloned.1.call-done = bf16[4096,2048]{1,0:T(8,128)(2,1)} async-done(((bf16[256,2048]{1,0:T(8,128)(2,1)}), bf16[4096,2048]{1,0:T(8,128)(2,1)}) %all-gather.7.cloned.1.call-update) | async-done | bytes 16777232 | tf_op jit(solution)/shard_map/all_gather | solution.py:716
  457.0 38.9 %dispatch.3 = (bf16[4,16,96,2048]{3,2,1,0:T(8,128)(2,1)}, f32[4,16,96,1]{3,2,1,0:T(8,128)}) custom-call(bf16[16,384,256]{2,1,0:T(8,128)(2,1)} %fusion.4.pick_ref, bf16[16,256,2048]{2,1,0:T(8,128)(2,1)} %bitcast.163, f32[16,256,32]{2,1,0:T(8,128)} %bitcast.139, bf16[2048,32]{1,0:T(8,128)(2,1)} %copy.53.router_ref, f32[384,32]{1,0:T(8,128)} %fusion.25.select_ref), custom_call_target="tpu_custom_call" | custom-call | flops 6442450944 | bytes 41943040 | tf_op jit(solution)/shard_map/dispatch/pallas_call | solution.py:562
  496.0 63.3 %expert.1 = (bf16[4,1536,2048]{2,1,0:T(8,128)(2,1)}, f32[4,1536,1]{2,1,0:T(8,128)}, bf16[4,1536,256]{2,1,0:T(8,128)(2,1)}, bf16[4,1536,256]{2,1,0:T(8,128)(2,1)}...) custom-call(bf16[4,1536,2048]{2,1,0:T(8,128)(2,1)} %bitcast.165, bf16[4,2048,512]{2,1,0:T(8,128)(2,1)} %reshape.185.w0_ref, ...), custom_call_target="tpu_custom_call" | custom-call | flops 51539607552 | bytes 98566144 | tf_op jit(solution)/shard_map/expert/pallas_call | solution.py:668
  559.3 20.6 %combine.2 = (bf16[16,256,2048]{2,1,0:T(8,128)(2,1)}, f32[16,4,256]{2,1,0:T(4,128)}) custom-call(bf16[16,384,256]{2,1,0:T(8,128)(2,1)} %fusion.4.pick_ref, bf16[4,16,96,2048]{3,2,1,0:T(8,128)(2,1)} %bitcast.132, f32[4,16,96,1]{3,2,1,0:T(8,128)} %bitcast.138), custom_call_target="tpu_custom_call" | custom-call | flops 6442450944 | bytes 41943040 | tf_op jit(solution)/shard_map/combine/pallas_call | solution.py:606
  579.9 9.1 spread.5
  589.0 0.9 bitcast_reduce_fusion
  589.9 158.4 %plane_reduce.2 = f32[256,2048]{1,0:T(8,128)} custom-call(bf16[4,2,2,256,2048]{4,3,2,1,0:T(8,128)(2,1)} %bitcast.134), custom_call_target="tpu_custom_call" | custom-call | tf_op jit(solution)/shard_map/plane_reduce/pallas_call | solution.py:292
  748.3 4.6 multiply_reduce_fusion
  752.9 1.4 copy-done.4
  754.3 1.6 fusion.46
  756.0 27.0 %down_rows.1 = bf16[4,1536,2048]{2,1,0:T(8,128)(2,1)} custom-call(bf16[4,1536,256]{2,1,0:T(8,128)(2,1)} %get-tuple-element.42.h0_ref, bf16[4,1536,256]{2,1,0:T(8,128)(2,1)} %get-tuple-element.43.h1_ref, bf16[4,256,2048]{2,1,0:T(8,128)(2,1)} %w0_ref.1, bf16[4,256,2048]{2,1,0:T(8,128)(2,1)} %collective-permute-done.w1_ref), custom_call_target="tpu_custom_call" | custom-call | flops 12884901888 | bytes 33554432 | tf_op jit(solution)/shard_map/down_rows/pallas_call | solution.py:626
  783.0 18.4 %combine.3 = bf16[16,256,2048]{2,1,0:T(8,128)(2,1)} custom-call(bf16[16,384,256]{2,1,0:T(8,128)(2,1)} %fusion.4.pick_ref, bf16[4,16,96,2048]{3,2,1,0:T(8,128)(2,1)} %bitcast.133), custom_call_target="tpu_custom_call" | custom-call | flops 6442450944 | bytes 41943040 | tf_op jit(solution)/shard_map/combine/pallas_call | solution.py:606
  801.5 0.9 all-gather.11.cloned.1.call-done
  802.4 5.9 convolution_convert_fusion.3
  808.3 5.5 convolution_convert_fusion.7.go_ref
  813.9 30.6 %attention.3 = (bf16[1024,512]{1,0:T(8,128)(2,1)}, bf16[1024,512]{1,0:T(8,128)(2,1)}, bf16[1024,512]{1,0:T(8,128)(2,1)}, f32[1,128]{1,0:T(1,128)}, f32[1,128]{1,0:T(1,128)}) custom-call(f32[1024,512]{1,0:T(8,128)} %fusion.19.q_ref, f32[1024,512]{1,0:T(8,128)} %fusion.21.k_ref, f32[1024,512]{1,0:T(8,128)} %fusion.22.v_ref, ...), custom_call_target="tpu_custom_call" | custom-call | flops 5368709120 | bytes 8388608 | tf_op jit(solution)/shard_map/attention/pallas_call | solution.py:489
  844.5 4.4 fusion.18
  848.9 4.1 fusion.20
  853.0 6.0 add_convert_fusion
  859.1 20.4 %convolution_convert_fusion = bf16[4,2048,512]{1,2,0:T(8,128)(2,1)} fusion(bf16[4,1536,2048]{2,1,0:T(8,128)(2,1)} %bitcast.166, bf16[4,1536,512]{2,1,0:T(8,128)(2,1)} %get-tuple-element.54), kind=kOutput, calls=%fused_computation.12 | convolution fusion | flops 12889096192 | bytes 39845888 | tf_op jit(solution)/shard_map/emd,emf->edf/dot_general | solution.py:708
  879.8 5.0 fusion.10
  884.8 2.7 fusion.11
  887.5 2.7 fusion.9
  890.2 3.1 pad_maximum_fusion
  893.4 19.5 %convolution_convert_fusion.1 = bf16[4,256,2048]{2,1,0:T(8,128)(2,1)} fusion(bf16[4,1536,256]{2,1,0:T(8,128)(2,1)} %get-tuple-element.43.h1_ref, bf16[4,1536,2048]{2,1,0:T(8,128)(2,1)} %bitcast.130), kind=kOutput, calls=%fused_computation.15 | convolution fusion | flops 6444548096 | bytes 32505856 | tf_op jit(solution)/shard_map/emf,emd->efd/dot_general | solution.py:708
  913.9 6.3 collective-permute-done.3
  920.2 17.9 %convert_add_fusion.1 = f32[4,256,2048]{2,1,0:T(8,128)} fusion(bf16[4,256,2048]{2,1,0:T(8,128)(2,1)S(1)} %collective-permute-done.3, bf16[4,1536,256]{2,1,0:T(8,128)(2,1)} %get-tuple-element.42.h0_ref, bf16[4,1536,2048]{2,1,0:T(8,128)(2,1)} %bitcast.131), kind=kOutput, calls=%fused_computation.6 | convolution fusion | flops 6446645248 | bytes 40894464 | tf_op jit(solution)/shard_map/emf,emd->efd/dot_general | solution.py:708
  938.2 23.8 %convert_add_fusion = f32[4,2048,512]{1,2,0:T(8,128)} fusion(bf16[4,2048,512]{1,2,0:T(8,128)(2,1)} %collective-permute-done.2, bf16[4,1536,2048]{2,1,0:T(8,128)(2,1)} %bitcast.167, bf16[4,1536,512]{2,1,0:T(8,128)(2,1)} %get-tuple-element.53), kind=kOutput, calls=%fused_computation | convolution fusion | flops 12893290496 | bytes 56623104 | tf_op jit(solution)/shard_map/emd,emf->edf/dot_general | solution.py:708
  962.0 25.6 %copy.60 = f32[4,2048,2,256]{3,2,1,0:T(2,128)} copy(f32[4,2048,2,256]{1,3,2,0:T(8,128)} %bitcast.135) | data formatting | bytes 33554432
  987.5 1.8 convert_element_type.125
  989.3 2.0 fusion.16
  992.2 23.1 %spread.6 = f32[32,24,128]{2,1,0:T(8,128)} custom-call(f32[32,24,128]{2,1,0:T(8,128)} %bitcast.140), custom_call_target="tpu_custom_call" | custom-call | tf_op jit(solution)/shard_map/spread/pallas_call | solution.py:107
  1015.3 1.6 reduce_sum.132.v_ref
  1017.0 17.9 %spread.7 = f32[32,24,128]{2,1,0:T(8,128)} custom-call(f32[24,128]{1,0:T(8,128)} %reduce_sum.132.v_ref), custom_call_target="tpu_custom_call" | custom-call | tf_op jit(solution)/shard_map/spread/pallas_call | solution.py:107
  1034.9 167.0 %plane_reduce.3 = f32[256,2048]{1,0:T(8,128)} custom-call(bf16[4,2,2,256,2048]{4,3,2,1,0:T(8,128)(2,1)} %bitcast.127), custom_call_target="tpu_custom_call" | custom-call | tf_op jit(solution)/shard_map/plane_reduce/pallas_call | solution.py:292
  1203.9 6.4 fusion.14
  1210.3 2.5 convert_bitcast_fusion
  (141 shorter events, 10.3 us)
Async XLA Ops:
  7.2 78.7 %copy-start = (bf16[512,2048]{1,0:T(8,128)(2,1)S(1)}, bf16[512,2048]{1,0:T(8,128)(2,1)}, u32[]{:S(2)}) copy-start(bf16[512,2048]{1,0:T(8,128)(2,1)} %param.20) | copy-start | bytes 6291460
  7.2 8.9 copy-start.32
  7.2 8.9 copy-start.31
  7.2 39.6 %all-gather.5.cloned.1.call-start = ((), (), s32[]{:S(2)}) async-start(), calls=%async_computation.3 | async-start | bytes 5242880 | tf_op jit(solution)/shard_map/all_gather | solution.py:716
  7.9 256.4 %all-gather.9.cloned.1.call-start = ((), (), s32[]{:S(2)}) async-start(), calls=%async_computation.5 | async-start | bytes 17825792 | tf_op jit(solution)/shard_map/all_gather | solution.py:716
  8.7 448.3 %all-gather.7.cloned.1.call-start = ((), (), s32[]{:S(2)}) async-start(), calls=%async_computation.4 | async-start | bytes 17825792 | tf_op jit(solution)/shard_map/all_gather | solution.py:716
  9.4 50.3 %copy-start.19 = (f32[2048]{0:T(1024)}, f32[2048]{0:T(1024)S(1)}, u32[]{:S(2)}) copy-start(f32[2048]{0:T(1024)S(1)} %convert_element_type.103) | copy-start | bytes 24580
  10.4 39.7 %copy-start.21 = (s32[1024]{0:T(1024)}, s32[1024]{0:T(1024)S(1)}, u32[]{:S(2)}) copy-start(s32[1024]{0:T(1024)S(1)} %convert_reduce_fusion) | copy-start | bytes 12292
  12.1 740.8 %copy-start.17 = (f32[2048]{0:T(1024)}, f32[2048]{0:T(1024)S(1)}, u32[]{:S(2)}) copy-start(f32[2048]{0:T(1024)S(1)} %convert_element_type.111) | copy-start | bytes 24580
  46.8 3.4 copy-start.10
  46.8 9.2 slice-start
  50.1 9.6 copy-start.29
  50.3 5.7 slice-start.1
  91.7 51.5 %copy-start.5 = (bf16[256,2048]{1,0:T(8,128)(2,1)S(1)}, bf16[256,2048]{1,0:T(8,128)(2,1)}, u32[]{:S(2)}) copy-start(bf16[256,2048]{1,0:T(8,128)(2,1)} %param.13) | copy-start | bytes 3145732
  145.9 1.3 copy-start.2
  145.9 607.0 %copy-start.24 = (f32[256]{0:T(256)}, f32[256]{0:T(256)S(1)}, u32[]{:S(2)}) copy-start(f32[256]{0:T(256)S(1)} %add_rsqrt_fusion.2) | copy-start | bytes 3076
  148.5 653.9 %all-gather.11.cloned.1.call-start = ((), (), s32[]{:S(2)}) async-start(), calls=%async_computation.6 | async-start | bytes 5242880 | tf_op jit(solution)/shard_map/all_gather | solution.py:716
  162.9 17.3 %copy-start.12 = (bf16[2048,32]{0,1:T(8,128)(2,1)S(1)}, bf16[2048,32]{0,1:T(8,128)(2,1)}, u32[]{:S(2)}) copy-start(bf16[2048,32]{0,1:T(8,128)(2,1)} %param.22) | copy-start | bytes 393220
  162.9 21.1 %copy-start.23 = (s32[256,8]{0,1:T(8,128)S(1)}, s32[256,8]{0,1:T(8,128)}, u32[]{:S(2)}) copy-start(s32[256,8]{0,1:T(8,128)} %param.14) | copy-start | bytes 24580
  162.9 21.9 %copy-start.7 = (bf16[256,2048]{1,0:T(8,128)(2,1)S(1)}, bf16[256,2048]{1,0:T(8,128)(2,1)}, u32[]{:S(2)}) copy-start(bf16[256,2048]{1,0:T(8,128)(2,1)} %multiply_convert_fusion) | copy-start | bytes 3145732
  162.9 333.1 %collective-permute-start.1 = (bf16[4,2048,512]{2,1,0:T(8,128)(2,1)}, bf16[4,2048,512]{2,1,0:T(8,128)(2,1)}, u32[]{:S(2)}, u32[]{:S(2)}) collective-permute-start(bf16[4,2048,512]{2,1,0:T(8,128)(2,1)} %reshape.185.w0_ref), channel_id=1, source_target_pairs={{0,1},{1,0},{2,3},{3,2},{4,5},{5,4},{6,7},{7,6},{8,9},{9,8},{10,11... | collective-permute-start | bytes 25165832 | tf_op jit(solution)/shard_map/ppermute | solution.py:712
  162.9 133.6 %collective-permute-start = (bf16[4,256,2048]{2,1,0:T(8,128)(2,1)}, bf16[4,256,2048]{2,1,0:T(8,128)(2,1)}, u32[]{:S(2)}, u32[]{:S(2)}) collective-permute-start(bf16[4,256,2048]{2,1,0:T(8,128)(2,1)} %w0_ref.1), channel_id=1, source_target_pairs={{0,1},{1,0},{2,3},{3,2},{4,5},{5,4},{6,7},{7,6},{8,9},{9,8},{10,11... | collective-permute-start | bytes 12582920 | tf_op jit(solution)/shard_map/ppermute | solution.py:712
  748.3 6.0 copy-start.3
  748.3 6.0 copy-start.9
  752.9 1.4 copy-start.4
  752.9 30.1 %copy-start.26 = (f32[256]{0:T(256)}, f32[256]{0:T(256)S(1)}, u32[]{:S(2)}) copy-start(f32[256]{0:T(256)S(1)} %broadcast_multiply_fusion.1) | copy-start | bytes 3076
  755.9 231.6 %reduce-scatter.8.cloned.1.call-start = ((), (), s32[]{:S(2)}) async-start(), calls=%async_computation.9 | async-start | bytes 2359296 | tf_op jit(solution)/shard_map/reduce_scatter | solution.py:720
  783.0 19.3 %copy-start.14 = (bf16[1024,512]{1,0:T(8,128)(2,1)S(1)}, bf16[1024,512]{1,0:T(8,128)(2,1)}, u32[]{:S(2)}) copy-start(bf16[1024,512]{1,0:T(8,128)(2,1)} %attention.2) | copy-start | bytes 3145732
  808.3 181.0 %reduce-scatter.4.cloned.1.call-start = ((), (), s32[]{:S(2)}) async-start(), calls=%async_computation.7 | async-start | bytes 5242880 | tf_op jit(solution)/shard_map/reduce_scatter | solution.py:720
  844.5 4.4 copy-start.36
  848.9 4.1 copy-start.15
  859.0 351.3 %reduce-scatter.6.cloned.1.call-start = ((), (), s32[]{:S(2)}) async-start(), calls=%async_computation.8 | async-start | bytes 7077888 | tf_op jit(solution)/shard_map/reduce_scatter | solution.py:720
  859.1 20.7 %copy-start.20 = (f32[2048]{0:T(1024)S(1)}, f32[2048]{0:T(1024)}, u32[]{:S(2)}) copy-start(f32[2048]{0:T(1024)} %copy-done.19) | copy-start | bytes 24580
  859.1 20.7 %copy-start.30 = (f32[1024]{0:T(1024)S(1)}, f32[1024]{0:T(1024)}, u32[]{:S(2)}) copy-start(f32[1024]{0:T(1024)} %copy-done.29) | copy-start | bytes 12292
  859.1 20.7 %copy-start.37 = (bf16[1024,512]{1,0:T(8,128)(2,1)S(1)}, bf16[1024,512]{1,0:T(8,128)(2,1)}, u32[]{:S(2)}) copy-start(bf16[1024,512]{1,0:T(8,128)(2,1)} %get-tuple-element.47) | copy-start | bytes 3145732
  879.5 5.3 copy-start.11
  879.5 5.3 copy-start.16
  879.5 58.6 %collective-permute-start.2 = (bf16[4,2048,512]{1,2,0:T(8,128)(2,1)}, bf16[4,2048,512]{1,2,0:T(8,128)(2,1)}, u32[]{:S(2)}, u32[]{:S(2)}) collective-permute-start(bf16[4,2048,512]{1,2,0:T(8,128)(2,1)} %convolution_convert_fusion), channel_id=1, source_target_pairs={{0,1},{1,0},{2,3},{3,2},{4,5},{5,4},{6,7},{7,6},{8,9},{9,8},{10,11... | collective-permute-start | bytes 25165832 | tf_op jit(solution)/shard_map/ppermute | solution.py:712
  884.8 2.7 copy-start.35
  893.3 19.8 %copy-start.28 = (f32[256]{0:T(256)S(1)}, f32[256]{0:T(256)}, u32[]{:S(2)}) copy-start(f32[256]{0:T(256)} %get-tuple-element.96) | copy-start | bytes 3076
  893.4 19.8 %copy-start.8 = (bf16[256,2048]{1,0:T(8,128)(2,1)S(1)}, bf16[256,2048]{1,0:T(8,128)(2,1)}, u32[]{:S(2)}) copy-start(bf16[256,2048]{1,0:T(8,128)(2,1)} %multiply_convert_fusion) | copy-start | bytes 3145732
  912.8 7.4 collective-permute-start.3
  961.9 27.4 %copy-start.6 = (bf16[256,2048]{1,0:T(8,128)(2,1)S(1)}, bf16[256,2048]{1,0:T(8,128)(2,1)}, u32[]{:S(2)}) copy-start(bf16[256,2048]{1,0:T(8,128)(2,1)} %param.13) | copy-start | bytes 3145732
  961.9 29.4 %copy-start.22 = (f32[2048]{0:T(1024)S(1)}, f32[2048]{0:T(1024)}, u32[]{:S(2)}) copy-start(f32[2048]{0:T(1024)} %get-tuple-element.88) | copy-start | bytes 24580
  961.9 29.5 %copy-start.34 = (f32[1,128]{1,0:T(1,128)S(1)}, f32[1,128]{1,0:T(1,128)}, u32[]{:S(2)}) copy-start(f32[1,128]{1,0:T(1,128)} %get-tuple-element.49) | copy-start | bytes 1540
  961.9 29.5 %copy-start.33 = (f32[1,128]{1,0:T(1,128)S(1)}, f32[1,128]{1,0:T(1,128)}, u32[]{:S(2)}) copy-start(f32[1,128]{1,0:T(1,128)} %get-tuple-element.50) | copy-start | bytes 1540
  1034.9 167.1 %copy-start.13 = (f32[32,24,128]{2,1,0:T(8,128)S(1)}, f32[32,24,128]{2,1,0:T(8,128)}, u32[]{:S(2)}) copy-start(f32[32,24,128]{2,1,0:T(8,128)} %spread.7) | copy-start | bytes 1179652
  1034.9 169.0 %copy-start.18 = (f32[2048]{0:T(1024)S(1)}, f32[2048]{0:T(1024)}, u32[]{:S(2)}) copy-start(f32[2048]{0:T(1024)} %copy-done.17) | copy-start | bytes 24580
  1034.9 169.0 %copy-start.25 = (f32[256]{0:T(256)S(1)}, f32[256]{0:T(256)}, u32[]{:S(2)}) copy-start(f32[256]{0:T(256)} %copy-done.24) | copy-start | bytes 3076
  1034.9 169.0 %copy-start.27 = (f32[256]{0:T(256)S(1)}, f32[256]{0:T(256)}, u32[]{:S(2)}) copy-start(f32[256]{0:T(256)} %copy-done.26) | copy-start | bytes 3076
  1203.9 8.9 copy-start.1
Sparse Core Ops, SparseCore 0:
  9.6 37.2 all-gather.4
  49.6 214.7 all-gather.8
  267.7 189.2 all-gather.6
  756.1 46.2 all-gather.10
  808.4 79.5 reduce-scatter.7
  890.4 43.9 reduce-scatter.3
  937.9 123.8 reduce-scatter.5

commit v5 on v4

--- a/solution.py
+++ b/solution.py
@@ -132,10 +132,87 @@
     return order
 
 
-def reduce_kernel(
-    depth, half, p_ref, out_ref, own, one, two, right, left,
-    own_sem, s1, r1, s2, r2, sr, rr, sl, rl,
-):
+def fill_job(big_hbm, small_hbm, own_hbm, other_hbm, big_is_left, big, small, wide, narrow, sems):
+    tile = big.shape[-1]
+    columns = small_hbm[0].shape[-1]
+    tiles = big_hbm.shape[-1] // tile
+    small_at = pl.ds(0, columns)
+
+    def loads(unit, slot):
+        expert_at, tile_at = unit // tiles, lax.rem(unit, tiles)
+        cut = pl.ds(pl.multiple_of(tile_at * tile, tile), tile)
+        yield pltpu.make_async_copy(big_hbm.at[expert_at, :, cut], big.at[slot], sems.at[slot, 0])
+        for side in (0, 1):
+            yield pltpu.make_async_copy(
+                small_hbm[side].at[expert_at],
+                small.at[slot, side, :, small_at],
+                sems.at[slot, 1 + side],
+            )
+
+    def stores(unit):
+        expert_at, tile_at = unit // tiles, lax.rem(unit, tiles)
+        cut = pl.ds(pl.multiple_of(tile_at * tile, tile), tile)
+        for side, (stage, target) in enumerate(((wide, own_hbm), (narrow, other_hbm))):
+            if big_is_left:
+                source, where = stage.at[:, small_at], target.at[expert_at, cut, :]
+            else:
+                source, where = stage.at[small_at, :], target.at[expert_at, :, cut]
+            yield pltpu.make_async_copy(source, where, sems.at[2, side])
+
+    def run(start, count):
+        for copy in loads(start, 0):
+            copy.start()
+
+        def body(index, carry):
+            slot = lax.rem(index, 2)
+
+            @pl.when(index + 1 < count)
+            def _():
+                for copy in loads(start + index + 1, 1 - slot):
+                    copy.start()
+
+            for copy in loads(start + index, slot):
+                copy.wait()
+            sums = []
+            for side in (0, 1):
+                left, right = big[slot], small[slot, side, :, small_at]
+                sums.append(dot_tn(left, right) if big_is_left else dot_tn(right, left))
+
+            @pl.when(index > 0)
+            def _():
+                for copy in stores(start + index - 1):
+                    copy.wait()
+
+            for stage, total in zip((wide, narrow), sums):
+                if big_is_left:
+                    stage[:, small_at] = total.astype(stage.dtype)
+                else:
+                    stage[small_at, :] = total.astype(stage.dtype)
+            for copy in stores(start + index):
+                copy.start()
+            return carry
+
+        lax.fori_loop(0, count, body, 0)
+        for copy in stores(start + count - 1):
+            copy.wait()
+
+    return run, tiles
+
+
+def reduce_kernel(depth, half, filled, *refs):
+    refs = list(refs)
+
+    def take(count):
+        taken = refs[:count]
+        del refs[:count]
+        return taken
+
+    pick_ref, rows_ref = take(2)
+    factors = take(6) if filled else ()
+    (out_ref,) = take(1)
+    grads = take(4) if filled else ()
+    part, value, pick, one, two, right, left = take(7)
+    load_sem, s1, r1, s2, r2, sr, rr, sl, rl = take(9)
     ep = lax.axis_index("ep")
     x = lax.axis_index("x")
     z = ep // 2
@@ -151,107 +228,144 @@
     peers = 2 + (z > 0).astype(jnp.int32) + (z < depth - 1).astype(jnp.int32)
     pl.semaphore_wait(barrier, peers)
 
-    order = visiting_order(depth)
-    cols = (pl.ds(0, half), pl.ds(half, half))
-    mine = (y, x)
-
-    def block(part, level, step, theirs):
-        near = (x, y)[part]
-        near = 1 - near if theirs else near
-        far = 1 - mine[part] if step == 0 else mine[part]
-        at = (far, near) if part == 0 else (near, far)
-        return p_ref.at[level, at[0], at[1], :, cols[part]]
-
-    def send_one(part, level, step):
+    local, _, capacity, _ = rows_ref.shape
+    total = 4 * depth
+
+    def level_of(turn):
+        return jnp.where(lax.rem(turn, 2) == 0, depth - 1 - turn // 2, turn // 2)
+
+    def place(number):
+        later = number - depth
+        level = jnp.where(later < 0, level_of(number), level_of(later // 3))
+        kind = jnp.where(later < 0, 0, 1 + lax.rem(later, 3))
+        return level, kind
+
+    def fetch(number, slot):
+        level, kind = place(number)
+        near_y = jnp.where(lax.rem(kind, 2) == 1, y, 1 - y)
+        near_x = jnp.where(kind >= 2, x, 1 - x)
+        block = (level * 2 + near_y) * 2 + near_x
+        yield pltpu.make_async_copy(rows_ref.at[:, block], value.at[slot], load_sem.at[slot, 0])
+        yield pltpu.make_async_copy(pick_ref.at[block], pick.at[slot], load_sem.at[slot, 1])
+
+    def compute(number):
+        slot = lax.rem(number, 2)
+
+        @pl.when(number + 1 < total)
+        def _():
+            for copy in fetch(number + 1, 1 - slot):
+                copy.start()
+
+        for copy in fetch(number, slot):
+            copy.wait()
+        level, kind = place(number)
+        for side in (0, 1):
+            picked = value[slot, :, :, side * half : (side + 1) * half]
+            picked = picked.reshape(local * capacity, half)
+            part[level, kind, side] = dot_tn(pick[slot], picked).astype(BF16)
+
+    def send_one(side, level, step):
         return remote(
-            block(part, level, step, True),
-            one.at[part, level, step],
-            s1.at[part, level, step],
-            r1.at[part, level, step],
-            first[part],
+            part.at[level, 0 if step == 0 else 1 + side, side],
+            one.at[side, level, step],
+            s1.at[side, level, step],
+            r1.at[side, level, step],
+            first[side],
         )
 
-    def send_two(part, level):
+    def send_two(side, level):
         return remote(
-            one.at[part, level, 0],
-            two.at[part, level],
-            s2.at[part, level],
-            r2.at[part, level],
-            second[part],
+            one.at[side, level, 0],
+            two.at[side, level],
+            s2.at[side, level],
+            r2.at[side, level],
+            second[side],
         )
 
-    def load(part, level, step):
-        return pltpu.make_async_copy(
-            block(part, level, step, False),
-            own.at[part, level, step],
-            own_sem.at[part, level, step],
-        )
-
-    def go_right(part, level):
-        ref = right.at[part, level]
-        return remote(ref, ref, sr.at[part, level], rr.at[part, level], up)
-
-    def go_left(part, level):
-        ref = left.at[part, level]
-        return remote(ref, ref, sl.at[part, level], rl.at[part, level], down)
-
-    for level in order:
-        for part in (0, 1):
-            send_one(part, level, 0).start()
-    for step in (0, 1):
-        for level in order:
-            for part in (0, 1):
-                load(part, level, step).start()
-    for level in order:
-        for part in (0, 1):
-            load(part, level, 0).wait()
-            send_one(part, level, 0).wait()
-            arrived = one.at[part, level, 0]
-            add_into(arrived, [arrived, own.at[part, level, 0]])
-            send_two(part, level).start()
-            send_one(part, level, 1).start()
+    def go_right(side, level):
+        ref = right.at[side, level]
+        return remote(ref, ref, sr.at[side, level], rr.at[side, level], up)
+
+    def go_left(side, level):
+        ref = left.at[side, level]
+        return remote(ref, ref, sl.at[side, level], rl.at[side, level], down)
+
+    fills = []
+    if filled:
+        hidden, gates, outs = factors[:3], factors[3:], grads
+        scratch = take(5)
+        fills.append(fill_job(gates[0], gates[1:], outs[0], outs[1], True, *scratch))
+        fills.append(fill_job(hidden[0], hidden[1:], outs[2], outs[3], False, *scratch))
+
+    for copy in fetch(0, 0):
+        copy.start()
+
+    def open_turn(turn, carry):
+        compute(turn)
+        level = level_of(turn)
+        for side in (0, 1):
+            send_one(side, level, 0).start()
+        return carry
+
+    lax.fori_loop(0, depth, open_turn, 0)
+
+    def turn_one(turn, carry):
+        lax.fori_loop(0, 3, lambda k, c: (compute(depth + turn * 3 + k), c)[1], 0)
+        level = level_of(turn)
+        for side in (0, 1):
+            send_one(side, level, 0).wait()
+            arrived = one.at[side, level, 0]
+            add_into(arrived, [arrived, part.at[level, 2 - side, side]])
+            send_two(side, level).start()
+            send_one(side, level, 1).start()
+        for run, tiles in fills:
+            share = local * tiles // depth
+            run(turn * share, share)
+        return carry
+
+    lax.fori_loop(0, depth, turn_one, 0)
 
     def begin(level):
-        for part in (0, 1):
+        for side in (0, 1):
             if level > 0:
 
                 @pl.when(z == 0)
                 def _():
-                    add_into(right.at[part, level], [two.at[part, level]])
-                    go_right(part, level).start()
+                    add_into(right.at[side, level], [two.at[side, level]])
+                    go_right(side, level).start()
 
             if level < depth - 1:
 
                 @pl.when(z == depth - 1)
                 def _():
-                    add_into(left.at[part, level], [two.at[part, level]])
-                    go_left(part, level).start()
+                    add_into(left.at[side, level], [two.at[side, level]])
+                    go_left(side, level).start()
 
     def forward(level):
-        for part in (0, 1):
+        for side in (0, 1):
 
             @pl.when((z > 0) & (z < level))
             def _():
-                go_right(part, level).wait_recv()
-                ref = right.at[part, level]
-                add_into(ref, [ref, two.at[part, level]])
-                go_right(part, level).start()
+                go_right(side, level).wait_recv()
+                ref = right.at[side, level]
+                add_into(ref, [ref, two.at[side, level]])
+                go_right(side, level).start()
 
             @pl.when((z < depth - 1) & (z > level))
             def _():
-                go_left(part, level).wait_recv()
-                ref = left.at[part, level]
-                add_into(ref, [ref, two.at[part, level]])
-                go_left(part, level).start()
-
+                go_left(side, level).wait_recv()
+                ref = left.at[side, level]
+                add_into(ref, [ref, two.at[side, level]])
+                go_left(side, level).start()
+
+    order = visiting_order(depth)
     for turn, level in enumerate(order):
-        for part in (0, 1):
-            load(part, level, 1).wait()
-            send_one(part, level, 1).wait()
-            kept = own.at[part, level, 1]
-            add_into(kept, [one.at[part, level, 1], kept])
-            send_two(part, level).wait()
-            add_into(two.at[part, level], [two.at[part, level], kept])
+        for side in (0, 1):
+            send_one(side, level, 1).wait()
+            kept = part.at[level, 3, side]
+            add_into(kept, [one.at[side, level, 1], kept])
+            send_two(side, level).wait()
+            add_into(two.at[side, level], [two.at[side, level], kept])
         begin(level)
         if turn > 0:
             forward(order[turn - 1])
@@ -260,52 +374,85 @@
 
         @pl.when(z == level)
         def _():
-            for part in (0, 1):
-                terms = [two.at[part, level]]
+            for side in (0, 1):
+                terms = [two.at[side, level]]
                 if level > 0:
-                    go_right(part, level).wait_recv()
-                    terms.append(right.at[part, level])
+                    go_right(side, level).wait_recv()
+                    terms.append(right.at[side, level])
                 if level < depth - 1:
-                    go_left(part, level).wait_recv()
-                    terms.append(left.at[part, level])
-                add_into(out_ref.at[:, cols[part]], terms)
-
-        for part in (0, 1):
-            pl.when(z < level)(lambda: go_right(part, level).wait_send())
-            pl.when(z > level)(lambda: go_left(part, level).wait_send())
-
-
-def plane_reduce(parts, collective_id):
-    blocks, rows, columns = parts.shape
+                    go_left(side, level).wait_recv()
+                    terms.append(left.at[side, level])
+                add_into(out_ref.at[:, pl.ds(side * half, half)], terms)
+
+        for side in (0, 1):
+            pl.when(z < level)(lambda: go_right(side, level).wait_send())
+            pl.when(z > level)(lambda: go_left(side, level).wait_send())
+
+
+def plane_reduce(pick, values, collective_id, factors=()):
+    local, blocks, capacity, columns = values.shape
+    rows = pick.shape[-1]
     ep_count, x_count = lax.axis_size("ep"), lax.axis_size("x")
-    if x_count != 2 or ep_count % 2 or blocks * rows * columns > 2**24:
-        flat = parts.reshape(blocks * rows, columns)
-        return lax.psum_scatter(flat, PLANE, scatter_dimension=0, tiled=True).astype(F32)
+    if x_count != 2 or ep_count % 2 or blocks * rows * columns > 2**23 or local * 4 % ep_count:
+        (flat,) = combine(pick, values, group=4)
+        flat = flat.reshape(blocks * rows, columns)
+        total = lax.psum_scatter(flat, PLANE, scatter_dimension=0, tiled=True).astype(F32)
+        if not factors:
+            return total
+        g_rows, h0, h1, h_rows, g0, g1 = factors
+        return (
+            total,
+            einsum("emd,emf->edf", h_rows, g0),
+            einsum("emd,emf->edf", h_rows, g1).astype(BF16),
+            einsum("emf,emd->efd", h0, g_rows),
+            einsum("emf,emd->efd", h1, g_rows).astype(BF16),
+        )
     depth, half = ep_count // 2, columns // 2
 
     def buffer(*lead):
-        return pltpu.VMEM(lead + (rows, half), parts.dtype)
+        return pltpu.VMEM(lead + (rows, half), BF16)
 
     def sems(*lead):
         return pltpu.SemaphoreType.DMA(lead)
 
-    return pl.pallas_call(
-        functools.partial(reduce_kernel, depth, half),
-        out_shape=jax.ShapeDtypeStruct((rows, columns), F32),
-        in_specs=[pl.BlockSpec(memory_space=pl.ANY)],
-        out_specs=pl.BlockSpec(memory_space=pltpu.VMEM),
-        scratch_shapes=[
-            buffer(2, depth, 2), buffer(2, depth, 2),
-            buffer(2, depth), buffer(2, depth), buffer(2, depth),
-            sems(2, depth, 2), sems(2, depth, 2), sems(2, depth, 2),
-            sems(2, depth), sems(2, depth), sems(2, depth),
-            sems(2, depth), sems(2, depth), sems(2, depth),
-        ],
+    shapes = [jax.ShapeDtypeStruct((rows, columns), F32)]
+    scratch = [
+        buffer(depth, 4, 2),
+        pltpu.VMEM((2, local, capacity, columns), BF16),
+        pltpu.VMEM((2, local * capacity, rows), BF16),
+        buffer(2, depth, 2), buffer(2, depth), buffer(2, depth), buffer(2, depth),
+        sems(2, 2), sems(2, depth, 2), sems(2, depth, 2),
+        sems(2, depth), sems(2, depth), sems(2, depth),
+        sems(2, depth), sems(2, depth), sems(2, depth),
+    ]
+    if factors:
+        count, hidden, gates = factors[0].shape[1], factors[1].shape[2], factors[4].shape[2]
+        shapes += [
+            jax.ShapeDtypeStruct((local, columns, gates), F32),
+            jax.ShapeDtypeStruct((local, columns, gates), BF16),
+            jax.ShapeDtypeStruct((local, hidden, columns), F32),
+            jax.ShapeDtypeStruct((local, hidden, columns), BF16),
+        ]
+        scratch += [
+            pltpu.VMEM((2, count, gates), BF16),
+            pltpu.VMEM((2, 2, count, gates), BF16),
+            pltpu.VMEM((gates, gates), F32),
+            pltpu.VMEM((gates, gates), BF16),
+            sems(3, 3),
+        ]
+    anywhere = pl.BlockSpec(memory_space=pl.ANY)
+    results = pl.pallas_call(
+        functools.partial(reduce_kernel, depth, half, bool(factors)),
+        out_shape=shapes,
+        in_specs=[anywhere] * (2 + len(factors)),
+        out_specs=[pl.BlockSpec(memory_space=pltpu.VMEM)] + [anywhere] * (len(shapes) - 1),
+        scratch_shapes=scratch,
         compiler_params=pltpu.CompilerParams(
             collective_id=collective_id, has_side_effects=True, vmem_limit_bytes=VMEM_BYTES
         ),
         name="plane_reduce",
-    )(parts.reshape(depth, 2, 2, rows, columns))
+    )(pick, values, *factors)
+    return results if factors else results[0]
 
 
 def group_kernel(pieces, p_ref, out_ref, near, far, kept, got, own_sem, s1, r1, s2, r2, s3, r3):
@@ -517,57 +664,22 @@
         pick_rows_of(pick_ref[index], value_ref[index], out_ref, index)
 
 
-def route_kernel(pick_ref, value_ref, mask_ref, router_ref, select_ref, out_ref, prob_ref):
-    local, _, capacity, _ = out_ref.shape
-    for index in range(pick_ref.shape[0]):
-        pick, value, mask = pick_ref[index], value_ref[index], mask_ref[index] > 0
-        pick_rows_of(pick, value, out_ref, index)
-        kept = jnp.where(mask, dot_nn(value, router_ref[...]), MASKED)
-        lifted = jnp.exp(kept - jnp.max(kept, axis=-1, keepdims=True))
-        lifted = jnp.where(mask, lifted, 0.0)
-        rest = lifted / jnp.sum(lifted, axis=-1, keepdims=True)
-        picked = jnp.zeros((pick.shape[0], rest.shape[1]), F32)
-        for _ in range(3):
-            piece = rest.astype(BF16)
-            rest = rest - piece.astype(F32)
-            picked = picked + dot_nn(pick, piece)
-        prob = jnp.sum(picked * select_ref[...], axis=-1, keepdims=True)
-        for expert_at in range(local):
-            prob_ref[expert_at, index] = prob[expert_at * capacity : (expert_at + 1) * capacity]
-
-
-def dispatch(pick, value, local, routing=None, group=2):
+def dispatch(pick, value, local, group):
     blocks, picked, rows = pick.shape
     width = value.shape[-1]
     capacity = picked // local
-
-    def block(*shape):
-        return pl.BlockSpec((group,) + shape, lambda b: (b, 0, 0))
-
-    def result(columns):
-        return pl.BlockSpec((local, group, capacity, columns), lambda b: (0, b, 0, 0))
-
-    def shape(columns, kind):
-        return jax.ShapeDtypeStruct((local, blocks, capacity, columns), kind)
-
-    ins, specs = [pick, value], [block(picked, rows), block(rows, width)]
-    shapes, outs = [shape(width, BF16)], [result(width)]
-    if routing is not None:
-        mask, router, select = routing
-        ins += [mask, router, select]
-        specs += [block(rows, mask.shape[-1])]
-        specs += [pl.BlockSpec(t.shape, lambda b: (0, 0)) for t in (router, select)]
-        shapes += [shape(1, F32)]
-        outs += [result(1)]
     return pl.pallas_call(
-        dispatch_kernel if routing is None else route_kernel,
+        dispatch_kernel,
         grid=(blocks // group,),
-        out_shape=shapes,
-        in_specs=specs,
-        out_specs=outs,
+        out_shape=jax.ShapeDtypeStruct((local, blocks, capacity, width), BF16),
+        in_specs=[
+            pl.BlockSpec((group, picked, rows), lambda b: (b, 0, 0)),
+            pl.BlockSpec((group, rows, width), lambda b: (b, 0, 0)),
+        ],
+        out_specs=pl.BlockSpec((local, group, capacity, width), lambda b: (0, b, 0, 0)),
         name="dispatch",
         **params(2 * blocks * picked * rows * width, 2 * blocks * width * (picked + rows)),
-    )(*ins)
+    )(pick, value)
 
 
 def combine_kernel(pick_ref, value_ref, *refs):
@@ -789,16 +901,17 @@
     h_two = norm_rows(middle, gain_two).astype(BF16)
 
     g_plane = g_flat.reshape(blocks, rows, width)
-    routes_plane = spread(routes.T, PLANE, 1).transpose(0, 2, 1).reshape(blocks * rows, topk)
+    mask_own = route_mask(routes, experts_all)
+    probs_own = masked_softmax(jnp.dot(h_two, w_router, preferred_element_type=F32), mask_own)
+    shared = spread(jnp.where(mask_own, probs_own, -1.0).T, PLANE, 1)
     h_flat = gather(h_two, PLANE)
     pair_other = swap_cores(expert_gate_up.reshape(local, width, 2 * hidden_local))
     down_other = swap_cores(expert_down)
     pair_own = expert_gate_up.reshape(local, width, 2 * hidden_local)
 
-    mask_plane = route_mask(routes_plane, experts_all)
     first = my_ep * local
-    mask_here = lax.dynamic_slice_in_dim(mask_plane, first, local, axis=1)
-    mask_here = mask_here.reshape(blocks, rows, local).transpose(0, 2, 1)
+    here = lax.dynamic_slice_in_dim(shared, first, local, axis=1)
+    mask_here = here >= 0.0
     before = jnp.triu(jnp.ones((rows, rows), BF16), 1)
     rank = einsum("bet,tu->beu", mask_here.astype(BF16), before).astype(jnp.int32)
     slots = jnp.arange(capacity, dtype=jnp.int32)[None, None, :, None]
@@ -807,53 +920,39 @@
     pick_rows = pick.reshape(blocks, local * capacity, rows)
     count = blocks * capacity
 
-    (g_rows,) = dispatch(pick_rows, g_plane, local, group=4)
+    g_rows = dispatch(pick_rows, g_plane, local, group=4)
     g_rows = g_rows.reshape(local, count, width)
     back_own = einsum("emd,efd->emf", g_rows, expert_down)
     back_other = einsum("emd,efd->emf", g_rows, down_other)
-    h_flat, back_own, back_other = lax.optimization_barrier((h_flat, back_own, back_other))
-    select_column = first + jnp.arange(local * capacity, dtype=jnp.int32) // capacity
-    select = select_column[:, None] == jnp.arange(experts_all, dtype=jnp.int32)[None, :]
-    routing = (
-        mask_plane.astype(F32).reshape(blocks, rows, experts_all),
-        w_router,
-        select.astype(F32),
-    )
-    h_rows, prob_rows = dispatch(
-        pick_rows, h_flat.reshape(blocks, rows, width), local, routing, group=2
-    )
+    prob_rows = jnp.sum(jnp.where(picks, here[:, :, None, :], 0.0), axis=-1)
+    prob_rows = prob_rows.transpose(1, 0, 2).reshape(local, count, 1)
+    h_flat, back_own, back_other, prob_rows = lax.optimization_barrier(
+        (h_flat, back_own, back_other, prob_rows)
+    )
+    h_rows = dispatch(pick_rows, h_flat.reshape(blocks, rows, width), local, group=4)
     h_rows = h_rows.reshape(local, count, width)
-    prob_rows = prob_rows.reshape(local, count, 1)
     back_rows, dot_rows, weighted_own, weighted_other, ggu_own, ggu_other = expert(
         h_rows, pair_own, pair_other, back_own, back_other, prob_rows, min(384, count)
     )
-    back_part, dots_token = combine(
-        pick_rows,
-        back_rows.reshape(local, blocks, capacity, width),
-        dot_rows.reshape(local, blocks, capacity, 1),
-        group=2,
-    )
+    dot_rows = dot_rows.reshape(local, blocks, capacity).transpose(1, 0, 2)
+    dots_token = jnp.sum(jnp.where(picks, dot_rows[..., None], 0.0), axis=2)
     grad_probs = spread(dots_token, PLANE, 2, True)
     grad_probs = jnp.sum(grad_probs.reshape(ep_count, x_count, local, rows), axis=1)
     grad_probs = grad_probs.reshape(experts_all, rows).T
-    back_sum = plane_reduce(back_part, 3)
+    back_sum, grad_pair_own, grad_pair_other, grad_down_own, grad_down_other = plane_reduce(
+        pick_rows,
+        back_rows.reshape(local, blocks, capacity, width),
+        3,
+        (g_rows, weighted_own, weighted_other, h_rows, ggu_own, ggu_other),
+    )
     out_rows = down_rows(
         weighted_own, weighted_other, expert_down, down_other, min(384, count)
-    )
-    (out_part,) = combine(
-        pick_rows, out_rows.reshape(local, blocks, capacity, width), group=4
-    )
-
-    grad_pair_own = einsum("emd,emf->edf", h_rows, ggu_own)
-    grad_pair_other = einsum("emd,emf->edf", h_rows, ggu_other)
-    grad_down_own = einsum("emf,emd->efd", weighted_own, g_rows)
-    grad_down_other = einsum("emf,emd->efd", weighted_other, g_rows)
-    grad_pair = grad_pair_own + swap_cores(grad_pair_other.astype(BF16)).astype(F32)
-    grad_down = grad_down_own + swap_cores(grad_down_other.astype(BF16)).astype(F32)
+    ).reshape(local, blocks, capacity, width)
+
+    grad_pair = grad_pair_own + swap_cores(grad_pair_other).astype(F32)
+    grad_down = grad_down_own + swap_cores(grad_down_other).astype(F32)
     grad_gate_up = grad_pair.reshape(local, width, 2, hidden_local)
 
-    mask_own = route_mask(routes, experts_all)
-    probs_own = masked_softmax(jnp.dot(h_two, w_router, preferred_element_type=F32), mask_own)
     inner = jnp.sum(probs_own * grad_probs, axis=-1, keepdims=True)
     grad_logits = probs_own * (grad_probs - inner)
     grad_router = lax.dot_general(
@@ -866,7 +965,7 @@
     grad_mid = grad_out + grad_mid_norm
 
     ga_seq = gather(grad_mid.astype(BF16), GROUP)
-    ga_seq, out_part = lax.optimization_barrier((ga_seq, out_part))
+    ga_seq, out_rows = lax.optimization_barrier((ga_seq, out_rows))
     grad_wout = lax.dot_general(
         attn_vals, ga_seq, (((0,), (0,)), ((), ())), preferred_element_type=F32
     )
@@ -909,8 +1008,8 @@
     small = jnp.pad(small, (0, padded - length)).reshape(devices, -1, 128)
     small = jnp.sum(spread(small, ALL, 5, True), axis=0)
     small = spread(small, ALL, 6).reshape(-1)
-    out_part, small = lax.optimization_barrier((out_part, small))
-    output = (middle + plane_reduce(out_part, 4)).astype(BF16)
+    out_rows, small = lax.optimization_barrier((out_rows, small))
+    output = (middle + plane_reduce(pick_rows, out_rows, 4)).astype(BF16)
     cuts = (experts_all * width, width, width, head_dim, head_dim)
     starts = [sum(cuts[:index]) for index in range(5)]
     router_sum, *gains = (small[at : at + cut] for at, cut in zip(starts, cuts))

time: 1240 us -> 1210 us (0.976)
  matrix products: 172 us -> 89.8 us
  other arithmetic: 39.7 us -> 69.3 us
  waiting for transfers between devices: 264 us -> 285 us
    dot_general x7 -> x3, matrix products: 111 us -> 29.2 us  [einsum(): return jnp.einsum(spec, left, right, preferred_element_type=F32)]
    unnamed x88 -> x71, local copies, waits for them, and re-layouts: 29.7 us -> 3.17 us
    add x1 -> x2, other arithmetic: 0.01 us -> 23.6 us  [the longest x1 14 us: per_device(): grad_pair = grad_pair_own + swap_cores(grad_pair_other).astype(F32)]
    all_gather x4, waiting for transfers between devices: 256 us -> 278 us  [gather(): return lax.all_gather(value, axes, axis=0, tiled=True)]
    reshape x0 -> x3, local copies, waits for them, and re-layouts: none -> 20.2 us  [the longest x1 20.1 us: per_device(): grad_gate_up = grad_pair.reshape(local, width, 2, hidden_local)]
    pallas_call x4, Pallas kernels: 61.1 us -> 78.1 us  [spread(): pl.pallas_call(functools.partial(spread_kernel, axes, counts, own_slices)...]
    pallas_call x6 -> x4, Pallas kernels: 421 us -> 408 us  [the longest x2 374 us: plane_reduce(): pl.pallas_call(functools.partial(reduce_kernel, depth, half, bool(factors...]
  transfers between devices with their start and end apart: 11 -> 11, of which waited for: 5 -> 5; matrix products, arithmetic and copies ran while one was open for 20% -> 15% of each run, Pallas kernels for 35% -> 36%
where the time goes in v5:
time: 1210 us; the launch traced here: 1190 us
  Pallas kernels  681 us (56%)
  waiting for transfers between devices  285 us (24%)
  matrix products  89.8 us (7%)
  other arithmetic  69.3 us (6%)
  local copies, waits for them, and re-layouts  45.6 us (4%)
  between operations  15.1 us (1%)
    pallas_call x2, Pallas kernels, plane_reduce(): pl.pallas_call(functools.partial(reduce_kernel, depth, half, bool(factors...  374 us
    all_gather x4, waiting for transfers between devices, gather(): return lax.all_gather(value, axes, axis=0, tiled=True)  278 us
    pallas_call x4, Pallas kernels, spread(): pl.pallas_call(functools.partial(spread_kernel, axes, counts, own_slices)...  78.1 us
    pallas_call x1, Pallas kernels, expert(): pl.pallas_call(expert_kernel, grid=(local, count // step), out_shape=[s(w...  63.4 us
    pallas_call x2, Pallas kernels, attention_call(): pl.pallas_call(functools.partial(kernel, min(512, seq_len)), grid=(heads,...  53.4 us
    pallas_call x1, Pallas kernels, group_reduce(): pl.pallas_call(functools.partial(group_kernel, pieces), out_shape=jax.Sha...  51.5 us
    pallas_call x2, Pallas kernels, dispatch(): pl.pallas_call(dispatch_kernel, grid=(blocks // group,), out_shape=jax.Sh...  34.5 us
    dot_general x3, matrix products, einsum(): return jnp.einsum(spec, left, right, preferred_element_type=F32)  29.2 us
  transfers between devices with their start and end apart: 11, of which 5 were waited for; matrix products, arithmetic and copies ran while one was open for 15% of the time, Pallas kernels for 36%

profile of v5, /device:TPU:0, one launch (start us, length us, event | category | flops | bytes accessed | tf_op | source)
XLA Modules:
  0.0 1187.3 jit_solution(18308359932194382379)
XLA Ops:
  8.0 0.7 all-gather.9.cloned.1.call-update
  10.1 0.8 reduce-window.4
  11.1 1.0 copy.43.dr_ref
  12.9 1.9 fusion.25
  14.8 1.3 pad_maximum_fusion.1
  16.6 30.2 %all-gather.5.cloned.1.call-done = bf16[1024,2048]{1,0:T(8,128)(2,1)} async-done(((bf16[256,2048]{1,0:T(8,128)(2,1)}), bf16[1024,2048]{1,0:T(8,128)(2,1)}) %all-gather.5.cloned.1.call-update) | async-done | bytes 4194320 | tf_op jit(solution)/shard_map/all_gather | solution.py:828
  46.8 3.2 fusion
  50.2 5.7 fusion.21.k_ref
  56.0 3.7 fusion.22.v_ref
  59.7 3.7 fusion.19.q_ref
  63.4 22.8 %attention.2 = bf16[1024,512]{1,0:T(8,128)(2,1)} custom-call(f32[1024,512]{1,0:T(8,128)} %fusion.19.q_ref, f32[1024,512]{1,0:T(8,128)} %fusion.21.k_ref, f32[1024,512]{1,0:T(8,128)} %fusion.22.v_ref, f32[1,128]{1,0:T(1,128)} %get-tuple-element.83.qg_ref, f32[1,128]{1,0:T(1,128)} %get-tuple-element.82.kg_ref, f32[1024,128]{1,0:T(8,128)} %get-tuple-element.80.cos_ref, ...), custom_call_target="tpu_custom_call" | custom-call | flops 2147483648 | bytes 8388608 | tf_op jit(solution)/shard_map/attention/pallas_call | solution.py:636
  86.2 5.6 convolution_convert_fusion
  91.8 51.5 %group_reduce.1 = f32[256,2048]{1,0:T(8,128)} custom-call(bf16[2,2,256,2048]{3,2,1,0:T(8,128)(2,1)} %bitcast.123), custom_call_target="tpu_custom_call" | custom-call | tf_op jit(solution)/shard_map/group_reduce/pallas_call | solution.py:518
  143.3 2.7 multiply_reduce_fusion.2
  146.0 1.3 copy-done.1
  147.3 1.2 multiply_convert_fusion
  148.6 14.3 %reshape.159.w0_ref = bf16[4,2048,512]{2,1,0:T(8,128)(2,1)} reshape(bf16[4,2048,2,256]{3,2,1,0:T(2,128)(2,1)} %param.23) | data formatting | bytes 16777216 | tf_op jit(solution)/shard_map/reshape | solution.py:910
  164.7 24.1 %spread.4 = f32[16,32,256]{2,1,0:T(8,128)} custom-call(f32[32,256]{1,0:T(8,128)} %fusion.37.v_ref), custom_call_target="tpu_custom_call" | custom-call | tf_op jit(solution)/shard_map/spread/pallas_call | solution.py:107
  188.8 0.9 broadcast_compare_fusion
  189.9 1.5 select_reduce_fusion.1
  191.5 2.7 fusion.5.pick_ref.refs_0_
  194.2 78.0 %all-gather.9.cloned.1.call-done = bf16[4096,2048]{1,0:T(8,128)(2,1)} async-done(((bf16[256,2048]{1,0:T(8,128)(2,1)}), bf16[4096,2048]{1,0:T(8,128)(2,1)}) %all-gather.9.cloned.1.call-update) | async-done | bytes 16777232 | tf_op jit(solution)/shard_map/all_gather | solution.py:828
  272.2 17.5 %dispatch.2 = bf16[4,16,96,2048]{3,2,1,0:T(8,128)(2,1)} custom-call(bf16[16,384,256]{2,1,0:T(8,128)(2,1)} %fusion.5.pick_ref.refs_0_, bf16[16,256,2048]{2,1,0:T(8,128)(2,1)} %bitcast.121), custom_call_target="tpu_custom_call" | custom-call | flops 6442450944 | bytes 41943040 | tf_op jit(solution)/shard_map/dispatch/pallas_call | solution.py:671
  289.6 14.6 %fusion.58.u0_ref = f32[4,1536,256]{2,1,0:T(8,128)} fusion(bf16[4,1536,2048]{2,1,0:T(8,128)(2,1)} %bitcast.114, bf16[4,256,2048]{2,1,0:T(8,128)(2,1)} %w0_ref.1), kind=kOutput, calls=%fused_computation.112 | convolution fusion | flops 6442450944 | bytes 35651584 | tf_op jit(solution)/shard_map/emd,efd->emf/dot_general | solution.py:820
  304.2 14.5 %fusion.59.u1_ref = f32[4,1536,256]{2,1,0:T(8,128)} fusion(bf16[4,1536,2048]{2,1,0:T(8,128)(2,1)} %bitcast.115, bf16[4,256,2048]{2,1,0:T(8,128)(2,1)} %collective-permute-done.w1_ref), kind=kOutput, calls=%fused_computation.113 | convolution fusion | flops 6442450944 | bytes 35651584 | tf_op jit(solution)/shard_map/emd,efd->emf/dot_general | solution.py:820
  318.7 146.9 %all-gather.7.cloned.1.call-done = bf16[4096,2048]{1,0:T(8,128)(2,1)} async-done(((bf16[256,2048]{1,0:T(8,128)(2,1)}), bf16[4096,2048]{1,0:T(8,128)(2,1)}) %all-gather.7.cloned.1.call-update) | async-done | bytes 16777232 | tf_op jit(solution)/shard_map/all_gather | solution.py:828
  465.6 2.4 copy.47.pr_ref
  468.0 17.1 %dispatch.3 = bf16[4,16,96,2048]{3,2,1,0:T(8,128)(2,1)} custom-call(bf16[16,384,256]{2,1,0:T(8,128)(2,1)} %fusion.5.pick_ref.refs_0_, bf16[16,256,2048]{2,1,0:T(8,128)(2,1)} %bitcast.122), custom_call_target="tpu_custom_call" | custom-call | flops 6442450944 | bytes 41943040 | tf_op jit(solution)/shard_map/dispatch/pallas_call | solution.py:671
  485.0 63.4 %expert.1 = (bf16[4,1536,2048]{2,1,0:T(8,128)(2,1)}, f32[4,1536,1]{2,1,0:T(8,128)}, bf16[4,1536,256]{2,1,0:T(8,128)(2,1)}, bf16[4,1536,256]{2,1,0:T(8,128)(2,1)}...) custom-call(bf16[4,1536,2048]{2,1,0:T(8,128)(2,1)} %bitcast.117, bf16[4,2048,512]{2,1,0:T(8,128)(2,1)} %reshape.159.w0_ref, ...), custom_call_target="tpu_custom_call" | custom-call | flops 51539607552 | bytes 98566144 | tf_op jit(solution)/shard_map/expert/pallas_call | solution.py:780
  548.4 2.8 reduce
  551.3 3.3 select_reduce_fusion.v_ref
  554.5 9.1 spread.5
  563.6 0.9 bitcast_reduce_fusion
  564.5 176.7 %plane_reduce.2 = (f32[256,2048]{1,0:T(8,128)}, f32[4,2048,512]{2,1,0:T(8,128)}, bf16[4,2048,512]{2,1,0:T(8,128)(2,1)}, f32[4,256,2048]{2,1,0:T(8,128)}, bf16[4,256,2048]{2,1,0:T(8,128)(2,1)}) custom-call(bf16[16,384,256]{2,1,0:T(8,128)(2,1)} %fusion.5.pick_ref.refs_0_, bf16[4,16,96,2048]{3,2,1,0:T(8,128)(2,1)} %bitcast.120, ...), custom_call_target="tpu_custom_call" | custom-call | tf_op jit(solution)/shard_map/plane_reduce/pallas_call | solution.py:444
  741.3 4.0 multiply_reduce_fusion
  745.3 2.4 fusion.55
  747.8 26.8 %down_rows.1 = bf16[4,1536,2048]{2,1,0:T(8,128)(2,1)} custom-call(bf16[4,1536,256]{2,1,0:T(8,128)(2,1)} %get-tuple-element.40.refs_3_.h0_ref, bf16[4,1536,256]{2,1,0:T(8,128)(2,1)} %get-tuple-element.41.refs_4_.h1_ref, bf16[4,256,2048]{2,1,0:T(8,128)(2,1)} %w0_ref.1, bf16[4,256,2048]{2,1,0:T(8,128)(2,1)} %collective-permute-done.w1_ref), custom_call_target="tpu_custom_call" | custom-call | flops 12884901888 | bytes 33554432 | tf_op jit(solution)/shard_map/down_rows/pallas_call | solution.py:738
  774.6 22.5 %all-gather.11.cloned.1.call-done = bf16[1024,2048]{1,0:T(8,128)(2,1)} async-done(((bf16[256,2048]{1,0:T(8,128)(2,1)}), bf16[1024,2048]{1,0:T(8,128)(2,1)}) %all-gather.11.cloned.1.call-update) | async-done | bytes 4194320 | tf_op jit(solution)/shard_map/all_gather | solution.py:828
  797.1 5.9 convolution_convert_fusion.1
  803.0 5.5 convolution_convert_fusion.5.go_ref
  808.5 30.6 %attention.3 = (bf16[1024,512]{1,0:T(8,128)(2,1)}, bf16[1024,512]{1,0:T(8,128)(2,1)}, bf16[1024,512]{1,0:T(8,128)(2,1)}, f32[1,128]{1,0:T(1,128)}, f32[1,128]{1,0:T(1,128)}) custom-call(f32[1024,512]{1,0:T(8,128)} %fusion.19.q_ref, f32[1024,512]{1,0:T(8,128)} %fusion.21.k_ref, f32[1024,512]{1,0:T(8,128)} %fusion.22.v_ref, ...), custom_call_target="tpu_custom_call" | custom-call | flops 5368709120 | bytes 8388608 | tf_op jit(solution)/shard_map/attention/pallas_call | solution.py:636
  839.1 4.4 fusion.20
  843.5 4.0 fusion.18
  847.5 6.2 add_convert_fusion
  855.0 5.5 fusion.9
  860.5 2.7 fusion.10
  863.2 2.7 fusion.11
  865.9 3.4 pad_maximum_fusion
  871.2 5.5 collective-permute-done.3
  876.7 9.6 convert_add_fusion.1
  886.3 14.0 %convert_add_fusion = f32[4,2048,512]{2,1,0:T(8,128)} fusion(f32[4,2048,512]{2,1,0:T(8,128)} %get-tuple-element.55, bf16[4,2048,512]{2,1,0:T(8,128)(2,1)} %collective-permute-done.2), kind=kLoop, calls=%fused_computation | loop fusion | flops 8388608 | bytes 41943040 | tf_op jit(solution)/shard_map/add | solution.py:952
  900.3 20.1 %reshape.168 = f32[4,2048,2,256]{3,2,1,0:T(2,128)} reshape(f32[4,2048,512]{2,1,0:T(8,128)} %convert_add_fusion) | data formatting | bytes 33554432 | tf_op jit(solution)/shard_map/reshape | solution.py:954
  920.3 1.8 convert_element_type.106
  922.1 2.0 fusion.16
  924.2 0.8 pad.4
  925.0 20.0 %spread.6 = f32[32,24,128]{2,1,0:T(8,128)} custom-call(f32[32,24,128]{2,1,0:T(8,128)} %bitcast.124), custom_call_target="tpu_custom_call" | custom-call | tf_op jit(solution)/shard_map/spread/pallas_call | solution.py:107
  944.9 1.6 reduce_sum.152.v_ref
  946.6 25.0 %spread.7 = f32[32,24,128]{2,1,0:T(8,128)} custom-call(f32[24,128]{1,0:T(8,128)} %reduce_sum.152.v_ref), custom_call_target="tpu_custom_call" | custom-call | tf_op jit(solution)/shard_map/spread/pallas_call | solution.py:107
  971.6 197.0 %plane_reduce.3 = f32[256,2048]{1,0:T(8,128)} custom-call(bf16[16,384,256]{2,1,0:T(8,128)(2,1)} %fusion.5.pick_ref.refs_0_, bf16[4,16,96,2048]{3,2,1,0:T(8,128)(2,1)} %bitcast.119), custom_call_target="tpu_custom_call" | custom-call | tf_op jit(solution)/shard_map/plane_reduce/pallas_call | solution.py:444
  1168.5 0.7 slice.41
  1169.3 1.7 slice.42
  1172.1 3.5 add_convert_fusion.1
  1175.5 2.0 fusion.14
  1177.5 2.5 convert_bitcast_fusion
  (125 shorter events, 10.5 us)
Async XLA Ops:
  7.2 79.0 %copy-start = (bf16[512,2048]{1,0:T(8,128)(2,1)S(1)}, bf16[512,2048]{1,0:T(8,128)(2,1)}, u32[]{:S(2)}) copy-start(bf16[512,2048]{1,0:T(8,128)(2,1)} %param.20) | copy-start | bytes 6291460
  7.2 8.9 copy-start.24
  7.2 8.9 copy-start.25
  7.2 39.6 %all-gather.5.cloned.1.call-start = ((), (), s32[]{:S(2)}) async-start(), calls=%async_computation.3 | async-start | bytes 5242880 | tf_op jit(solution)/shard_map/all_gather | solution.py:828
  7.9 264.2 %all-gather.9.cloned.1.call-start = ((), (), s32[]{:S(2)}) async-start(), calls=%async_computation.5 | async-start | bytes 17825792 | tf_op jit(solution)/shard_map/all_gather | solution.py:828
  8.7 456.9 %all-gather.7.cloned.1.call-start = ((), (), s32[]{:S(2)}) async-start(), calls=%async_computation.4 | async-start | bytes 17825792 | tf_op jit(solution)/shard_map/all_gather | solution.py:828
  9.4 50.2 %copy-start.17 = (f32[2048]{0:T(1024)}, f32[2048]{0:T(1024)S(1)}, u32[]{:S(2)}) copy-start(f32[2048]{0:T(1024)S(1)} %convert_element_type.87) | copy-start | bytes 24580
  11.0 39.0 %copy-start.19 = (s32[1024]{0:T(1024)}, s32[1024]{0:T(1024)S(1)}, u32[]{:S(2)}) copy-start(s32[1024]{0:T(1024)S(1)} %convert_reduce_fusion) | copy-start | bytes 12292
  46.8 3.4 copy-start.10
  46.8 9.2 slice-start
  50.0 9.6 copy-start.22
  50.2 5.7 slice-start.1
  91.8 51.5 %copy-start.3 = (bf16[256,2048]{1,0:T(8,128)(2,1)S(1)}, bf16[256,2048]{1,0:T(8,128)(2,1)}, u32[]{:S(2)}) copy-start(bf16[256,2048]{1,0:T(8,128)(2,1)} %param.13) | copy-start | bytes 3145732
  146.0 1.3 copy-start.1
  148.5 15.0 %copy-start.20 = (s32[256,8]{0,1:T(8,128)S(1)}, s32[256,8]{0,1:T(8,128)}, u32[]{:S(2)}) copy-start(s32[256,8]{0,1:T(8,128)} %param.14) | copy-start | bytes 24580
  148.5 15.0 %copy-start.5 = (bf16[256,2048]{1,0:T(8,128)(2,1)S(1)}, bf16[256,2048]{1,0:T(8,128)(2,1)}, u32[]{:S(2)}) copy-start(bf16[256,2048]{1,0:T(8,128)(2,1)} %multiply_convert_fusion) | copy-start | bytes 3145732
  148.5 15.0 %copy-start.16 = (bf16[2048,32]{0,1:T(8,128)(2,1)S(1)}, bf16[2048,32]{0,1:T(8,128)(2,1)}, u32[]{:S(2)}) copy-start(bf16[2048,32]{0,1:T(8,128)(2,1)} %param.22) | copy-start | bytes 393220
  148.6 648.5 %all-gather.11.cloned.1.call-start = ((), (), s32[]{:S(2)}) async-start(), calls=%async_computation.6 | async-start | bytes 5242880 | tf_op jit(solution)/shard_map/all_gather | solution.py:828
  162.9 322.1 %collective-permute-start.1 = (bf16[4,2048,512]{2,1,0:T(8,128)(2,1)}, bf16[4,2048,512]{2,1,0:T(8,128)(2,1)}, u32[]{:S(2)}, u32[]{:S(2)}) collective-permute-start(bf16[4,2048,512]{2,1,0:T(8,128)(2,1)} %reshape.159.w0_ref), channel_id=1, source_target_pairs={{0,1},{1,0},{2,3},{3,2},{4,5},{5,4},{6,7},{7,6},{8,9},{9,8},{10,11... | collective-permute-start | bytes 25165832 | tf_op jit(solution)/shard_map/ppermute | solution.py:824
  162.9 141.3 %collective-permute-start = (bf16[4,256,2048]{2,1,0:T(8,128)(2,1)}, bf16[4,256,2048]{2,1,0:T(8,128)(2,1)}, u32[]{:S(2)}, u32[]{:S(2)}) collective-permute-start(bf16[4,256,2048]{2,1,0:T(8,128)(2,1)} %w0_ref.1), channel_id=1, source_target_pairs={{0,1},{1,0},{2,3},{3,2},{4,5},{5,4},{6,7},{7,6},{8,9},{9,8},{10,11... | collective-permute-start | bytes 12582920 | tf_op jit(solution)/shard_map/ppermute | solution.py:824
  741.2 4.0 copy-start.2
  741.2 4.0 copy-start.8
  741.3 4.0 copy-start.9
  747.7 49.3 %copy-start.14 = (bf16[1024,512]{1,0:T(8,128)(2,1)S(1)}, bf16[1024,512]{1,0:T(8,128)(2,1)}, u32[]{:S(2)}) copy-start(bf16[1024,512]{1,0:T(8,128)(2,1)} %attention.2) | copy-start | bytes 3145732
  747.7 172.6 %reduce-scatter.8.cloned.1.call-start = ((), (), s32[]{:S(2)}) async-start(), calls=%async_computation.9 | async-start | bytes 2359296 | tf_op jit(solution)/shard_map/reduce_scatter | solution.py:832
  802.9 119.2 %reduce-scatter.4.cloned.1.call-start = ((), (), s32[]{:S(2)}) async-start(), calls=%async_computation.7 | async-start | bytes 5242880 | tf_op jit(solution)/shard_map/reduce_scatter | solution.py:832
  839.1 4.4 copy-start.29
  853.8 0.7 copy-start.18
  853.8 0.7 copy-start.23
  853.8 1.2 copy-start.30
  853.8 323.7 %reduce-scatter.6.cloned.1.call-start = ((), (), s32[]{:S(2)}) async-start(), calls=%async_computation.8 | async-start | bytes 7077888 | tf_op jit(solution)/shard_map/reduce_scatter | solution.py:832
  854.1 6.4 copy-start.11
  854.1 6.4 copy-start.28
  854.1 32.2 %collective-permute-start.2 = (bf16[4,2048,512]{2,1,0:T(8,128)(2,1)}, bf16[4,2048,512]{2,1,0:T(8,128)(2,1)}, u32[]{:S(2)}, u32[]{:S(2)}) collective-permute-start(bf16[4,2048,512]{2,1,0:T(8,128)(2,1)} %get-tuple-element.56), channel_id=1, source_target_pairs={{0,1},{1,0},{2,3},{3,2},{4,5},{5,4},{6,7},{7,6},{8,9},{9,8},{10,11... | collective-permute-start | bytes 25165832 | tf_op jit(solution)/shard_map/ppermute | solution.py:824
  860.5 2.7 copy-start.15
  869.2 0.7 copy-start.21
  869.2 1.2 copy-start.6
  869.3 7.4 collective-permute-start.3
  900.3 21.9 %copy-start.4 = (bf16[256,2048]{1,0:T(8,128)(2,1)S(1)}, bf16[256,2048]{1,0:T(8,128)(2,1)}, u32[]{:S(2)}) copy-start(bf16[256,2048]{1,0:T(8,128)(2,1)} %param.13) | copy-start | bytes 3145732
  900.3 23.9 %copy-start.27 = (f32[1,128]{1,0:T(1,128)S(1)}, f32[1,128]{1,0:T(1,128)}, u32[]{:S(2)}) copy-start(f32[1,128]{1,0:T(1,128)} %get-tuple-element.51) | copy-start | bytes 1540
  900.3 23.9 %copy-start.26 = (f32[1,128]{1,0:T(1,128)S(1)}, f32[1,128]{1,0:T(1,128)}, u32[]{:S(2)}) copy-start(f32[1,128]{1,0:T(1,128)} %get-tuple-element.52) | copy-start | bytes 1540
  971.6 197.0 %copy-start.13 = (f32[32,24,128]{2,1,0:T(8,128)S(1)}, f32[32,24,128]{2,1,0:T(8,128)}, u32[]{:S(2)}) copy-start(f32[32,24,128]{2,1,0:T(8,128)} %spread.7) | copy-start | bytes 1179652
  1171.0 4.6 copy-start.7
  1171.0 4.6 copy-start.12
Sparse Core Ops, SparseCore 0:
  9.6 37.1 all-gather.4
  49.6 222.5 all-gather.8
  275.5 190.0 all-gather.6
  747.8 49.1 all-gather.10
  803.1 68.8 reduce-scatter.7
  874.4 43.5 reduce-scatter.3
  921.6 158.8 reduce-scatter.5

commit v6 on v5

--- a/solution.py
+++ b/solution.py
@@ -538,6 +538,68 @@
     )(parts.reshape(2, 2, rows, columns))
 
 
+def group_gather_kernel(pieces, v_ref, out_ref, local_sem, s1, r1, s2, r2, s3, r3):
+    x, core = lax.axis_index("x"), lax.axis_index("core")
+    partner, across = {"core": 1 - core}, {"x": 1 - x}
+    greet(partner)
+    greet(across)
+    pl.semaphore_wait(pltpu.get_barrier_semaphore(), 2)
+    step = v_ref.shape[0] // pieces
+
+    def over(piece):
+        at = pl.ds(piece * step, step)
+        return remote(
+            v_ref.at[at, :], out_ref.at[x, core, at, :], s2.at[piece], r2.at[piece], across
+        )
+
+    def pass_on(piece):
+        ref = out_ref.at[1 - x, core, pl.ds(piece * step, step), :]
+        return remote(ref, ref, s3.at[piece], r3.at[piece], partner)
+
+    direct = remote(v_ref, out_ref.at[x, core], s1, r1, partner)
+    mine = pltpu.make_async_copy(v_ref, out_ref.at[x, core], local_sem)
+    for piece in range(pieces):
+        over(piece).start()
+    direct.start()
+    mine.start()
+    for piece in range(pieces):
+        over(piece).wait()
+        pass_on(piece).start()
+    mine.wait()
+    direct.wait()
+    for piece in range(pieces):
+        pass_on(piece).wait()
+
+
+def group_gather(value, collective_id):
+    if lax.axis_size("x") != 2:
+        return gather(value, GROUP)
+    rows, columns = value.shape
+    pieces = 4
+
+    def sems(*lead):
+        return pltpu.SemaphoreType.DMA(lead)
+
+    gathered = pl.pallas_call(
+        functools.partial(group_gather_kernel, pieces),
+        out_shape=jax.ShapeDtypeStruct((2, 2, rows, columns), value.dtype),
+        in_specs=[pl.BlockSpec(memory_space=pltpu.VMEM)],
+        out_specs=pl.BlockSpec(memory_space=pltpu.VMEM),
+        scratch_shapes=[
+            pltpu.SemaphoreType.DMA,
+            pltpu.SemaphoreType.DMA,
+            pltpu.SemaphoreType.DMA,
+            sems(pieces),
+            sems(pieces),
+            sems(pieces),
+            sems(pieces),
+        ],
+        compiler_params=pltpu.CompilerParams(collective_id=collective_id, has_side_effects=True),
+        name="group_gather",
+    )(value)
+    return gathered.reshape(4 * rows, columns)
+
+
 def turn(value, cosine, sine):
     return value * cosine + pltpu.roll(value, value.shape[-1] // 2, 1) * sine
 
@@ -877,7 +939,7 @@
     gain_two = norm2_gain.astype(F32)
     inputs = layer_input.astype(F32)
     grad_out = d_out.astype(F32)
-    input_seq = gather(layer_input, GROUP)
+    input_seq = group_gather(layer_input, 8)
     g_flat = gather(d_out, PLANE)
     h_seq = norm_rows(input_seq.astype(F32), gain_one).astype(BF16)
     w_parts = w_qkv.transpose(1, 0, 2)
@@ -951,7 +1013,6 @@
 
     grad_pair = grad_pair_own + swap_cores(grad_pair_other).astype(F32)
     grad_down = grad_down_own + swap_cores(grad_down_other).astype(F32)
-    grad_gate_up = grad_pair.reshape(local, width, 2, hidden_local)
 
     inner = jnp.sum(probs_own * grad_probs, axis=-1, keepdims=True)
     grad_logits = probs_own * (grad_probs - inner)
@@ -965,7 +1026,10 @@
     grad_mid = grad_out + grad_mid_norm
 
     ga_seq = gather(grad_mid.astype(BF16), GROUP)
-    ga_seq, out_rows = lax.optimization_barrier((ga_seq, out_rows))
+    ga_seq, out_rows, grad_down, grad_pair = lax.optimization_barrier(
+        (ga_seq, out_rows, grad_down, grad_pair)
+    )
+    grad_gate_up = grad_pair.reshape(local, width, 2, hidden_local)
     grad_wout = lax.dot_general(
         attn_vals, ga_seq, (((0,), (0,)), ((), ())), preferred_element_type=F32
     )

time: 1210 us -> 1170 us (0.967)
  waiting for transfers between devices: 285 us -> 216 us
  Pallas kernels: 681 us -> 714 us
    all_gather x4 -> x3, waiting for transfers between devices: 278 us -> 191 us  [gather(): return lax.all_gather(value, axes, axis=0, tiled=True)]
    pallas_call x0 -> x1, Pallas kernels: none -> 38.9 us  [group_gather(): pl.pallas_call(functools.partial(group_gather_kernel, pieces), out_shape=...]
    reduce_scatter x3, waiting for transfers between devices: 0.01 us -> 24.1 us  [scatter(): return lax.psum_scatter(value, axes, scatter_dimension=dim, tiled=True)]
    pallas_call x1, Pallas kernels: 51.5 us -> 39.3 us  [group_reduce(): pl.pallas_call(functools.partial(group_kernel, pieces), out_shape=jax.Sha...]
  transfers between devices with their start and end apart: 11 -> 10, of which waited for: 5 -> 3; matrix products, arithmetic and copies ran while one was open for 15% -> 17% of each run, Pallas kernels for 36% -> 41%
where the time goes in v6:
time: 1170 us; the launch traced here: 1150 us
  Pallas kernels  714 us (61%)
  waiting for transfers between devices  216 us (18%)
  matrix products  84.2 us (7%)
  other arithmetic  72.2 us (6%)
  local copies, waits for them, and re-layouts  46.7 us (4%)
  between operations  15.1 us (1%)
    pallas_call x2, Pallas kernels, plane_reduce(): pl.pallas_call(functools.partial(reduce_kernel, depth, half, bool(factors...  376 us
    all_gather x3, waiting for transfers between devices, gather(): return lax.all_gather(value, axes, axis=0, tiled=True)  191 us
    pallas_call x4, Pallas kernels, spread(): pl.pallas_call(functools.partial(spread_kernel, axes, counts, own_slices)...  82.3 us
    pallas_call x1, Pallas kernels, expert(): pl.pallas_call(expert_kernel, grid=(local, count // step), out_shape=[s(w...  63.3 us
    pallas_call x2, Pallas kernels, attention_call(): pl.pallas_call(functools.partial(kernel, min(512, seq_len)), grid=(heads,...  53.2 us
    pallas_call x1, Pallas kernels, group_reduce(): pl.pallas_call(functools.partial(group_kernel, pieces), out_shape=jax.Sha...  39.3 us
    pallas_call x1, Pallas kernels, group_gather(): pl.pallas_call(functools.partial(group_gather_kernel, pieces), out_shape=...  38.9 us
    pallas_call x2, Pallas kernels, dispatch(): pl.pallas_call(dispatch_kernel, grid=(blocks // group,), out_shape=jax.Sh...  34.4 us
  transfers between devices with their start and end apart: 10, of which 3 were waited for; matrix products, arithmetic and copies ran while one was open for 17% of the time, Pallas kernels for 41%

profile of v6, /device:TPU:0, one launch (start us, length us, event | category | flops | bytes accessed | tf_op | source)
XLA Modules:
  0.0 1149.9 jit_solution(11927007667129916200)
XLA Ops:
  9.4 0.8 reduce-window.4
  10.3 1.0 copy.43.dr_ref
  11.3 38.9 %group_gather.1 = bf16[2,2,256,2048]{3,2,1,0:T(8,128)(2,1)} custom-call(bf16[256,2048]{1,0:T(8,128)(2,1)} %v_ref.1), custom_call_target="tpu_custom_call" | custom-call | tf_op jit(solution)/shard_map/group_gather/pallas_call | solution.py:583
  50.4 1.9 fusion.24
  52.3 1.3 pad_maximum_fusion.1
  54.2 0.9 multiply_reduce_fusion
  55.7 1.0 multiply_convert_fusion
  57.4 3.7 fusion.21.v_ref
  61.1 3.6 fusion.20.k_ref
  64.8 3.6 fusion.18.q_ref
  68.4 22.8 %attention.2 = bf16[1024,512]{1,0:T(8,128)(2,1)} custom-call(f32[1024,512]{1,0:T(8,128)} %fusion.18.q_ref, f32[1024,512]{1,0:T(8,128)} %fusion.20.k_ref, f32[1024,512]{1,0:T(8,128)} %fusion.21.v_ref, f32[1,128]{1,0:T(1,128)} %get-tuple-element.89.qg_ref, f32[1,128]{1,0:T(1,128)} %get-tuple-element.88.kg_ref, f32[1024,128]{1,0:T(8,128)} %get-tuple-element.86.cos_ref, ...), custom_call_target="tpu_custom_call" | custom-call | flops 2147483648 | bytes 8388608 | tf_op jit(solution)/shard_map/attention/pallas_call | solution.py:698
  91.2 5.6 convolution_convert_fusion
  96.8 39.3 %group_reduce.1 = f32[256,2048]{1,0:T(8,128)} custom-call(bf16[2,2,256,2048]{3,2,1,0:T(8,128)(2,1)} %bitcast.139), custom_call_target="tpu_custom_call" | custom-call | tf_op jit(solution)/shard_map/group_reduce/pallas_call | solution.py:518
  136.2 2.7 multiply_reduce_fusion.3
  138.9 1.3 copy-done.2
  140.2 1.2 multiply_convert_fusion.1
  141.5 14.3 %reshape.202.w0_ref = bf16[4,2048,512]{2,1,0:T(8,128)(2,1)} reshape(bf16[4,2048,2,256]{3,2,1,0:T(2,128)(2,1)} %param.23) | data formatting | bytes 16777216 | tf_op jit(solution)/shard_map/reshape | solution.py:972
  157.6 16.4 %spread.4 = f32[16,32,256]{2,1,0:T(8,128)} custom-call(f32[32,256]{1,0:T(8,128)} %fusion.36.v_ref), custom_call_target="tpu_custom_call" | custom-call | tf_op jit(solution)/shard_map/spread/pallas_call | solution.py:107
  174.0 0.9 broadcast_compare_fusion
  175.1 1.5 select_reduce_fusion.1
  176.7 2.7 fusion.4.pick_ref.refs_0_
  179.4 44.7 %all-gather.6.cloned.1.call-done = bf16[4096,2048]{1,0:T(8,128)(2,1)} async-done(((bf16[256,2048]{1,0:T(8,128)(2,1)}), bf16[4096,2048]{1,0:T(8,128)(2,1)}) %all-gather.6.cloned.1.call-update) | async-done | bytes 16777232 | tf_op jit(solution)/shard_map/all_gather | solution.py:890
  224.1 17.4 %dispatch.2 = bf16[4,16,96,2048]{3,2,1,0:T(8,128)(2,1)} custom-call(bf16[16,384,256]{2,1,0:T(8,128)(2,1)} %fusion.4.pick_ref.refs_0_, bf16[16,256,2048]{2,1,0:T(8,128)(2,1)} %bitcast.137), custom_call_target="tpu_custom_call" | custom-call | flops 6442450944 | bytes 41943040 | tf_op jit(solution)/shard_map/dispatch/pallas_call | solution.py:733
  241.5 14.6 %fusion.52.u0_ref = f32[4,1536,256]{2,1,0:T(8,128)} fusion(bf16[4,1536,2048]{2,1,0:T(8,128)(2,1)} %bitcast.130, bf16[4,256,2048]{2,1,0:T(8,128)(2,1)} %w0_ref.1), kind=kOutput, calls=%fused_computation.113 | convolution fusion | flops 6442450944 | bytes 35651584 | tf_op jit(solution)/shard_map/emd,efd->emf/dot_general | solution.py:882
  256.1 14.5 %fusion.53.u1_ref = f32[4,1536,256]{2,1,0:T(8,128)} fusion(bf16[4,1536,2048]{2,1,0:T(8,128)(2,1)} %bitcast.131, bf16[4,256,2048]{2,1,0:T(8,128)(2,1)} %collective-permute-done.w1_ref), kind=kOutput, calls=%fused_computation.114 | convolution fusion | flops 6442450944 | bytes 35651584 | tf_op jit(solution)/shard_map/emd,efd->emf/dot_general | solution.py:882
  270.6 146.7 %all-gather.4.cloned.1.call-done = bf16[4096,2048]{1,0:T(8,128)(2,1)} async-done(((bf16[256,2048]{1,0:T(8,128)(2,1)}), bf16[4096,2048]{1,0:T(8,128)(2,1)}) %all-gather.4.cloned.1.call-update) | async-done | bytes 16777232 | tf_op jit(solution)/shard_map/all_gather | solution.py:890
  417.3 2.4 copy.47.pr_ref
  419.7 17.0 %dispatch.3 = bf16[4,16,96,2048]{3,2,1,0:T(8,128)(2,1)} custom-call(bf16[16,384,256]{2,1,0:T(8,128)(2,1)} %fusion.4.pick_ref.refs_0_, bf16[16,256,2048]{2,1,0:T(8,128)(2,1)} %bitcast.138), custom_call_target="tpu_custom_call" | custom-call | flops 6442450944 | bytes 41943040 | tf_op jit(solution)/shard_map/dispatch/pallas_call | solution.py:733
  436.7 63.3 %expert.1 = (bf16[4,1536,2048]{2,1,0:T(8,128)(2,1)}, f32[4,1536,1]{2,1,0:T(8,128)}, bf16[4,1536,256]{2,1,0:T(8,128)(2,1)}, bf16[4,1536,256]{2,1,0:T(8,128)(2,1)}...) custom-call(bf16[4,1536,2048]{2,1,0:T(8,128)(2,1)} %bitcast.133, bf16[4,2048,512]{2,1,0:T(8,128)(2,1)} %reshape.202.w0_ref, ...), custom_call_target="tpu_custom_call" | custom-call | flops 51539607552 | bytes 98566144 | tf_op jit(solution)/shard_map/expert/pallas_call | solution.py:842
  500.0 180.0 %plane_reduce.2 = (f32[256,2048]{1,0:T(8,128)}, f32[4,2048,512]{2,1,0:T(8,128)}, bf16[4,2048,512]{2,1,0:T(8,128)(2,1)}, f32[4,256,2048]{2,1,0:T(8,128)}, bf16[4,256,2048]{2,1,0:T(8,128)(2,1)}) custom-call(bf16[16,384,256]{2,1,0:T(8,128)(2,1)} %fusion.4.pick_ref.refs_0_, bf16[4,16,96,2048]{3,2,1,0:T(8,128)(2,1)} %bitcast.136, ...), custom_call_target="tpu_custom_call" | custom-call | tf_op jit(solution)/shard_map/plane_reduce/pallas_call | solution.py:444
  680.2 2.8 reduce.1
  683.1 3.7 select_reduce_fusion.v_ref
  686.7 22.1 %spread.5 = f32[16,4,256]{2,1,0:T(4,128)} custom-call(f32[16,4,256]{2,1,0:T(4,128)} %select_reduce_fusion.v_ref), custom_call_target="tpu_custom_call" | custom-call | tf_op jit(solution)/shard_map/spread/pallas_call | solution.py:107
  708.9 0.9 bitcast_reduce_fusion
  709.9 4.0 multiply_reduce_fusion.1
  713.9 2.5 fusion.49
  716.5 27.0 %down_rows.1 = bf16[4,1536,2048]{2,1,0:T(8,128)(2,1)} custom-call(bf16[4,1536,256]{2,1,0:T(8,128)(2,1)} %get-tuple-element.42.refs_3_.h0_ref, bf16[4,1536,256]{2,1,0:T(8,128)(2,1)} %get-tuple-element.43.refs_4_.h1_ref, bf16[4,256,2048]{2,1,0:T(8,128)(2,1)} %w0_ref.1, bf16[4,256,2048]{2,1,0:T(8,128)(2,1)} %collective-permute-done.w1_ref), custom_call_target="tpu_custom_call" | custom-call | flops 12884901888 | bytes 33554432 | tf_op jit(solution)/shard_map/down_rows/pallas_call | solution.py:800
  743.5 10.1 convert_add_fusion.1
  753.6 14.0 %convert_add_fusion = f32[4,2048,512]{2,1,0:T(8,128)} fusion(f32[4,2048,512]{2,1,0:T(8,128)} %get-tuple-element.50, bf16[4,2048,512]{2,1,0:T(8,128)(2,1)} %collective-permute-done.3), kind=kLoop, calls=%fused_computation | loop fusion | flops 8388608 | bytes 41943040 | tf_op jit(solution)/shard_map/add | solution.py:1014
  767.6 5.9 convolution_convert_fusion.1
  773.6 5.5 convolution_convert_fusion.5.go_ref
  779.1 30.4 %attention.3 = (bf16[1024,512]{1,0:T(8,128)(2,1)}, bf16[1024,512]{1,0:T(8,128)(2,1)}, bf16[1024,512]{1,0:T(8,128)(2,1)}, f32[1,128]{1,0:T(1,128)}, f32[1,128]{1,0:T(1,128)}) custom-call(f32[1024,512]{1,0:T(8,128)} %fusion.18.q_ref, f32[1024,512]{1,0:T(8,128)} %fusion.20.k_ref, f32[1024,512]{1,0:T(8,128)} %fusion.21.v_ref, ...), custom_call_target="tpu_custom_call" | custom-call | flops 5368709120 | bytes 8388608 | tf_op jit(solution)/shard_map/attention/pallas_call | solution.py:698
  809.5 4.4 fusion.19
  813.9 4.0 fusion.17
  817.9 6.3 add_convert_fusion
  824.9 3.5 fusion.1
  828.4 2.4 fusion.8
  830.9 2.4 fusion.9
  833.3 2.4 fusion.10
  835.8 3.1 pad_maximum_fusion
  840.9 20.4 %reshape.211 = f32[4,2048,2,256]{3,2,1,0:T(2,128)} reshape(f32[4,2048,512]{2,1,0:T(8,128)} %convert_add_fusion) | data formatting | bytes 33554432 | tf_op jit(solution)/shard_map/reshape | solution.py:1032
  861.3 1.8 convert_element_type.128
  863.1 24.1 %reduce-scatter.4.cloned.1.call-done = bf16[256,2048]{1,0:T(8,128)(2,1)} async-done(((bf16[1024,2048]{1,0:T(8,128)(2,1)}), bf16[256,2048]{1,0:T(8,128)(2,1)}) %reduce-scatter.4.cloned.1.call-update) | async-done | bytes 1048592 | tf_op jit(solution)/shard_map/reduce_scatter | solution.py:894
  887.1 2.0 fusion.15
  889.2 0.8 pad.4
  890.0 18.4 %spread.6 = f32[32,24,128]{2,1,0:T(8,128)} custom-call(f32[32,24,128]{2,1,0:T(8,128)} %bitcast.143), custom_call_target="tpu_custom_call" | custom-call | tf_op jit(solution)/shard_map/spread/pallas_call | solution.py:107
  908.4 1.6 reduce_sum.152.v_ref
  910.0 25.4 %spread.7 = f32[32,24,128]{2,1,0:T(8,128)} custom-call(f32[24,128]{1,0:T(8,128)} %reduce_sum.152.v_ref), custom_call_target="tpu_custom_call" | custom-call | tf_op jit(solution)/shard_map/spread/pallas_call | solution.py:107
  935.5 195.6 %plane_reduce.3 = f32[256,2048]{1,0:T(8,128)} custom-call(bf16[16,384,256]{2,1,0:T(8,128)(2,1)} %fusion.4.pick_ref.refs_0_, bf16[4,16,96,2048]{3,2,1,0:T(8,128)(2,1)} %bitcast.135), custom_call_target="tpu_custom_call" | custom-call | tf_op jit(solution)/shard_map/plane_reduce/pallas_call | solution.py:444
  1131.1 0.7 slice.41
  1131.8 1.7 slice.42
  1134.7 3.5 add_convert_fusion.1
  1138.1 2.0 fusion.13
  1140.1 2.5 convert_bitcast_fusion
  (124 shorter events, 10.6 us)
Async XLA Ops:
  7.2 84.1 %copy-start = (bf16[512,2048]{1,0:T(8,128)(2,1)S(1)}, bf16[512,2048]{1,0:T(8,128)(2,1)}, u32[]{:S(2)}) copy-start(bf16[512,2048]{1,0:T(8,128)(2,1)} %param.20) | copy-start | bytes 6291460
  7.2 43.1 %copy-start.24 = (s32[1,4]{1,0:T(1,128)S(1)}, s32[1,4]{1,0:T(1,128)}, u32[]{:S(2)}) copy-start(s32[1,4]{1,0:T(1,128)} %param.15) | copy-start | bytes 52
  7.2 216.9 %all-gather.6.cloned.1.call-start = ((), (), s32[]{:S(2)}) async-start(), calls=%async_computation.4 | async-start | bytes 17825792 | tf_op jit(solution)/shard_map/all_gather | solution.py:890
  7.9 409.4 %all-gather.4.cloned.1.call-start = ((), (), s32[]{:S(2)}) async-start(), calls=%async_computation.3 | async-start | bytes 17825792 | tf_op jit(solution)/shard_map/all_gather | solution.py:890
  8.7 47.0 %copy-start.16 = (f32[2048]{0:T(1024)}, f32[2048]{0:T(1024)S(1)}, u32[]{:S(2)}) copy-start(f32[2048]{0:T(1024)S(1)} %convert_element_type.103) | copy-start | bytes 24580
  10.3 43.4 %copy-start.18 = (s32[1024]{0:T(1024)}, s32[1024]{0:T(1024)S(1)}, u32[]{:S(2)}) copy-start(s32[1024]{0:T(1024)S(1)} %convert_reduce_fusion) | copy-start | bytes 12292
  11.3 42.3 %copy-start.22 = (bf16[128]{0:T(256)(128)(2,1)S(1)}, bf16[128]{0:T(256)(128)(2,1)}, u32[]{:S(2)}) copy-start(bf16[128]{0:T(256)(128)(2,1)} %param.19) | copy-start | bytes 772
  11.3 42.3 %copy-start.23 = (bf16[128]{0:T(256)(128)(2,1)S(1)}, bf16[128]{0:T(256)(128)(2,1)}, u32[]{:S(2)}) copy-start(bf16[128]{0:T(256)(128)(2,1)} %param.18) | copy-start | bytes 772
  50.3 3.9 copy-start.1
  54.2 2.6 slice-start
  55.7 1.8 slice-start.1
  96.8 39.4 %copy-start.4 = (bf16[256,2048]{1,0:T(8,128)(2,1)S(1)}, bf16[256,2048]{1,0:T(8,128)(2,1)}, u32[]{:S(2)}) copy-start(bf16[256,2048]{1,0:T(8,128)(2,1)} %v_ref.1) | copy-start | bytes 3145732
  138.9 1.3 copy-start.2
  141.4 15.0 %copy-start.20 = (s32[256,8]{0,1:T(8,128)S(1)}, s32[256,8]{0,1:T(8,128)}, u32[]{:S(2)}) copy-start(s32[256,8]{0,1:T(8,128)} %param.14) | copy-start | bytes 24580
  141.4 15.0 %copy-start.6 = (bf16[256,2048]{1,0:T(8,128)(2,1)S(1)}, bf16[256,2048]{1,0:T(8,128)(2,1)}, u32[]{:S(2)}) copy-start(bf16[256,2048]{1,0:T(8,128)(2,1)} %multiply_convert_fusion.1) | copy-start | bytes 3145732
  141.4 15.0 %copy-start.15 = (bf16[2048,32]{0,1:T(8,128)(2,1)S(1)}, bf16[2048,32]{0,1:T(8,128)(2,1)}, u32[]{:S(2)}) copy-start(bf16[2048,32]{0,1:T(8,128)(2,1)} %param.22) | copy-start | bytes 393220
  141.5 626.2 %all-gather.8.cloned.1.call-start = ((), (), s32[]{:S(2)}) async-start(), calls=%async_computation.5 | async-start | bytes 5242880 | tf_op jit(solution)/shard_map/all_gather | solution.py:890
  155.8 280.9 %collective-permute-start.1 = (bf16[4,2048,512]{2,1,0:T(8,128)(2,1)}, bf16[4,2048,512]{2,1,0:T(8,128)(2,1)}, u32[]{:S(2)}, u32[]{:S(2)}) collective-permute-start(bf16[4,2048,512]{2,1,0:T(8,128)(2,1)} %reshape.202.w0_ref), channel_id=1, source_target_pairs={{0,1},{1,0},{2,3},{3,2},{4,5},{5,4},{6,7},{7,6},{8,9},{9,8},{10,11... | collective-permute-start | bytes 25165832 | tf_op jit(solution)/shard_map/ppermute | solution.py:886
  155.8 100.3 %collective-permute-start = (bf16[4,256,2048]{2,1,0:T(8,128)(2,1)}, bf16[4,256,2048]{2,1,0:T(8,128)(2,1)}, u32[]{:S(2)}, u32[]{:S(2)}) collective-permute-start(bf16[4,256,2048]{2,1,0:T(8,128)(2,1)} %w0_ref.1), channel_id=1, source_target_pairs={{0,1},{1,0},{2,3},{3,2},{4,5},{5,4},{6,7},{7,6},{8,9},{9,8},{10,11... | collective-permute-start | bytes 12582920 | tf_op jit(solution)/shard_map/ppermute | solution.py:886
  680.1 73.5 %collective-permute-start.3 = (bf16[4,2048,512]{2,1,0:T(8,128)(2,1)}, bf16[4,2048,512]{2,1,0:T(8,128)(2,1)}, u32[]{:S(2)}, u32[]{:S(2)}) collective-permute-start(bf16[4,2048,512]{2,1,0:T(8,128)(2,1)} %get-tuple-element.51), channel_id=1, source_target_pairs={{0,1},{1,0},{2,3},{3,2},{4,5},{5,4},{6,7},{7,6},{8,9},{9,8},{10,11... | collective-permute-start | bytes 25165832 | tf_op jit(solution)/shard_map/ppermute | solution.py:886
  682.9 31.0 %copy-start.10 = (bf16[256,2048]{1,0:T(8,128)(2,1)S(1)}, bf16[256,2048]{1,0:T(8,128)(2,1)}, u32[]{:S(2)}) copy-start(bf16[256,2048]{1,0:T(8,128)(2,1)} %param.25) | copy-start | bytes 3145732
  709.8 4.2 copy-start.3
  709.8 4.2 copy-start.9
  709.8 33.7 %collective-permute-start.2 = (bf16[4,256,2048]{2,1,0:T(8,128)(2,1)}, bf16[4,256,2048]{2,1,0:T(8,128)(2,1)}, u32[]{:S(2)}, u32[]{:S(2)}) collective-permute-start(bf16[4,256,2048]{2,1,0:T(8,128)(2,1)} %get-tuple-element.49), channel_id=1, source_target_pairs={{0,1},{1,0},{2,3},{3,2},{4,5},{5,4},{6,7},{7,6},{8,9},{9,8},{10,11... | collective-permute-start | bytes 12582920 | tf_op jit(solution)/shard_map/ppermute | solution.py:886
  716.4 144.9 %reduce-scatter.8.cloned.1.call-start = ((), (), s32[]{:S(2)}) async-start(), calls=%async_computation.8 | async-start | bytes 2359296 | tf_op jit(solution)/shard_map/reduce_scatter | solution.py:894
  753.6 14.0 %copy-start.13 = (bf16[1024,512]{1,0:T(8,128)(2,1)S(1)}, bf16[1024,512]{1,0:T(8,128)(2,1)}, u32[]{:S(2)}) copy-start(bf16[1024,512]{1,0:T(8,128)(2,1)} %attention.2) | copy-start | bytes 3145732
  773.5 113.6 %reduce-scatter.4.cloned.1.call-start = ((), (), s32[]{:S(2)}) async-start(), calls=%async_computation.6 | async-start | bytes 5242880 | tf_op jit(solution)/shard_map/reduce_scatter | solution.py:894
  809.5 4.4 copy-start.28
  824.2 0.7 copy-start.19
  824.2 0.7 copy-start.17
  824.2 315.9 %reduce-scatter.6.cloned.1.call-start = ((), (), s32[]{:S(2)}) async-start(), calls=%async_computation.7 | async-start | bytes 7077888 | tf_op jit(solution)/shard_map/reduce_scatter | solution.py:894
  824.9 3.5 copy-start.29
  828.4 2.5 copy-start.27
  830.9 2.5 copy-start.14
  838.9 0.7 copy-start.21
  838.9 1.2 copy-start.7
  840.8 46.3 %copy-start.5 = (bf16[256,2048]{1,0:T(8,128)(2,1)S(1)}, bf16[256,2048]{1,0:T(8,128)(2,1)}, u32[]{:S(2)}) copy-start(bf16[256,2048]{1,0:T(8,128)(2,1)} %v_ref.1) | copy-start | bytes 3145732
  840.8 48.4 %copy-start.26 = (f32[1,128]{1,0:T(1,128)S(1)}, f32[1,128]{1,0:T(1,128)}, u32[]{:S(2)}) copy-start(f32[1,128]{1,0:T(1,128)} %get-tuple-element.57) | copy-start | bytes 1540
  840.8 48.4 %copy-start.25 = (f32[1,128]{1,0:T(1,128)S(1)}, f32[1,128]{1,0:T(1,128)}, u32[]{:S(2)}) copy-start(f32[1,128]{1,0:T(1,128)} %get-tuple-element.58) | copy-start | bytes 1540
  935.4 195.7 %copy-start.12 = (f32[32,24,128]{2,1,0:T(8,128)S(1)}, f32[32,24,128]{2,1,0:T(8,128)}, u32[]{:S(2)}) copy-start(f32[32,24,128]{2,1,0:T(8,128)} %spread.7) | copy-start | bytes 1179652
  1133.5 4.6 copy-start.8
  1133.5 4.6 copy-start.11
Sparse Core Ops, SparseCore 0:
  10.8 213.3 all-gather.5
  227.5 189.7 all-gather.3
  716.5 33.0 all-gather.7
  773.7 67.3 reduce-scatter.7
  843.5 43.6 reduce-scatter.3
  890.6 156.8 reduce-scatter.5

commit v7 on v6

--- a/solution.py
+++ b/solution.py
@@ -199,7 +199,7 @@
     return run, tiles
 
 
-def reduce_kernel(depth, half, filled, *refs):
+def reduce_kernel(depth, half, sides, filled, *refs):
     refs = list(refs)
 
     def take(count):
@@ -259,7 +259,7 @@
         for copy in fetch(number, slot):
             copy.wait()
         level, kind = place(number)
-        for side in (0, 1):
+        for side in range(sides):
             picked = value[slot, :, :, side * half : (side + 1) * half]
             picked = picked.reshape(local * capacity, half)
             part[level, kind, side] = dot_tn(pick[slot], picked).astype(BF16)
@@ -303,7 +303,7 @@
     def open_turn(turn, carry):
         compute(turn)
         level = level_of(turn)
-        for side in (0, 1):
+        for side in range(sides):
             send_one(side, level, 0).start()
         return carry
 
@@ -312,7 +312,7 @@
     def turn_one(turn, carry):
         lax.fori_loop(0, 3, lambda k, c: (compute(depth + turn * 3 + k), c)[1], 0)
         level = level_of(turn)
-        for side in (0, 1):
+        for side in range(sides):
             send_one(side, level, 0).wait()
             arrived = one.at[side, level, 0]
             add_into(arrived, [arrived, part.at[level, 2 - side, side]])
@@ -326,7 +326,7 @@
     lax.fori_loop(0, depth, turn_one, 0)
 
     def begin(level):
-        for side in (0, 1):
+        for side in range(sides):
             if level > 0:
 
                 @pl.when(z == 0)
@@ -342,7 +342,7 @@
                     go_left(side, level).start()
 
     def forward(level):
-        for side in (0, 1):
+        for side in range(sides):
 
             @pl.when((z > 0) & (z < level))
             def _():
@@ -360,7 +360,7 @@
 
     order = visiting_order(depth)
     for turn, level in enumerate(order):
-        for side in (0, 1):
+        for side in range(sides):
             send_one(side, level, 1).wait()
             kept = part.at[level, 3, side]
             add_into(kept, [one.at[side, level, 1], kept])
@@ -374,7 +374,7 @@
 
         @pl.when(z == level)
         def _():
-            for side in (0, 1):
+            for side in range(sides):
                 terms = [two.at[side, level]]
                 if level > 0:
                     go_right(side, level).wait_recv()
@@ -384,12 +384,12 @@
                     terms.append(left.at[side, level])
                 add_into(out_ref.at[:, pl.ds(side * half, half)], terms)
 
-        for side in (0, 1):
+        for side in range(sides):
             pl.when(z < level)(lambda: go_right(side, level).wait_send())
             pl.when(z > level)(lambda: go_left(side, level).wait_send())
 
 
-def plane_reduce(pick, values, collective_id, factors=()):
+def plane_reduce(pick, values, collective_id, factors=(), sides=2):
     local, blocks, capacity, columns = values.shape
     rows = pick.shape[-1]
     ep_count, x_count = lax.axis_size("ep"), lax.axis_size("x")
@@ -407,7 +407,7 @@
             einsum("emf,emd->efd", h0, g_rows),
             einsum("emf,emd->efd", h1, g_rows).astype(BF16),
         )
-    depth, half = ep_count // 2, columns // 2
+    depth, half = ep_count // 2, columns // sides
 
     def buffer(*lead):
         return pltpu.VMEM(lead + (rows, half), BF16)
@@ -417,10 +417,11 @@
 
     shapes = [jax.ShapeDtypeStruct((rows, columns), F32)]
     scratch = [
-        buffer(depth, 4, 2),
+        buffer(depth, 4, sides),
         pltpu.VMEM((2, local, capacity, columns), BF16),
         pltpu.VMEM((2, local * capacity, rows), BF16),
-        buffer(2, depth, 2), buffer(2, depth), buffer(2, depth), buffer(2, depth),
+        buffer(sides, depth, 2),
+        buffer(sides, depth), buffer(sides, depth), buffer(sides, depth),
         sems(2, 2), sems(2, depth, 2), sems(2, depth, 2),
         sems(2, depth), sems(2, depth), sems(2, depth),
         sems(2, depth), sems(2, depth), sems(2, depth),
@@ -442,7 +443,7 @@
         ]
     anywhere = pl.BlockSpec(memory_space=pl.ANY)
     results = pl.pallas_call(
-        functools.partial(reduce_kernel, depth, half, bool(factors)),
+        functools.partial(reduce_kernel, depth, half, sides, bool(factors)),
         out_shape=shapes,
         in_specs=[anywhere] * (2 + len(factors)),
         out_specs=[pl.BlockSpec(memory_space=pltpu.VMEM)] + [anywhere] * (len(shapes) - 1),
@@ -999,6 +1000,7 @@
     dot_rows = dot_rows.reshape(local, blocks, capacity).transpose(1, 0, 2)
     dots_token = jnp.sum(jnp.where(picks, dot_rows[..., None], 0.0), axis=2)
     grad_probs = spread(dots_token, PLANE, 2, True)
+    back_rows, grad_probs = lax.optimization_barrier((back_rows, grad_probs))
     grad_probs = jnp.sum(grad_probs.reshape(ep_count, x_count, local, rows), axis=1)
     grad_probs = grad_probs.reshape(experts_all, rows).T
     back_sum, grad_pair_own, grad_pair_other, grad_down_own, grad_down_other = plane_reduce(
@@ -1073,7 +1075,7 @@
     small = jnp.sum(spread(small, ALL, 5, True), axis=0)
     small = spread(small, ALL, 6).reshape(-1)
     out_rows, small = lax.optimization_barrier((out_rows, small))
-    output = (middle + plane_reduce(pick_rows, out_rows, 4)).astype(BF16)
+    output = (middle + plane_reduce(pick_rows, out_rows, 4, sides=1)).astype(BF16)
     cuts = (experts_all * width, width, width, head_dim, head_dim)
     starts = [sum(cuts[:index]) for index in range(5)]
     router_sum, *gains = (small[at : at + cut] for at, cut in zip(starts, cuts))

time: 1170 us -> 1200 us (1.026)
  the two profiles are of different devices: /device:TPU:0 before, /device:TPU:8 now
where the time goes in v7:
time: 1200 us; the launch traced here: 1190 us
  Pallas kernels  769 us (64%)
  waiting for transfers between devices  206 us (17%)
  matrix products  84.6 us (7%)
  other arithmetic  70.9 us (6%)
  local copies, waits for them, and re-layouts  46.6 us (4%)
  between operations  14.9 us (1%)
    pallas_call x2, Pallas kernels, plane_reduce(): pl.pallas_call(functools.partial(reduce_kernel, depth, half, sides, bool(...  431 us
    all_gather x3, waiting for transfers between devices, gather(): return lax.all_gather(value, axes, axis=0, tiled=True)  181 us
    pallas_call x4, Pallas kernels, spread(): pl.pallas_call(functools.partial(spread_kernel, axes, counts, own_slices)...  83.2 us
    pallas_call x1, Pallas kernels, expert(): pl.pallas_call(expert_kernel, grid=(local, count // step), out_shape=[s(w...  63.3 us
    pallas_call x2, Pallas kernels, attention_call(): pl.pallas_call(functools.partial(kernel, min(512, seq_len)), grid=(heads,...  53.1 us
    pallas_call x1, Pallas kernels, group_reduce(): pl.pallas_call(functools.partial(group_kernel, pieces), out_shape=jax.Sha...  39.5 us
    pallas_call x1, Pallas kernels, group_gather(): pl.pallas_call(functools.partial(group_gather_kernel, pieces), out_shape=...  37.5 us
    pallas_call x2, Pallas kernels, dispatch(): pl.pallas_call(dispatch_kernel, grid=(blocks // group,), out_shape=jax.Sh...  34.2 us
  transfers between devices with their start and end apart: 10, of which 3 were waited for; matrix products, arithmetic and copies ran while one was open for 15% of the time, Pallas kernels for 42%

profile of v7, /device:TPU:8, one launch (start us, length us, event | category | flops | bytes accessed | tf_op | source)
XLA Modules:
  0.0 1193.4 jit_solution(14497060857402212163)
XLA Ops:
  9.4 0.8 reduce-window.4
  10.3 1.1 copy.43.dr_ref
  11.4 37.5 %group_gather.1 = bf16[2,2,256,2048]{3,2,1,0:T(8,128)(2,1)} custom-call(bf16[256,2048]{1,0:T(8,128)(2,1)} %v_ref.1), custom_call_target="tpu_custom_call" | custom-call | tf_op jit(solution)/shard_map/group_gather/pallas_call | solution.py:584
  49.0 1.9 fusion.24
  50.9 1.3 pad_maximum_fusion.1
  52.7 0.9 multiply_reduce_fusion
  54.2 1.0 multiply_convert_fusion
  55.3 0.7 slice-done.1
  56.0 3.6 fusion.21.v_ref
  59.6 3.8 fusion.20.k_ref
  63.4 3.7 fusion.18.q_ref
  67.0 22.8 %attention.2 = bf16[1024,512]{1,0:T(8,128)(2,1)} custom-call(f32[1024,512]{1,0:T(8,128)} %fusion.18.q_ref, f32[1024,512]{1,0:T(8,128)} %fusion.20.k_ref, f32[1024,512]{1,0:T(8,128)} %fusion.21.v_ref, f32[1,128]{1,0:T(1,128)} %get-tuple-element.93.qg_ref, f32[1,128]{1,0:T(1,128)} %get-tuple-element.92.kg_ref, f32[1024,128]{1,0:T(8,128)} %get-tuple-element.90.cos_ref, ...), custom_call_target="tpu_custom_call" | custom-call | flops 2147483648 | bytes 8388608 | tf_op jit(solution)/shard_map/attention/pallas_call | solution.py:699
  89.8 5.6 convolution_convert_fusion
  95.4 39.5 %group_reduce.1 = f32[256,2048]{1,0:T(8,128)} custom-call(bf16[2,2,256,2048]{3,2,1,0:T(8,128)(2,1)} %bitcast.139), custom_call_target="tpu_custom_call" | custom-call | tf_op jit(solution)/shard_map/group_reduce/pallas_call | solution.py:519
  134.8 2.6 multiply_reduce_fusion.3
  137.5 1.3 copy-done.2
  138.8 1.2 multiply_convert_fusion.1
  140.1 14.3 %reshape.202.w0_ref = bf16[4,2048,512]{2,1,0:T(8,128)(2,1)} reshape(bf16[4,2048,2,256]{3,2,1,0:T(2,128)(2,1)} %param.23) | data formatting | bytes 16777216 | tf_op jit(solution)/shard_map/reshape | solution.py:973
  156.2 24.7 %spread.4 = f32[16,32,256]{2,1,0:T(8,128)} custom-call(f32[32,256]{1,0:T(8,128)} %fusion.36.v_ref), custom_call_target="tpu_custom_call" | custom-call | tf_op jit(solution)/shard_map/spread/pallas_call | solution.py:107
  180.9 0.9 broadcast_compare_fusion
  182.1 1.5 select_reduce_fusion.1
  183.6 2.7 fusion.4.pick_ref.refs_0_
  186.3 34.3 %all-gather.6.cloned.1.call-done = bf16[4096,2048]{1,0:T(8,128)(2,1)} async-done(((bf16[256,2048]{1,0:T(8,128)(2,1)}), bf16[4096,2048]{1,0:T(8,128)(2,1)}) %all-gather.6.cloned.1.call-update) | async-done | bytes 16777232 | tf_op jit(solution)/shard_map/all_gather | solution.py:891
  220.6 17.2 %dispatch.2 = bf16[4,16,96,2048]{3,2,1,0:T(8,128)(2,1)} custom-call(bf16[16,384,256]{2,1,0:T(8,128)(2,1)} %fusion.4.pick_ref.refs_0_, bf16[16,256,2048]{2,1,0:T(8,128)(2,1)} %bitcast.137), custom_call_target="tpu_custom_call" | custom-call | flops 6442450944 | bytes 41943040 | tf_op jit(solution)/shard_map/dispatch/pallas_call | solution.py:734
  237.7 14.6 %fusion.52.u0_ref = f32[4,1536,256]{2,1,0:T(8,128)} fusion(bf16[4,1536,2048]{2,1,0:T(8,128)(2,1)} %bitcast.130, bf16[4,256,2048]{2,1,0:T(8,128)(2,1)} %w0_ref.1), kind=kOutput, calls=%fused_computation.113 | convolution fusion | flops 6442450944 | bytes 35651584 | tf_op jit(solution)/shard_map/emd,efd->emf/dot_general | solution.py:883
  252.3 14.6 %fusion.53.u1_ref = f32[4,1536,256]{2,1,0:T(8,128)} fusion(bf16[4,1536,2048]{2,1,0:T(8,128)(2,1)} %bitcast.131, bf16[4,256,2048]{2,1,0:T(8,128)(2,1)} %collective-permute-done.w1_ref), kind=kOutput, calls=%fused_computation.114 | convolution fusion | flops 6442450944 | bytes 35651584 | tf_op jit(solution)/shard_map/emd,efd->emf/dot_general | solution.py:883
  267.0 147.0 %all-gather.4.cloned.1.call-done = bf16[4096,2048]{1,0:T(8,128)(2,1)} async-done(((bf16[256,2048]{1,0:T(8,128)(2,1)}), bf16[4096,2048]{1,0:T(8,128)(2,1)}) %all-gather.4.cloned.1.call-update) | async-done | bytes 16777232 | tf_op jit(solution)/shard_map/all_gather | solution.py:891
  413.9 2.4 copy.47.pr_ref
  416.4 17.1 %dispatch.3 = bf16[4,16,96,2048]{3,2,1,0:T(8,128)(2,1)} custom-call(bf16[16,384,256]{2,1,0:T(8,128)(2,1)} %fusion.4.pick_ref.refs_0_, bf16[16,256,2048]{2,1,0:T(8,128)(2,1)} %bitcast.138), custom_call_target="tpu_custom_call" | custom-call | flops 6442450944 | bytes 41943040 | tf_op jit(solution)/shard_map/dispatch/pallas_call | solution.py:734
  433.4 63.3 %expert.1 = (bf16[4,1536,2048]{2,1,0:T(8,128)(2,1)}, f32[4,1536,1]{2,1,0:T(8,128)}, bf16[4,1536,256]{2,1,0:T(8,128)(2,1)}, bf16[4,1536,256]{2,1,0:T(8,128)(2,1)}...) custom-call(bf16[4,1536,2048]{2,1,0:T(8,128)(2,1)} %bitcast.133, bf16[4,2048,512]{2,1,0:T(8,128)(2,1)} %reshape.202.w0_ref, ...), custom_call_target="tpu_custom_call" | custom-call | flops 51539607552 | bytes 98566144 | tf_op jit(solution)/shard_map/expert/pallas_call | solution.py:843
  496.7 2.8 reduce.1
  499.6 3.3 select_reduce_fusion.v_ref
  502.9 10.1 spread.5
  513.0 193.7 %plane_reduce.2 = (f32[256,2048]{1,0:T(8,128)}, f32[4,2048,512]{2,1,0:T(8,128)}, bf16[4,2048,512]{2,1,0:T(8,128)(2,1)}, f32[4,256,2048]{2,1,0:T(8,128)}, bf16[4,256,2048]{2,1,0:T(8,128)(2,1)}) custom-call(bf16[16,384,256]{2,1,0:T(8,128)(2,1)} %fusion.4.pick_ref.refs_0_, bf16[4,16,96,2048]{3,2,1,0:T(8,128)(2,1)} %bitcast.136, ...), custom_call_target="tpu_custom_call" | custom-call | tf_op jit(solution)/shard_map/plane_reduce/pallas_call | solution.py:445
  707.5 4.2 multiply_reduce_fusion.1
  711.8 2.5 fusion.49
  714.3 27.0 %down_rows.1 = bf16[4,1536,2048]{2,1,0:T(8,128)(2,1)} custom-call(bf16[4,1536,256]{2,1,0:T(8,128)(2,1)} %get-tuple-element.46.refs_3_.h0_ref, bf16[4,1536,256]{2,1,0:T(8,128)(2,1)} %get-tuple-element.47.refs_4_.h1_ref, bf16[4,256,2048]{2,1,0:T(8,128)(2,1)} %w0_ref.1, bf16[4,256,2048]{2,1,0:T(8,128)(2,1)} %collective-permute-done.w1_ref), custom_call_target="tpu_custom_call" | custom-call | flops 12884901888 | bytes 33554432 | tf_op jit(solution)/shard_map/down_rows/pallas_call | solution.py:801
  741.3 10.1 convert_add_fusion.1
  751.4 14.0 %convert_add_fusion = f32[4,2048,512]{2,1,0:T(8,128)} fusion(f32[4,2048,512]{2,1,0:T(8,128)} %get-tuple-element.54, bf16[4,2048,512]{2,1,0:T(8,128)(2,1)} %collective-permute-done.3), kind=kLoop, calls=%fused_computation | loop fusion | flops 8388608 | bytes 41943040 | tf_op jit(solution)/shard_map/add | solution.py:1016
  765.5 5.9 convolution_convert_fusion.1
  771.4 5.5 convolution_convert_fusion.5.go_ref
  776.9 30.4 %attention.3 = (bf16[1024,512]{1,0:T(8,128)(2,1)}, bf16[1024,512]{1,0:T(8,128)(2,1)}, bf16[1024,512]{1,0:T(8,128)(2,1)}, f32[1,128]{1,0:T(1,128)}, f32[1,128]{1,0:T(1,128)}) custom-call(f32[1024,512]{1,0:T(8,128)} %fusion.18.q_ref, f32[1024,512]{1,0:T(8,128)} %fusion.20.k_ref, f32[1024,512]{1,0:T(8,128)} %fusion.21.v_ref, ...), custom_call_target="tpu_custom_call" | custom-call | flops 5368709120 | bytes 8388608 | tf_op jit(solution)/shard_map/attention/pallas_call | solution.py:699
  807.3 4.4 fusion.19
  811.7 4.0 fusion.17
  815.7 6.3 add_convert_fusion
  822.7 3.5 fusion.1
  826.2 2.4 fusion.8
  828.7 2.4 fusion.9
  831.1 2.4 fusion.10
  833.6 3.1 pad_maximum_fusion
  838.7 20.3 %reshape.211 = f32[4,2048,2,256]{3,2,1,0:T(2,128)} reshape(f32[4,2048,512]{2,1,0:T(8,128)} %convert_add_fusion) | data formatting | bytes 33554432 | tf_op jit(solution)/shard_map/reshape | solution.py:1034
  859.0 1.8 convert_element_type.128
  860.8 23.6 %reduce-scatter.4.cloned.1.call-done = bf16[256,2048]{1,0:T(8,128)(2,1)} async-done(((bf16[1024,2048]{1,0:T(8,128)(2,1)}), bf16[256,2048]{1,0:T(8,128)(2,1)}) %reduce-scatter.4.cloned.1.call-update) | async-done | bytes 1048592 | tf_op jit(solution)/shard_map/reduce_scatter | solution.py:895
  884.4 2.0 fusion.15
  886.5 0.8 pad.4
  887.2 20.7 %spread.6 = f32[32,24,128]{2,1,0:T(8,128)} custom-call(f32[32,24,128]{2,1,0:T(8,128)} %bitcast.143), custom_call_target="tpu_custom_call" | custom-call | tf_op jit(solution)/shard_map/spread/pallas_call | solution.py:107
  907.9 1.6 reduce_sum.152.v_ref
  909.6 27.7 %spread.7 = f32[32,24,128]{2,1,0:T(8,128)} custom-call(f32[24,128]{1,0:T(8,128)} %reduce_sum.152.v_ref), custom_call_target="tpu_custom_call" | custom-call | tf_op jit(solution)/shard_map/spread/pallas_call | solution.py:107
  937.3 237.5 %plane_reduce.3 = f32[256,2048]{1,0:T(8,128)} custom-call(bf16[16,384,256]{2,1,0:T(8,128)(2,1)} %fusion.4.pick_ref.refs_0_, bf16[4,16,96,2048]{3,2,1,0:T(8,128)(2,1)} %bitcast.135), custom_call_target="tpu_custom_call" | custom-call | tf_op jit(solution)/shard_map/plane_reduce/pallas_call | solution.py:445
  1174.8 0.7 slice.41
  1175.5 1.7 slice.42
  1178.4 3.5 add_convert_fusion.1
  1181.8 2.0 fusion.13
  1183.8 2.5 convert_bitcast_fusion
  (126 shorter events, 10.4 us)
Async XLA Ops:
  7.2 82.6 %copy-start = (bf16[512,2048]{1,0:T(8,128)(2,1)S(1)}, bf16[512,2048]{1,0:T(8,128)(2,1)}, u32[]{:S(2)}) copy-start(bf16[512,2048]{1,0:T(8,128)(2,1)} %param.20) | copy-start | bytes 6291460
  7.2 41.7 %copy-start.25 = (s32[1,4]{1,0:T(1,128)S(1)}, s32[1,4]{1,0:T(1,128)}, u32[]{:S(2)}) copy-start(s32[1,4]{1,0:T(1,128)} %param.15) | copy-start | bytes 52
  7.2 213.4 %all-gather.6.cloned.1.call-start = ((), (), s32[]{:S(2)}) async-start(), calls=%async_computation.4 | async-start | bytes 17825792 | tf_op jit(solution)/shard_map/all_gather | solution.py:891
  7.9 406.0 %all-gather.4.cloned.1.call-start = ((), (), s32[]{:S(2)}) async-start(), calls=%async_computation.3 | async-start | bytes 17825792 | tf_op jit(solution)/shard_map/all_gather | solution.py:891
  8.7 45.5 %copy-start.17 = (f32[2048]{0:T(1024)}, f32[2048]{0:T(1024)S(1)}, u32[]{:S(2)}) copy-start(f32[2048]{0:T(1024)S(1)} %convert_element_type.103) | copy-start | bytes 24580
  10.3 41.9 %copy-start.19 = (s32[1024]{0:T(1024)}, s32[1024]{0:T(1024)S(1)}, u32[]{:S(2)}) copy-start(s32[1024]{0:T(1024)S(1)} %convert_reduce_fusion) | copy-start | bytes 12292
  11.3 40.8 %copy-start.23 = (bf16[128]{0:T(256)(128)(2,1)S(1)}, bf16[128]{0:T(256)(128)(2,1)}, u32[]{:S(2)}) copy-start(bf16[128]{0:T(256)(128)(2,1)} %param.19) | copy-start | bytes 772
  11.3 40.8 %copy-start.24 = (bf16[128]{0:T(256)(128)(2,1)S(1)}, bf16[128]{0:T(256)(128)(2,1)}, u32[]{:S(2)}) copy-start(bf16[128]{0:T(256)(128)(2,1)} %param.18) | copy-start | bytes 772
  48.8 3.9 copy-start.1
  52.7 2.6 slice-start
  54.2 1.8 slice-start.1
  95.4 39.5 %copy-start.4 = (bf16[256,2048]{1,0:T(8,128)(2,1)S(1)}, bf16[256,2048]{1,0:T(8,128)(2,1)}, u32[]{:S(2)}) copy-start(bf16[256,2048]{1,0:T(8,128)(2,1)} %v_ref.1) | copy-start | bytes 3145732
  137.5 1.3 copy-start.2
  140.0 15.0 %copy-start.21 = (s32[256,8]{0,1:T(8,128)S(1)}, s32[256,8]{0,1:T(8,128)}, u32[]{:S(2)}) copy-start(s32[256,8]{0,1:T(8,128)} %param.14) | copy-start | bytes 24580
  140.0 15.0 %copy-start.6 = (bf16[256,2048]{1,0:T(8,128)(2,1)S(1)}, bf16[256,2048]{1,0:T(8,128)(2,1)}, u32[]{:S(2)}) copy-start(bf16[256,2048]{1,0:T(8,128)(2,1)} %multiply_convert_fusion.1) | copy-start | bytes 3145732
  140.0 15.0 %copy-start.15 = (bf16[2048,32]{0,1:T(8,128)(2,1)S(1)}, bf16[2048,32]{0,1:T(8,128)(2,1)}, u32[]{:S(2)}) copy-start(bf16[2048,32]{0,1:T(8,128)(2,1)} %param.22) | copy-start | bytes 393220
  140.1 625.4 %all-gather.8.cloned.1.call-start = ((), (), s32[]{:S(2)}) async-start(), calls=%async_computation.5 | async-start | bytes 5242880 | tf_op jit(solution)/shard_map/all_gather | solution.py:891
  154.4 279.0 %collective-permute-start.1 = (bf16[4,2048,512]{2,1,0:T(8,128)(2,1)}, bf16[4,2048,512]{2,1,0:T(8,128)(2,1)}, u32[]{:S(2)}, u32[]{:S(2)}) collective-permute-start(bf16[4,2048,512]{2,1,0:T(8,128)(2,1)} %reshape.202.w0_ref), channel_id=1, source_target_pairs={{0,1},{1,0},{2,3},{3,2},{4,5},{5,4},{6,7},{7,6},{8,9},{9,8},{10,11... | collective-permute-start | bytes 25165832 | tf_op jit(solution)/shard_map/ppermute | solution.py:887
  154.4 97.9 %collective-permute-start = (bf16[4,256,2048]{2,1,0:T(8,128)(2,1)}, bf16[4,256,2048]{2,1,0:T(8,128)(2,1)}, u32[]{:S(2)}, u32[]{:S(2)}) collective-permute-start(bf16[4,256,2048]{2,1,0:T(8,128)(2,1)} %w0_ref.1), channel_id=1, source_target_pairs={{0,1},{1,0},{2,3},{3,2},{4,5},{5,4},{6,7},{7,6},{8,9},{9,8},{10,11... | collective-permute-start | bytes 12582920 | tf_op jit(solution)/shard_map/ppermute | solution.py:887
  513.0 193.8 %copy-start.16 = (f32[16,4,256]{2,1,0:T(4,128)S(1)}, f32[16,4,256]{2,1,0:T(4,128)}, u32[]{:S(2)}) copy-start(f32[16,4,256]{2,1,0:T(4,128)} %spread.5) | copy-start | bytes 196612
  706.8 5.0 copy-start.10
  706.8 44.7 %collective-permute-start.3 = (bf16[4,2048,512]{2,1,0:T(8,128)(2,1)}, bf16[4,2048,512]{2,1,0:T(8,128)(2,1)}, u32[]{:S(2)}, u32[]{:S(2)}) collective-permute-start(bf16[4,2048,512]{2,1,0:T(8,128)(2,1)} %get-tuple-element.55), channel_id=1, source_target_pairs={{0,1},{1,0},{2,3},{3,2},{4,5},{5,4},{6,7},{7,6},{8,9},{9,8},{10,11... | collective-permute-start | bytes 25165832 | tf_op jit(solution)/shard_map/ppermute | solution.py:887
  706.9 4.8 copy-start.3
  706.9 4.8 copy-start.9
  706.9 34.4 %collective-permute-start.2 = (bf16[4,256,2048]{2,1,0:T(8,128)(2,1)}, bf16[4,256,2048]{2,1,0:T(8,128)(2,1)}, u32[]{:S(2)}, u32[]{:S(2)}) collective-permute-start(bf16[4,256,2048]{2,1,0:T(8,128)(2,1)} %get-tuple-element.53), channel_id=1, source_target_pairs={{0,1},{1,0},{2,3},{3,2},{4,5},{5,4},{6,7},{7,6},{8,9},{9,8},{10,11... | collective-permute-start | bytes 12582920 | tf_op jit(solution)/shard_map/ppermute | solution.py:887
  714.2 144.7 %reduce-scatter.8.cloned.1.call-start = ((), (), s32[]{:S(2)}) async-start(), calls=%async_computation.8 | async-start | bytes 2359296 | tf_op jit(solution)/shard_map/reduce_scatter | solution.py:895
  751.4 14.0 %copy-start.13 = (bf16[1024,512]{1,0:T(8,128)(2,1)S(1)}, bf16[1024,512]{1,0:T(8,128)(2,1)}, u32[]{:S(2)}) copy-start(bf16[1024,512]{1,0:T(8,128)(2,1)} %attention.2) | copy-start | bytes 3145732
  771.4 113.0 %reduce-scatter.4.cloned.1.call-start = ((), (), s32[]{:S(2)}) async-start(), calls=%async_computation.6 | async-start | bytes 5242880 | tf_op jit(solution)/shard_map/reduce_scatter | solution.py:895
  807.3 4.4 copy-start.29
  822.0 0.7 copy-start.20
  822.0 0.7 copy-start.18
  822.0 361.8 %reduce-scatter.6.cloned.1.call-start = ((), (), s32[]{:S(2)}) async-start(), calls=%async_computation.7 | async-start | bytes 7077888 | tf_op jit(solution)/shard_map/reduce_scatter | solution.py:895
  822.7 3.5 copy-start.30
  826.2 2.5 copy-start.28
  828.7 2.5 copy-start.14
  836.7 0.6 copy-start.22
  836.7 1.2 copy-start.7
  838.6 45.7 %copy-start.5 = (bf16[256,2048]{1,0:T(8,128)(2,1)S(1)}, bf16[256,2048]{1,0:T(8,128)(2,1)}, u32[]{:S(2)}) copy-start(bf16[256,2048]{1,0:T(8,128)(2,1)} %v_ref.1) | copy-start | bytes 3145732
  838.6 47.8 %copy-start.27 = (f32[1,128]{1,0:T(1,128)S(1)}, f32[1,128]{1,0:T(1,128)}, u32[]{:S(2)}) copy-start(f32[1,128]{1,0:T(1,128)} %get-tuple-element.61) | copy-start | bytes 1540
  838.6 47.8 %copy-start.26 = (f32[1,128]{1,0:T(1,128)S(1)}, f32[1,128]{1,0:T(1,128)}, u32[]{:S(2)}) copy-start(f32[1,128]{1,0:T(1,128)} %get-tuple-element.62) | copy-start | bytes 1540
  937.3 237.5 %copy-start.12 = (f32[32,24,128]{2,1,0:T(8,128)S(1)}, f32[32,24,128]{2,1,0:T(8,128)}, u32[]{:S(2)}) copy-start(f32[32,24,128]{2,1,0:T(8,128)} %spread.7) | copy-start | bytes 1179652
  1177.2 4.6 copy-start.8
  1177.2 4.6 copy-start.11
Sparse Core Ops, SparseCore 0:
  10.8 209.7 all-gather.5
  223.9 189.9 all-gather.3
  714.3 32.5 all-gather.7
  771.5 66.3 reduce-scatter.7
  840.2 44.0 reduce-scatter.3
  887.8 147.2 reduce-scatter.5
